TPU v7x, 32 devices: a whole 2x2x4 slice. The times are simulated.
32 devices in a mesh: cuts: 2 (over x), ma: 8 (over z, y), mb: 2 (over core).
Axes of the slice: x: 2, y: 2, z: 4, core: 2. Of those that a mesh axis runs over, the one named last changes fastest.
Arguments:
- stem_field: bfloat16 [64, 512, 2, 512], P(('cuts', 'ma', 'mb')), parts along dimension 0, may hold values from -6 to 6
- first_branch_tensors: bfloat16 [2, 2, 512, 512], P(None, None, 'ma'), may hold values from -0.1875 to 0.1875
- second_branch_tensors: bfloat16 [2, 2, 512, 512], P(None, None, 'ma'), may hold values from -0.1875 to 0.1875
- relabel: int32 [2, 512], replicated, may hold values from 0 to 511, each once within a row
- sample_block: int32 [8192, 1], P(('cuts', 'ma', 'mb')), parts along dimension 0, may hold values from 0 to 31; in each aligned block of 256 rows (0 to 255, 256 to 511, ...) at most 16 rows name the same one
- sample_state: bfloat16 [8192, 2, 512], P(('cuts', 'ma', 'mb')), parts along dimension 0, may hold values from -0.1875 to 0.1875
Outputs:
- amplitudes: bfloat16 [8192, 2, 512], P(('cuts', 'ma', 'mb')), parts along dimension 0
There are 2 independent parts, one for each index of `cuts`. A program takes and returns all parts, laid end to end along the dimension named above; an argument that names none is the same for every part. Nothing has to cross between parts.
Inputs may be any that keep to these rules, and one draw needn't show every extreme that they name: `relabel`: each row is a permutation of 0 to 511. `sample_block`: within the 256 rows of one device no prefix block is named more than 16 times.
All inputs are finite; a program needn't handle non-finite values.
Results may differ from a plain program's by a relative error of at most 0.0075.
Values may be sent and summed in bfloat16 or wider, within the bound.
No kernel may reach another device: no remote copies, remote signals or barrier semaphores. Data moves between devices by JAX's collectives and lax.ppermute only.
A program may use at most 64 MiB of HBM per device.

v0:
```python
import functools

import jax
import jax.numpy as jnp
from jax import lax
from jax.experimental import pallas as pl
from jax.experimental.pallas import tpu as pltpu
from jax.sharding import PartitionSpec as P

AXES = ("ma", "mb")
BF16 = jnp.bfloat16
F32 = jnp.float32
VMEM = pl.BlockSpec(memory_space=pltpu.VMEM)
SMEM = pl.BlockSpec(memory_space=pltpu.SMEM)


def permute(value, pairs):
    count = lax.axis_size("mb")
    full = [(a * count + c, b * count + c) for a, b in pairs for c in range(count)]
    return lax.ppermute(value, AXES, full)


def swap_ma(value, offset):
    return permute(value, [(m, m ^ offset) for m in range(lax.axis_size("ma"))])


def swap_mb(value, offset):
    count = lax.axis_size("ma") * lax.axis_size("mb")
    return lax.ppermute(value, AXES, [(m, m ^ offset) for m in range(count)])


def relay_groups(length):
    owner, groups = {}, {}
    for distance in range(1, length):
        for z in range(length):
            for x in range(1, length):
                if abs((z ^ x) - z) != distance:
                    continue
                sender = z + (1 if (z ^ x) > z else -1)
                held = sender ^ z ^ x
                key = (x, owner.get((sender, held)))
                owner[(z, x)] = key
                groups.setdefault(key, []).append((sender, z))
    return groups


def relay_gather(value):
    length = lax.axis_size("ma") // 2
    sent = {None: value}
    slots = {0: [value]}
    for key, moves in relay_groups(length).items():
        pairs = [(2 * a + y, 2 * b + y) for a, b in moves for y in range(2)]
        sent[key] = permute(sent[key[1]], pairs)
        slots.setdefault(key[0], []).append(sent[key])
    gathered = {}
    for x in sorted(slots):
        whole = functools.reduce(jnp.add, slots[x])
        gathered[2 * x] = whole
        gathered[2 * x + 1] = swap_ma(whole, 1)
    return [gathered[d] for d in range(2 * length)]


def scalars(*values):
    return jnp.stack([jnp.asarray(v, jnp.int32) for v in values])


def pack_kernel(place_ref, *refs):
    count = refs[0].shape[0]
    sources, outs = refs[:-count], refs[-count:]
    for d, out_ref in enumerate(outs):
        for s, source in enumerate(sources):
            out_ref[s] = source[place_ref[0] ^ d]


def pack(here_ma, sources):
    count = sources[0].shape[0]
    shape = (len(sources),) + sources[0].shape[1:]
    return pl.pallas_call(
        pack_kernel,
        in_specs=[SMEM] + [VMEM] * len(sources),
        out_specs=[VMEM] * count,
        out_shape=[jax.ShapeDtypeStruct(shape, BF16)] * count,
        name="pack",
    )(scalars(here_ma), *sources)


def collect_kernel(place_ref, *refs):
    slots, out_ref = refs[:-1], refs[-1]
    depth = slots[0].shape[2]
    for d, slot in enumerate(slots):
        start = pl.multiple_of((place_ref[0] ^ d) * depth, depth)
        out_ref[:, :, pl.ds(start, depth), :] = slot[...]


def collect(here_ma, slots):
    rounds, parts, depth, width = slots[0].shape
    return pl.pallas_call(
        collect_kernel,
        in_specs=[SMEM] + [VMEM] * len(slots),
        out_specs=VMEM,
        out_shape=jax.ShapeDtypeStruct((rounds, parts, depth * len(slots), width), BF16),
        name="collect",
    )(scalars(here_ma), *slots)


def table_kernel(inner, count_mb, relative, place_ref, relabel_ref, first_ref, second_ref, *refs):
    stem_ref, final_ref, product_ref, right_ref = refs
    size = first_ref.shape[2]
    column = lax.broadcasted_iota(jnp.int32, (size, size), 0)
    seat, rest = column // inner, column % inner
    ma, mb = seat // count_mb, seat % count_mb
    near = (((ma ^ place_ref[0]) * count_mb) + (mb ^ place_ref[1])) * inner + rest
    for r in range(2):
        position = near if relative[r] else column
        selector = jnp.where(relabel_ref[r : r + 1, :] == position, 1.0, 0.0).astype(BF16)
        for p in range(2):
            ordered = jnp.dot(selector, first_ref[r, p], preferred_element_type=F32)
            if r == 0:
                turned = ordered.T.astype(BF16)
                if p == 0:
                    stem_ref[:size, :size] = turned
                    stem_ref[size:, size:] = turned
                else:
                    stem_ref[size:, :size] = turned
                    stem_ref[:size, size:] = -turned
            else:
                ordered = ordered.astype(BF16)
                if p == 0:
                    final_ref[:size, :size] = ordered
                    final_ref[size:, size:] = ordered
                else:
                    final_ref[:size, size:] = ordered
                    final_ref[size:, :size] = -ordered
    width = second_ref.shape[2]
    right_ref[:width, :width] = second_ref[1, 0]
    right_ref[:width, width:] = second_ref[1, 1]
    right_ref[width:, :width] = -second_ref[1, 1]
    right_ref[width:, width:] = second_ref[1, 0]
    both = jnp.dot(second_ref[0, 0], right_ref[:width, :], preferred_element_type=F32)
    both += jnp.dot(second_ref[0, 1], right_ref[width:, :], preferred_element_type=F32)
    both = both.astype(BF16)
    product_ref[:width, :] = both
    product_ref[width:, :width] = -both[:, width:]
    product_ref[width:, width:] = both[:, :width]


def tables(here, relabel, first, second, inner, count_mb, relative):
    size, width = 2 * first.shape[2], 2 * second.shape[2]
    return pl.pallas_call(
        functools.partial(table_kernel, inner, count_mb, relative),
        in_specs=[SMEM] + [VMEM] * 3,
        out_specs=[VMEM] * 3,
        out_shape=[
            jax.ShapeDtypeStruct((size, size), BF16),
            jax.ShapeDtypeStruct((size, size), BF16),
            jax.ShapeDtypeStruct((width, width), BF16),
        ],
        scratch_shapes=[pltpu.VMEM((width, width), BF16)],
        cost_estimate=pl.CostEstimate(
            flops=size**3 + width**3, bytes_accessed=10 * size * size, transcendentals=0
        ),
        name="tables",
    )(here, relabel, first, second)


def stem_kernel(*refs):
    arrived, (table_ref, product_ref, out_ref, rows_ref, mid_ref) = refs[:-5], refs[-5:]
    seats, parts, _, inner, _ = arrived[0].shape
    for d, piece in enumerate(arrived):
        for s in range(seats):
            for p in range(parts):
                start = ((p * len(arrived) + d) * seats + s) * inner
                rows_ref[start : start + inner, :] = piece[s, p, 0]
    half = mid_ref.shape[0] // 2
    step = min(256, half)
    for top in range(0, 2 * half, step):
        part = jnp.dot(table_ref[top : top + step, :], rows_ref[...], preferred_element_type=F32)
        mid_ref[top : top + step, :] = part.astype(BF16)
    depth = mid_ref.shape[1]
    for top in range(0, half, step):
        part = jnp.dot(
            mid_ref[top : top + step, :], product_ref[:depth, :], preferred_element_type=F32
        )
        part += jnp.dot(
            mid_ref[half + top : half + top + step, :],
            product_ref[depth:, :],
            preferred_element_type=F32,
        )
        out_ref[0, top : top + step, :] = part.astype(BF16)


def contract_stem(arrived, table, product):
    seats, parts, local, inner, width = arrived[0].shape
    size = table.shape[0]
    piece = pl.BlockSpec((seats, parts, 1, inner, width), lambda l: (0, 0, l, 0, 0))
    return pl.pallas_call(
        stem_kernel,
        grid=(local,),
        in_specs=[piece] * len(arrived)
        + [
            pl.BlockSpec(table.shape, lambda l: (0, 0)),
            pl.BlockSpec(product.shape, lambda l: (0, 0)),
        ],
        out_specs=pl.BlockSpec((1, size // 2, 2 * width), lambda l: (l, 0, 0)),
        out_shape=jax.ShapeDtypeStruct((local, size // 2, 2 * width), BF16),
        scratch_shapes=[pltpu.VMEM((size, width), BF16), pltpu.VMEM((size, width), BF16)],
        cost_estimate=pl.CostEstimate(
            flops=2 * local * (size * size * width + 2 * size * width * width),
            bytes_accessed=4 * (local * size * width + table.size),
            transcendentals=0,
        ),
        name="contract_stem",
    )(*arrived, table, product)


def sample_kernel(groups, many, *refs):
    states, refs = refs[:many], refs[many:]
    outs, (plus_ref, cross_ref, sum_ref) = refs[-3 - many : -3], refs[-3:]
    stems = refs[: -3 - many]
    block, last = pl.program_id(0), pl.num_programs(0) - 1
    depth = plus_ref.shape[1]
    width = depth // 2

    @pl.when(block == 0)
    def _():
        for m, state_ref in enumerate(states):
            plus_ref[m, :width, :] = state_ref[:width, :]
            plus_ref[m, width:, :] = -state_ref[width:depth, :]
            cross_ref[m, :width, :] = state_ref[width:depth, :]
            cross_ref[m, width:, :] = state_ref[:width, :]
        sum_ref[...] = jnp.zeros_like(sum_ref)

    local = pl.num_programs(0)
    for m, state_ref in enumerate(states):
        named = state_ref[depth : depth + 16, :].astype(F32)[:1, :]
        for s, stem_ref in enumerate(stems):
            rows = stem_ref.shape[1]
            inner = rows // groups
            step = min(256, rows)
            for part, weights in enumerate((plus_ref, cross_ref)):
                total = sum_ref[m, s, part]
                for top in range(0, rows, step):
                    value = jnp.dot(
                        stem_ref[0, top : top + step, :], weights[m], preferred_element_type=F32
                    )
                    for k in range(step // inner):
                        number = ((top // inner + k) * local + block).astype(F32)
                        part_of = value[k * inner : (k + 1) * inner, :]
                        total += jnp.where(named == number, part_of, 0.0)
                sum_ref[m, s, part] = total

    @pl.when(block == last)
    def _():
        for m, out_ref in enumerate(outs):
            out_ref[...] = sum_ref[m].astype(BF16)


def contract_samples(states, stems, groups):
    many = len(states)
    depth, samples = states[0].shape
    local, rows, width = stems[0].shape
    out = (len(stems), 2, rows // groups, samples)
    return pl.pallas_call(
        functools.partial(sample_kernel, groups, many),
        grid=(local,),
        in_specs=[pl.BlockSpec((depth, samples), lambda l: (0, 0))] * many
        + [pl.BlockSpec((1, rows, width), lambda l: (l, 0, 0))] * len(stems),
        out_specs=[pl.BlockSpec(out, lambda l: (0, 0, 0, 0))] * many,
        out_shape=[jax.ShapeDtypeStruct(out, BF16)] * many,
        scratch_shapes=[
            pltpu.VMEM((many, width, samples), BF16),
            pltpu.VMEM((many, width, samples), BF16),
            pltpu.VMEM((many,) + out, F32),
        ],
        cost_estimate=pl.CostEstimate(
            flops=2 * many * local * rows * width * 2 * samples * len(stems),
            bytes_accessed=2 * (many * states[0].size + len(stems) * stems[0].size),
            transcendentals=0,
        ),
        name="contract_samples",
    )(*states, *stems)


def final_kernel(*refs):
    found, (table_ref, out_ref, rows_ref) = refs[:-3], refs[-3:]
    seats, parts, inner, _ = found[0].shape
    for d, piece in enumerate(found):
        for s in range(seats):
            for p in range(parts):
                start = ((p * len(found) + d) * seats + s) * inner
                rows_ref[start : start + inner, :] = piece[s, p]
    out_ref[...] = lax.dot_general(
        rows_ref[...], table_ref[...], (((0,), (0,)), ((), ())), preferred_element_type=F32
    ).astype(BF16)


def contract_final(found, table):
    samples = found[0].shape[3]
    return pl.pallas_call(
        final_kernel,
        in_specs=[VMEM] * (len(found) + 1),
        out_specs=VMEM,
        out_shape=jax.ShapeDtypeStruct((samples, table.shape[1]), BF16),
        scratch_shapes=[pltpu.VMEM((table.shape[0], samples), BF16)],
        cost_estimate=pl.CostEstimate(
            flops=2 * table.size * samples, bytes_accessed=2 * table.size, transcendentals=0
        ),
        name="contract_final",
    )(*found, table)


def is_short(count_ma):
    return count_ma // 2 <= 4


def on_device(
    stem_field, first_branch_tensors, second_branch_tensors, relabel, sample_block, sample_state
):
    count_ma, count_mb = lax.axis_size("ma"), lax.axis_size("mb")
    here_ma, here_mb = lax.axis_index("ma"), lax.axis_index("mb")
    groups = count_ma * count_mb
    local, row_count, parts, width = stem_field.shape
    inner = row_count // groups
    samples = sample_state.shape[0]
    short = is_short(count_ma)

    flat = sample_state.reshape(samples, parts * width).T
    named = jnp.broadcast_to(sample_block[:, 0].astype(BF16)[None, :], (16, samples))
    states = jnp.concatenate([flat, named], axis=0)

    pieces = stem_field.reshape(local, count_ma, count_mb, inner, parts, width)
    pieces = jnp.transpose(pieces, (2, 1, 4, 0, 3, 5))

    if short:
        share = jnp.where(here_mb == 0, first_branch_tensors, second_branch_tensors)
        mine = collect(here_ma, relay_gather(share))
        other = swap_mb(mine, 1)
        every_first = jnp.where(here_mb == 0, mine, other)
        every_second = jnp.where(here_mb == 0, other, mine)
        held = [
            lax.dynamic_index_in_dim(pieces, here_mb ^ s, keepdims=False) for s in range(count_mb)
        ]
        sources = [held[0]] + [swap_mb(held[s], s) for s in range(1, count_mb)]
        arrived = [
            swap_ma(piece, d) if d else piece
            for d, piece in enumerate(pack(here_ma, sources))
        ]
        every_state = relay_gather(states)
    else:
        every_first = lax.all_gather(first_branch_tensors, "ma", axis=2, tiled=True)
        every_second = lax.all_gather(second_branch_tensors, "ma", axis=2, tiled=True)
        sent = jnp.transpose(pieces, (1, 0, 2, 3, 4, 5))
        sent = sent.reshape((groups,) + sent.shape[2:])
        arrived = lax.all_to_all(sent, AXES, split_axis=0, concat_axis=0, tiled=True)
        arrived = arrived.reshape((count_ma, count_mb) + arrived.shape[1:])
        arrived = [arrived[d] for d in range(count_ma)]
        every_state = lax.all_gather(states, "ma", axis=0)
        every_state = [every_state[d] for d in range(count_ma)]

    here = scalars(here_ma if short else 0, here_mb)
    table, final_table, product = tables(
        here, relabel, every_first, every_second, inner, count_mb, (short, True)
    )
    own = contract_stem(arrived, table, product)
    stems = [own] + [swap_mb(own, s) for s in range(1, count_mb)]
    found = []
    for d in range(0, count_ma, 2):
        found += contract_samples(every_state[d : d + 2], stems, groups)
    if short:
        found = [swap_ma(value, d) if d else value for d, value in enumerate(found)]
    else:
        found = lax.all_to_all(jnp.stack(found), "ma", split_axis=0, concat_axis=0, tiled=True)
        found = [found[d] for d in range(count_ma)]
    return contract_final(found, final_table).reshape(samples, parts, -1)


def solution(mesh):
    placed = (
        P(("cuts", "ma", "mb"), None, None, None),
        P(None, None, "ma", None),
        P(None, None, "ma", None),
        P(),
        P(("cuts", "ma", "mb"), None),
        P(("cuts", "ma", "mb"), None, None),
    )
    return jax.shard_map(
        on_device,
        mesh=mesh,
        in_specs=placed,
        out_specs=P(("cuts", "ma", "mb"), None, None),
        check_vma=False,
    )
```

profile of v0, /device:TPU:1, one launch (start us, length us, event | category | flops | bytes accessed | tf_op | source)
XLA Modules:
  0.0 226.9 jit_solution(10076111208643401718)
XLA Ops:
  0.0 1.0 broadcast_select_fusion.2.refs_0_
  1.0 2.2 collective-permute-start.10
  3.9 5.3 %collective-permute-done.10.refs_2_ = bf16[2,2,64,512]{3,2,1,0:T(8,128)(2,1)S(1)} collective-permute-done((bf16[2,2,64,512]{3,2,1,0:T(8,128)(2,1)S(1)}, bf16[2,2,64,512]{3,2,1,0:T(8,128)(2,1)S(1)}, u32[]{:S(2)}, u32[]{:S(2)}) %collective-permute-start.10) | collective-permute-done | bytes 262176 | tf_op jit(solution)/shard_map/ppermute | solution.py:20
  9.9 1.3 collective-permute-start.13
  11.2 1.3 collective-permute-start.16
  12.5 1.2 collective-permute-start.9
  14.0 5.7 %collective-permute-done.13 = bf16[2,2,64,512]{3,2,1,0:T(8,128)(2,1)S(1)} collective-permute-done((bf16[2,2,64,512]{3,2,1,0:T(8,128)(2,1)S(1)}, bf16[2,2,64,512]{3,2,1,0:T(8,128)(2,1)S(1)}, u32[]{:S(2)}, u32[]{:S(2)}) %collective-permute-start.13) | collective-permute-done | bytes 262176 | tf_op jit(solution)/shard_map/ppermute | solution.py:20
  19.8 1.3 collective-permute-start.15
  21.1 4.3 %collective-permute-done.16 = bf16[2,2,64,512]{3,2,1,0:T(8,128)(2,1)S(1)} collective-permute-done((bf16[2,2,64,512]{3,2,1,0:T(8,128)(2,1)S(1)}, bf16[2,2,64,512]{3,2,1,0:T(8,128)(2,1)S(1)}, u32[]{:S(2)}, u32[]{:S(2)}) %collective-permute-start.16) | collective-permute-done | bytes 262176 | tf_op jit(solution)/shard_map/ppermute | solution.py:20
  25.5 1.3 collective-permute-start.17
  26.8 3.6 %collective-permute-done.15.refs_5_ = bf16[2,2,64,512]{3,2,1,0:T(8,128)(2,1)S(1)} collective-permute-done((bf16[2,2,64,512]{3,2,1,0:T(8,128)(2,1)S(1)}, bf16[2,2,64,512]{3,2,1,0:T(8,128)(2,1)S(1)}, u32[]{:S(2)}, u32[]{:S(2)}) %collective-permute-start.15) | collective-permute-done | bytes 262176 | tf_op jit(solution)/shard_map/ppermute | solution.py:20
  30.4 5.6 %collective-permute-done.17.refs_7_ = bf16[2,2,64,512]{3,2,1,0:T(8,128)(2,1)S(1)} collective-permute-done((bf16[2,2,64,512]{3,2,1,0:T(8,128)(2,1)S(1)}, bf16[2,2,64,512]{3,2,1,0:T(8,128)(2,1)S(1)}, u32[]{:S(2)}, u32[]{:S(2)}) %collective-permute-start.17) | collective-permute-done | bytes 262176 | tf_op jit(solution)/shard_map/ppermute | solution.py:20
  36.8 3.1 %collect.1 = bf16[2,2,512,512]{3,2,1,0:T(8,128)(2,1)} custom-call(s32[1]{0:T(128)} %bitcast.2.place_ref, bf16[2,2,64,512]{3,2,1,0:T(8,128)(2,1)} %copy-done.5, bf16[2,2,64,512]{3,2,1,0:T(8,128)(2,1)} %copy-done.10, bf16[2,2,64,512]{3,2,1,0:T(8,128)(2,1)} %copy-done.9, bf16[2,2,64,512]{3,2,1,0:T(8,128)(2,1)} %copy-done.11, bf16[2,2,64,512]{3,2,1,0:T(8,128)(2,1)} %copy-done.2, ...), custom_call_target="tpu_custom_call" | custom-call | tf_op jit(solution)/shard_map/collect/pallas_call | solution.py:97
  39.9 2.1 collective-permute-start.18
  42.0 2.5 %constant_dynamic-slice_fusion = (bf16[2,8,1,32,2,512]{5,4,3,2,1,0:T(2,128)(2,1)S(1)}, bf16[2,8,1,32,2,512]{5,4,3,2,1,0:T(2,128)(2,1)S(1)}) fusion(bf16[2,8,2,32,2,512]{5,4,3,2,1,0:T(2,128)(2,1)S(1)} %bitcast.17, s32[]{:T(128)S(6)} %select_n.28, s32[]{:T(128)S(6)} %select_n.27), kind=kLoop, calls=%fused_computation.8 | loop fusion | bytes 4194312 | tf_op jit(solution)/shard_map/dynamic-slice.1
  44.8 1.3 copy.19
  46.1 1.4 collective-permute-done.1.refs_1_
  47.5 1.0 copy-done.4
  48.5 3.2 %pack.1 = (bf16[2,2,2,32,512]{4,3,2,1,0:T(8,128)(2,1)}, bf16[2,2,2,32,512]{4,3,2,1,0:T(8,128)(2,1)}, bf16[2,2,2,32,512]{4,3,2,1,0:T(8,128)(2,1)}, bf16[2,2,2,32,...) custom-call(s32[1]{0:T(128)} %bitcast.2.place_ref, ...), custom_call_target="tpu_custom_call" | custom-call | tf_op jit(solution)/shard_map/pack/pallas_call | solution.py:78
  51.6 1.1 collective-permute-start.2
  52.8 7.5 %collective-permute-start.3 = (bf16[2,2,2,32,512]{4,3,2,1,0:T(8,128)(2,1)}, bf16[2,2,2,32,512]{4,3,2,1,0:T(8,128)(2,1)}, u32[]{:S(2)}, u32[]{:S(2)}) collective-permute-start(bf16[2,2,2,32,512]{4,3,2,1,0:T(8,128)(2,1)} %get-tuple-element.26), channel_id=1, source_target_pairs={{0,4},{1,5},{2,6},{3,7},{4,0},{5,1},{6,2},{7,3},{8,12},{9,13},{10,... | collective-permute-start | bytes 786440 | tf_op jit(solution)/shard_map/ppermute | solution.py:20
  60.9 1.3 copy.8
  62.3 2.4 %collective-permute-start.5 = (bf16[2,2,2,32,512]{4,3,2,1,0:T(8,128)(2,1)}, bf16[2,2,2,32,512]{4,3,2,1,0:T(8,128)(2,1)S(1)}, u32[]{:S(2)}, u32[]{:S(2)}) collective-permute-start(bf16[2,2,2,32,512]{4,3,2,1,0:T(8,128)(2,1)} %get-tuple-element.28), channel_id=1, source_target_pairs={{0,8},{1,9},{2,10},{3,11},{4,12},{5,13},{6,14},{7,15},{8,0},{9,1},... | collective-permute-start | bytes 786440 | tf_op jit(solution)/shard_map/ppermute | solution.py:20
  64.7 4.1 %collective-permute-start.6 = (bf16[2,2,2,32,512]{4,3,2,1,0:T(8,128)(2,1)}, bf16[2,2,2,32,512]{4,3,2,1,0:T(8,128)(2,1)}, u32[]{:S(2)}, u32[]{:S(2)}) collective-permute-start(bf16[2,2,2,32,512]{4,3,2,1,0:T(8,128)(2,1)} %get-tuple-element.29), channel_id=1, source_target_pairs={{0,10},{1,11},{2,8},{3,9},{4,14},{5,15},{6,12},{7,13},{8,2},{9,3},... | collective-permute-start | bytes 786440 | tf_op jit(solution)/shard_map/ppermute | solution.py:20
  68.8 5.9 %collective-permute-done.3.refs_2_ = bf16[2,2,2,32,512]{4,3,2,1,0:T(8,128)(2,1)} collective-permute-done((bf16[2,2,2,32,512]{4,3,2,1,0:T(8,128)(2,1)}, bf16[2,2,2,32,512]{4,3,2,1,0:T(8,128)(2,1)}, u32[]{:S(2)}, u32[]{:S(2)}) %collective-permute-start.3) | collective-permute-done | bytes 262176 | tf_op jit(solution)/shard_map/ppermute | solution.py:20
  74.7 1.1 collective-permute-start.7
  75.8 3.9 %broadcast_select_fusion = (bf16[2,2,512,512]{3,2,1,0:T(8,128)(2,1)}, bf16[2,2,512,512]{3,2,1,0:T(8,128)(2,1)}) fusion(bf16[2,2,512,512]{3,2,1,0:T(8,128)(2,1)} %collective-permute-done.18, bf16[2,2,512,512]{3,2,1,0:T(8,128)(2,1)S(1)} %copy-done, pred[]{:T(512)S(6)} %eq.2), kind=kLoop, calls=%fused_computation | loop fusion | flops 2097152 | bytes 8388609 | tf_op jit(solution)/shard_map/jit(_where)/select_n | solution.py:339
  79.7 6.6 %tables.1 = (bf16[1024,1024]{1,0:T(8,128)(2,1)}, bf16[1024,1024]{1,0:T(8,128)(2,1)}, bf16[1024,1024]{1,0:T(8,128)(2,1)}) custom-call(s32[2]{0:T(128)} %pad_add_fusion.place_ref, s32[2,512]{1,0:T(2,128)} %relabel_ref.1, bf16[2,2,512,512]{3,2,1,0:T(8,128)(2,1)} %get-tuple-element.44.first_ref, bf16[2,2,512,512]{3,2,1,0:T(8,128)(2,1)} %get-tuple-element.43.second_ref), custom_call_target="tpu_custom_call" | custom-call | flops 2147483648 | bytes 10485760 | tf_op jit(solution)/shard_map/tables/pallas_call | solution.py:149
  86.3 13.4 %collective-permute-done.6.refs_5_ = bf16[2,2,2,32,512]{4,3,2,1,0:T(8,128)(2,1)} collective-permute-done((bf16[2,2,2,32,512]{4,3,2,1,0:T(8,128)(2,1)}, bf16[2,2,2,32,512]{4,3,2,1,0:T(8,128)(2,1)}, u32[]{:S(2)}, u32[]{:S(2)}) %collective-permute-start.6) | collective-permute-done | bytes 262176 | tf_op jit(solution)/shard_map/ppermute | solution.py:20
  99.7 8.4 %contract_stem.1.refs_2_ = bf16[2,512,1024]{2,1,0:T(8,128)(2,1)} custom-call(bf16[2,2,2,32,512]{4,3,2,1,0:T(8,128)(2,1)} %get-tuple-element.24.refs_0_, bf16[2,2,2,32,512]{4,3,2,1,0:T(8,128)(2,1)} %collective-permute-done.2.refs_1_, bf16[2,2,2,32,512]{4,3,2,1,0:T(8,128)(2,1)} %collective-permute-done.3.refs_2_, bf16[2,2,2,32,512]{4,3,2,1,0:T(8,128)(2,1)} %copy-done.26, ...), custom_call_target="tpu_custom_call" | custom-call | flops 4294967296 | bytes 8388608 | tf_op jit(solution)/shard_map/contract_stem/pallas_call | solution.py:196
  108.1 3.1 %collective-permute-start.19 = (bf16[2,512,1024]{2,1,0:T(8,128)(2,1)}, bf16[2,512,1024]{2,1,0:T(8,128)(2,1)}, u32[]{:S(2)}, u32[]{:S(2)}) collective-permute-start(bf16[2,512,1024]{2,1,0:T(8,128)(2,1)} %contract_stem.1.refs_2_), channel_id=1, source_target_pairs={{0,1},{1,0},{2,3},{3,2},{4,5},{5,4},{6,7},{7,6},{8,9},{9,8},{10,11... | collective-permute-start | bytes 6291464 | tf_op jit(solution)/shard_map/ppermute | solution.py:29
  112.7 1.3 collective-permute-start.31
  114.0 1.5 collective-permute-start.26
  115.5 33.8 %collective-permute-done.31 = bf16[1040,256]{1,0:T(8,128)(2,1)S(1)} collective-permute-done((bf16[1040,256]{1,0:T(8,128)(2,1)S(1)}, bf16[1040,256]{1,0:T(8,128)(2,1)S(1)}, u32[]{:S(2)}, u32[]{:S(2)}) %collective-permute-start.31) | collective-permute-done | bytes 532512 | tf_op jit(solution)/shard_map/ppermute | solution.py:20
  149.7 11.4 %collective-permute-done.26 = bf16[1040,256]{1,0:T(8,128)(2,1)S(1)} collective-permute-done((bf16[1040,256]{1,0:T(8,128)(2,1)S(1)}, bf16[1040,256]{1,0:T(8,128)(2,1)S(1)}, u32[]{:S(2)}, u32[]{:S(2)}) %collective-permute-start.26) | collective-permute-done | bytes 532512 | tf_op jit(solution)/shard_map/ppermute | solution.py:20
  161.6 1.2 collective-permute-start
  163.9 7.6 %contract_samples.7 = (bf16[2,2,32,256]{3,2,1,0:T(8,128)(2,1)}, bf16[2,2,32,256]{3,2,1,0:T(8,128)(2,1)}) custom-call(bf16[1040,256]{1,0:T(8,128)(2,1)} %copy-done.8, bf16[1040,256]{1,0:T(8,128)(2,1)} %copy-done.24, bf16[2,512,1024]{2,1,0:T(8,128)(2,1)} %contract_stem.1.refs_2_, bf16[2,512,1024]{2,1,0:T(8,128)(2,1)} %collective-permute-done.19.refs_3_), custom_call_target="tpu_custom_call" | custom-call | flops 4294967296 | bytes 5259264 | tf_op jit(solution)/shard_map/contract_samples/pallas_call | solution.py:263
  171.5 2.2 collective-permute-start.33
  173.7 2.0 collective-permute-start.34
  175.7 7.6 %contract_samples.6 = (bf16[2,2,32,256]{3,2,1,0:T(8,128)(2,1)}, bf16[2,2,32,256]{3,2,1,0:T(8,128)(2,1)}) custom-call(bf16[1040,256]{1,0:T(8,128)(2,1)} %copy-done.7, bf16[1040,256]{1,0:T(8,128)(2,1)} %collective-permute-done.28.refs_1_, bf16[2,512,1024]{2,1,0:T(8,128)(2,1)} %contract_stem.1.refs_2_, bf16[2,512,1024]{2,1,0:T(8,128)(2,1)} %collective-permute-done.19.refs_3_), custom_call_target="tpu_custom_call" | custom-call | flops 4294967296 | bytes 5259264 | tf_op jit(solution)/shard_map/contract_samples/pallas_call | solution.py:263
  183.3 14.5 %collective-permute-done.22.refs_1_ = bf16[1040,256]{1,0:T(8,128)(2,1)S(1)} collective-permute-done((bf16[1040,256]{1,0:T(8,128)(2,1)}, bf16[1040,256]{1,0:T(8,128)(2,1)S(1)}, u32[]{:S(2)}, u32[]{:S(2)}) %collective-permute-start.22) | collective-permute-done | bytes 532512 | tf_op jit(solution)/shard_map/ppermute | solution.py:20
  197.8 1.9 collective-permute-start.30
  199.7 7.6 %contract_samples.5 = (bf16[2,2,32,256]{3,2,1,0:T(8,128)(2,1)}, bf16[2,2,32,256]{3,2,1,0:T(8,128)(2,1)}) custom-call(bf16[1040,256]{1,0:T(8,128)(2,1)} %copy-done.21, bf16[1040,256]{1,0:T(8,128)(2,1)} %copy-done.23, bf16[2,512,1024]{2,1,0:T(8,128)(2,1)} %contract_stem.1.refs_2_, bf16[2,512,1024]{2,1,0:T(8,128)(2,1)} %collective-permute-done.19.refs_3_), custom_call_target="tpu_custom_call" | custom-call | flops 4294967296 | bytes 5259264 | tf_op jit(solution)/shard_map/contract_samples/pallas_call | solution.py:263
  208.2 7.6 %contract_samples.4 = (bf16[2,2,32,256]{3,2,1,0:T(8,128)(2,1)}, bf16[2,2,32,256]{3,2,1,0:T(8,128)(2,1)}) custom-call(bf16[1040,256]{1,0:T(8,128)(2,1)} %copy-done.6, bf16[1040,256]{1,0:T(8,128)(2,1)} %copy-done.22, bf16[2,512,1024]{2,1,0:T(8,128)(2,1)} %contract_stem.1.refs_2_, bf16[2,512,1024]{2,1,0:T(8,128)(2,1)} %collective-permute-done.19.refs_3_), custom_call_target="tpu_custom_call" | custom-call | flops 4294967296 | bytes 5259264 | tf_op jit(solution)/shard_map/contract_samples/pallas_call | solution.py:263
  215.7 1.6 collective-permute-start.24
  217.7 2.1 collective-permute-done.24.refs_3_
  221.3 3.4 %contract_final.1 = bf16[256,1024]{1,0:T(8,128)(2,1)} custom-call(bf16[2,2,32,256]{3,2,1,0:T(8,128)(2,1)} %get-tuple-element.34.refs_0_, bf16[2,2,32,256]{3,2,1,0:T(8,128)(2,1)} %copy-done.20, bf16[2,2,32,256]{3,2,1,0:T(8,128)(2,1)} %copy-done.18, bf16[2,2,32,256]{3,2,1,0:T(8,128)(2,1)} %copy-done.19, bf16[2,2,32,256]{3,2,1,0:T(8,128)(2,1)} %copy-done.16, ...), custom_call_target="tpu_custom_call" | custom-call | flops 536870912 | bytes 2097152 | tf_op jit(solution)/shard_map/contract_final/pallas_call | solution.py:299
  224.7 2.2 reshape.17
  (106 shorter events, 9.7 us)
Async XLA Ops:
  1.0 35.8 %copy-start.5 = (bf16[2,2,64,512]{3,2,1,0:T(8,128)(2,1)}, bf16[2,2,64,512]{3,2,1,0:T(8,128)(2,1)S(1)}, u32[]{:S(2)}) copy-start(bf16[2,2,64,512]{3,2,1,0:T(8,128)(2,1)S(1)} %broadcast_select_fusion.2.refs_0_) | copy-start | bytes 786436
  1.0 8.2 %collective-permute-start.10 = (bf16[2,2,64,512]{3,2,1,0:T(8,128)(2,1)S(1)}, bf16[2,2,64,512]{3,2,1,0:T(8,128)(2,1)S(1)}, u32[]{:S(2)}, u32[]{:S(2)}) collective-permute-start(bf16[2,2,64,512]{3,2,1,0:T(8,128)(2,1)S(1)} %broadcast_select_fusion.2.refs_0_), channel_id=1, source_target_pairs={{4,0},{5,1},{6,2},{7,3},{0,4},{1,5},{2,6},{3,7},{12,8},{13,9},{14,... | collective-permute-start | bytes 786440 | tf_op jit(solution)/shard_map/ppermute | solution.py:20
  3.2 6.7 %collective-permute-start.12 = (bf16[2,2,64,512]{3,2,1,0:T(8,128)(2,1)S(1)}, bf16[2,2,64,512]{3,2,1,0:T(8,128)(2,1)S(1)}, u32[]{:S(2)}, u32[]{:S(2)}) collective-permute-start(bf16[2,2,64,512]{3,2,1,0:T(8,128)(2,1)S(1)} %broadcast_select_fusion.2.refs_0_), channel_id=1, source_target_pairs={{8,4},{9,5},{10,6},{11,7},{4,8},{5,9},{6,10},{7,11},{24,20},{25,21... | collective-permute-start | bytes 786440 | tf_op jit(solution)/shard_map/ppermute | solution.py:20
  9.2 27.6 %copy-start.9 = (bf16[2,2,64,512]{3,2,1,0:T(8,128)(2,1)}, bf16[2,2,64,512]{3,2,1,0:T(8,128)(2,1)S(1)}, u32[]{:S(2)}) copy-start(bf16[2,2,64,512]{3,2,1,0:T(8,128)(2,1)S(1)} %collective-permute-done.10.refs_2_) | copy-start | bytes 786436
  9.2 2.0 collective-permute-start.14
  9.9 9.9 %collective-permute-start.13 = (bf16[2,2,64,512]{3,2,1,0:T(8,128)(2,1)S(1)}, bf16[2,2,64,512]{3,2,1,0:T(8,128)(2,1)S(1)}, u32[]{:S(2)}, u32[]{:S(2)}) collective-permute-start(bf16[2,2,64,512]{3,2,1,0:T(8,128)(2,1)S(1)} %collective-permute-done.12), channel_id=1, source_target_pairs={{4,0},{5,1},{6,2},{7,3},{8,12},{9,13},{10,14},{11,15},{20,16},{21,... | collective-permute-start | bytes 786440 | tf_op jit(solution)/shard_map/ppermute | solution.py:20
  11.2 14.2 %collective-permute-start.16 = (bf16[2,2,64,512]{3,2,1,0:T(8,128)(2,1)S(1)}, bf16[2,2,64,512]{3,2,1,0:T(8,128)(2,1)S(1)}, u32[]{:S(2)}, u32[]{:S(2)}) collective-permute-start(bf16[2,2,64,512]{3,2,1,0:T(8,128)(2,1)S(1)} %collective-permute-done.14), channel_id=1, source_target_pairs={{4,0},{5,1},{6,2},{7,3},{8,12},{9,13},{10,14},{11,15},{20,16},{21,... | collective-permute-start | bytes 786440 | tf_op jit(solution)/shard_map/ppermute | solution.py:20
  12.5 14.3 %collective-permute-start.9 = (bf16[2,2,64,512]{3,2,1,0:T(8,128)(2,1)S(1)}, bf16[2,2,64,512]{3,2,1,0:T(8,128)(2,1)S(1)}, u32[]{:S(2)}, u32[]{:S(2)}) collective-permute-start(bf16[2,2,64,512]{3,2,1,0:T(8,128)(2,1)S(1)} %broadcast_select_fusion.2.refs_0_), channel_id=1, source_target_pairs={{0,2},{1,3},{2,0},{3,1},{4,6},{5,7},{6,4},{7,5},{8,10},{9,11},{10,... | collective-permute-start | bytes 786440 | tf_op jit(solution)/shard_map/ppermute | solution.py:20
  13.7 13.1 %collective-permute-start.11 = (bf16[2,2,64,512]{3,2,1,0:T(8,128)(2,1)S(1)}, bf16[2,2,64,512]{3,2,1,0:T(8,128)(2,1)S(1)}, u32[]{:S(2)}, u32[]{:S(2)}) collective-permute-start(bf16[2,2,64,512]{3,2,1,0:T(8,128)(2,1)S(1)} %collective-permute-done.10.refs_2_), channel_id=1, source_target_pairs={{0,2},{1,3},{2,0},{3,1},{4,6},{5,7},{6,4},{7,5},{8,10},{9,11},{10,... | collective-permute-start | bytes 786440 | tf_op jit(solution)/shard_map/ppermute | solution.py:20
  19.8 17.0 %copy-start.2 = (bf16[2,2,64,512]{3,2,1,0:T(8,128)(2,1)}, bf16[2,2,64,512]{3,2,1,0:T(8,128)(2,1)S(1)}, u32[]{:S(2)}) copy-start(bf16[2,2,64,512]{3,2,1,0:T(8,128)(2,1)S(1)} %add.21.refs_4_) | copy-start | bytes 786436
  19.8 10.6 %collective-permute-start.15 = (bf16[2,2,64,512]{3,2,1,0:T(8,128)(2,1)S(1)}, bf16[2,2,64,512]{3,2,1,0:T(8,128)(2,1)S(1)}, u32[]{:S(2)}, u32[]{:S(2)}) collective-permute-start(bf16[2,2,64,512]{3,2,1,0:T(8,128)(2,1)S(1)} %add.21.refs_4_), channel_id=1, source_target_pairs={{0,2},{1,3},{2,0},{3,1},{4,6},{5,7},{6,4},{7,5},{8,10},{9,11},{10,... | collective-permute-start | bytes 786440 | tf_op jit(solution)/shard_map/ppermute | solution.py:20
  25.5 11.3 %copy-start.3 = (bf16[2,2,64,512]{3,2,1,0:T(8,128)(2,1)}, bf16[2,2,64,512]{3,2,1,0:T(8,128)(2,1)S(1)}, u32[]{:S(2)}) copy-start(bf16[2,2,64,512]{3,2,1,0:T(8,128)(2,1)S(1)} %add.22.refs_6_) | copy-start | bytes 786436
  25.5 10.5 %collective-permute-start.17 = (bf16[2,2,64,512]{3,2,1,0:T(8,128)(2,1)S(1)}, bf16[2,2,64,512]{3,2,1,0:T(8,128)(2,1)S(1)}, u32[]{:S(2)}, u32[]{:S(2)}) collective-permute-start(bf16[2,2,64,512]{3,2,1,0:T(8,128)(2,1)S(1)} %add.22.refs_6_), channel_id=1, source_target_pairs={{0,2},{1,3},{2,0},{3,1},{4,6},{5,7},{6,4},{7,5},{8,10},{9,11},{10,... | collective-permute-start | bytes 786440 | tf_op jit(solution)/shard_map/ppermute | solution.py:20
  26.8 10.0 %copy-start.10 = (bf16[2,2,64,512]{3,2,1,0:T(8,128)(2,1)}, bf16[2,2,64,512]{3,2,1,0:T(8,128)(2,1)S(1)}, u32[]{:S(2)}) copy-start(bf16[2,2,64,512]{3,2,1,0:T(8,128)(2,1)S(1)} %collective-permute-done.9.refs_1_) | copy-start | bytes 786436
  39.9 35.8 %collective-permute-start.18 = (bf16[2,2,512,512]{3,2,1,0:T(8,128)(2,1)}, bf16[2,2,512,512]{3,2,1,0:T(8,128)(2,1)}, u32[]{:S(2)}, u32[]{:S(2)}) collective-permute-start(bf16[2,2,512,512]{3,2,1,0:T(8,128)(2,1)} %collect.1), channel_id=1, source_target_pairs={{0,1},{1,0},{2,3},{3,2},{4,5},{5,4},{6,7},{7,6},{8,9},{9,8},{10,11... | collective-permute-start | bytes 6291464 | tf_op jit(solution)/shard_map/ppermute | solution.py:29
  44.8 2.8 %collective-permute-start.1 = (bf16[8,2,2,32,512]{4,3,2,1,0:T(8,128)(2,1)S(1)}, bf16[8,2,2,32,512]{4,3,2,1,0:T(8,128)(2,1)S(1)}, u32[]{:S(2)}, u32[]{:S(2)}) collective-permute-start(bf16[8,2,2,32,512]{4,3,2,1,0:T(8,128)(2,1)S(1)} %bitcast.19), channel_id=1, source_target_pairs={{0,1},{1,0},{2,3},{3,2},{4,5},{5,4},{6,7},{7,6},{8,9},{9,8},{10,11... | collective-permute-start | bytes 3145736 | tf_op jit(solution)/shard_map/ppermute | solution.py:29
  48.5 27.3 %copy-start = (bf16[2,2,512,512]{3,2,1,0:T(8,128)(2,1)S(1)}, bf16[2,2,512,512]{3,2,1,0:T(8,128)(2,1)}, u32[]{:S(2)}) copy-start(bf16[2,2,512,512]{3,2,1,0:T(8,128)(2,1)} %collect.1) | copy-start | bytes 6291460
  51.6 24.1 %copy-start.25 = (bf16[2,2,2,32,512]{4,3,2,1,0:T(8,128)(2,1)S(1)}, bf16[2,2,2,32,512]{4,3,2,1,0:T(8,128)(2,1)}, u32[]{:S(2)}) copy-start(bf16[2,2,2,32,512]{4,3,2,1,0:T(8,128)(2,1)} %get-tuple-element.31) | copy-start | bytes 786436
  51.6 13.1 %collective-permute-start.2 = (bf16[2,2,2,32,512]{4,3,2,1,0:T(8,128)(2,1)}, bf16[2,2,2,32,512]{4,3,2,1,0:T(8,128)(2,1)}, u32[]{:S(2)}, u32[]{:S(2)}) collective-permute-start(bf16[2,2,2,32,512]{4,3,2,1,0:T(8,128)(2,1)} %get-tuple-element.25), channel_id=1, source_target_pairs={{0,2},{1,3},{2,0},{3,1},{4,6},{5,7},{6,4},{7,5},{8,10},{9,11},{10,... | collective-permute-start | bytes 786440 | tf_op jit(solution)/shard_map/ppermute | solution.py:20
  52.8 21.9 %collective-permute-start.3 = (bf16[2,2,2,32,512]{4,3,2,1,0:T(8,128)(2,1)}, bf16[2,2,2,32,512]{4,3,2,1,0:T(8,128)(2,1)}, u32[]{:S(2)}, u32[]{:S(2)}) collective-permute-start(bf16[2,2,2,32,512]{4,3,2,1,0:T(8,128)(2,1)} %get-tuple-element.26), channel_id=1, source_target_pairs={{0,4},{1,5},{2,6},{3,7},{4,0},{5,1},{6,2},{7,3},{8,12},{9,13},{10,... | collective-permute-start | bytes 786440 | tf_op jit(solution)/shard_map/ppermute | solution.py:20
  62.2 99.4 %copy-start.6 = (bf16[1040,256]{1,0:T(8,128)(2,1)}, bf16[1040,256]{1,0:T(8,128)(2,1)S(1)}, u32[]{:S(2)}) copy-start(bf16[1040,256]{1,0:T(8,128)(2,1)S(1)} %pad_maximum_fusion.refs_0_) | copy-start | bytes 1597444
  62.2 24.0 %collective-permute-start.4 = (bf16[2,2,2,32,512]{4,3,2,1,0:T(8,128)(2,1)}, bf16[2,2,2,32,512]{4,3,2,1,0:T(8,128)(2,1)S(1)}, u32[]{:S(2)}, u32[]{:S(2)}) collective-permute-start(bf16[2,2,2,32,512]{4,3,2,1,0:T(8,128)(2,1)} %get-tuple-element.27), channel_id=1, source_target_pairs={{0,6},{1,7},{2,4},{3,5},{4,2},{5,3},{6,0},{7,1},{8,14},{9,15},{10,... | collective-permute-start | bytes 786440 | tf_op jit(solution)/shard_map/ppermute | solution.py:20
  62.3 24.0 %collective-permute-start.5 = (bf16[2,2,2,32,512]{4,3,2,1,0:T(8,128)(2,1)}, bf16[2,2,2,32,512]{4,3,2,1,0:T(8,128)(2,1)S(1)}, u32[]{:S(2)}, u32[]{:S(2)}) collective-permute-start(bf16[2,2,2,32,512]{4,3,2,1,0:T(8,128)(2,1)} %get-tuple-element.28), channel_id=1, source_target_pairs={{0,8},{1,9},{2,10},{3,11},{4,12},{5,13},{6,14},{7,15},{8,0},{9,1},... | collective-permute-start | bytes 786440 | tf_op jit(solution)/shard_map/ppermute | solution.py:20
  64.7 35.0 %collective-permute-start.6 = (bf16[2,2,2,32,512]{4,3,2,1,0:T(8,128)(2,1)}, bf16[2,2,2,32,512]{4,3,2,1,0:T(8,128)(2,1)}, u32[]{:S(2)}, u32[]{:S(2)}) collective-permute-start(bf16[2,2,2,32,512]{4,3,2,1,0:T(8,128)(2,1)} %get-tuple-element.29), channel_id=1, source_target_pairs={{0,10},{1,11},{2,8},{3,9},{4,14},{5,15},{6,12},{7,13},{8,2},{9,3},... | collective-permute-start | bytes 786440 | tf_op jit(solution)/shard_map/ppermute | solution.py:20
  74.7 25.0 %collective-permute-start.7 = (bf16[2,2,2,32,512]{4,3,2,1,0:T(8,128)(2,1)}, bf16[2,2,2,32,512]{4,3,2,1,0:T(8,128)(2,1)}, u32[]{:S(2)}, u32[]{:S(2)}) collective-permute-start(bf16[2,2,2,32,512]{4,3,2,1,0:T(8,128)(2,1)} %get-tuple-element.30), channel_id=1, source_target_pairs={{0,12},{1,13},{2,14},{3,15},{4,8},{5,9},{6,10},{7,11},{8,4},{9,5},... | collective-permute-start | bytes 786440 | tf_op jit(solution)/shard_map/ppermute | solution.py:20
  75.7 24.0 %collective-permute-start.8 = (bf16[2,2,2,32,512]{4,3,2,1,0:T(8,128)(2,1)S(1)}, bf16[2,2,2,32,512]{4,3,2,1,0:T(8,128)(2,1)}, u32[]{:S(2)}, u32[]{:S(2)}) collective-permute-start(bf16[2,2,2,32,512]{4,3,2,1,0:T(8,128)(2,1)S(1)} %copy-done.25), channel_id=1, source_target_pairs={{0,14},{1,15},{2,12},{3,13},{4,10},{5,11},{6,8},{7,9},{8,6},{9,7},... | collective-permute-start | bytes 786440 | tf_op jit(solution)/shard_map/ppermute | solution.py:20
  86.3 13.4 %copy-start.26 = (bf16[2,2,2,32,512]{4,3,2,1,0:T(8,128)(2,1)}, bf16[2,2,2,32,512]{4,3,2,1,0:T(8,128)(2,1)S(1)}, u32[]{:S(2)}) copy-start(bf16[2,2,2,32,512]{4,3,2,1,0:T(8,128)(2,1)S(1)} %collective-permute-done.4.refs_3_) | copy-start | bytes 786436
  86.3 25.0 %collective-permute-start.21 = (bf16[1040,256]{1,0:T(8,128)(2,1)S(1)}, bf16[1040,256]{1,0:T(8,128)(2,1)S(1)}, u32[]{:S(2)}, u32[]{:S(2)}) collective-permute-start(bf16[1040,256]{1,0:T(8,128)(2,1)S(1)} %pad_maximum_fusion.refs_0_), channel_id=1, source_target_pairs={{4,0},{5,1},{6,2},{7,3},{0,4},{1,5},{2,6},{3,7},{12,8},{13,9},{14,... | collective-permute-start | bytes 1597448 | tf_op jit(solution)/shard_map/ppermute | solution.py:20
  86.3 13.4 %copy-start.27 = (bf16[2,2,2,32,512]{4,3,2,1,0:T(8,128)(2,1)}, bf16[2,2,2,32,512]{4,3,2,1,0:T(8,128)(2,1)S(1)}, u32[]{:S(2)}) copy-start(bf16[2,2,2,32,512]{4,3,2,1,0:T(8,128)(2,1)S(1)} %collective-permute-done.5.refs_4_) | copy-start | bytes 786436
  108.1 55.8 %collective-permute-start.19 = (bf16[2,512,1024]{2,1,0:T(8,128)(2,1)}, bf16[2,512,1024]{2,1,0:T(8,128)(2,1)}, u32[]{:S(2)}, u32[]{:S(2)}) collective-permute-start(bf16[2,512,1024]{2,1,0:T(8,128)(2,1)} %contract_stem.1.refs_2_), channel_id=1, source_target_pairs={{0,1},{1,0},{2,3},{3,2},{4,5},{5,4},{6,7},{7,6},{8,9},{9,8},{10,11... | collective-permute-start | bytes 6291464 | tf_op jit(solution)/shard_map/ppermute | solution.py:29
  111.3 38.5 %copy-start.21 = (bf16[1040,256]{1,0:T(8,128)(2,1)}, bf16[1040,256]{1,0:T(8,128)(2,1)S(1)}, u32[]{:S(2)}) copy-start(bf16[1040,256]{1,0:T(8,128)(2,1)S(1)} %collective-permute-done.21.refs_0_) | copy-start | bytes 1597444
  111.3 1.4 collective-permute-start.27
  112.0 2.0 collective-permute-start.25
  112.7 36.6 %collective-permute-start.31 = (bf16[1040,256]{1,0:T(8,128)(2,1)S(1)}, bf16[1040,256]{1,0:T(8,128)(2,1)S(1)}, u32[]{:S(2)}, u32[]{:S(2)}) collective-permute-start(bf16[1040,256]{1,0:T(8,128)(2,1)S(1)} %collective-permute-done.27), channel_id=1, source_target_pairs={{4,0},{5,1},{6,2},{7,3},{8,12},{9,13},{10,14},{11,15},{20,16},{21,... | collective-permute-start | bytes 1597448 | tf_op jit(solution)/shard_map/ppermute | solution.py:20
  114.0 47.2 %collective-permute-start.26 = (bf16[1040,256]{1,0:T(8,128)(2,1)S(1)}, bf16[1040,256]{1,0:T(8,128)(2,1)S(1)}, u32[]{:S(2)}, u32[]{:S(2)}) collective-permute-start(bf16[1040,256]{1,0:T(8,128)(2,1)S(1)} %collective-permute-done.25), channel_id=1, source_target_pairs={{4,0},{5,1},{6,2},{7,3},{8,12},{9,13},{10,14},{11,15},{20,16},{21,... | collective-permute-start | bytes 1597448 | tf_op jit(solution)/shard_map/ppermute | solution.py:20
  149.4 14.5 %copy-start.8 = (bf16[1040,256]{1,0:T(8,128)(2,1)}, bf16[1040,256]{1,0:T(8,128)(2,1)S(1)}, u32[]{:S(2)}) copy-start(bf16[1040,256]{1,0:T(8,128)(2,1)S(1)} %add.24.refs_0_) | copy-start | bytes 1597444
  149.4 13.6 %collective-permute-start.32 = (bf16[1040,256]{1,0:T(8,128)(2,1)S(1)}, bf16[1040,256]{1,0:T(8,128)(2,1)S(1)}, u32[]{:S(2)}, u32[]{:S(2)}) collective-permute-start(bf16[1040,256]{1,0:T(8,128)(2,1)S(1)} %add.24.refs_0_), channel_id=1, source_target_pairs={{0,2},{1,3},{2,0},{3,1},{4,6},{5,7},{6,4},{7,5},{8,10},{9,11},{10,... | collective-permute-start | bytes 1597448 | tf_op jit(solution)/shard_map/ppermute | solution.py:20
  161.3 10.2 %copy-start.7 = (bf16[1040,256]{1,0:T(8,128)(2,1)}, bf16[1040,256]{1,0:T(8,128)(2,1)S(1)}, u32[]{:S(2)}) copy-start(bf16[1040,256]{1,0:T(8,128)(2,1)S(1)} %add.23.refs_0_) | copy-start | bytes 1597444
  161.3 14.4 %collective-permute-start.28 = (bf16[1040,256]{1,0:T(8,128)(2,1)S(1)}, bf16[1040,256]{1,0:T(8,128)(2,1)}, u32[]{:S(2)}, u32[]{:S(2)}) collective-permute-start(bf16[1040,256]{1,0:T(8,128)(2,1)S(1)} %add.23.refs_0_), channel_id=1, source_target_pairs={{0,2},{1,3},{2,0},{3,1},{4,6},{5,7},{6,4},{7,5},{8,10},{9,11},{10,... | collective-permute-start | bytes 1597448 | tf_op jit(solution)/shard_map/ppermute | solution.py:20
  161.6 45.7 %collective-permute-start = (bf16[1040,256]{1,0:T(8,128)(2,1)S(1)}, bf16[1040,256]{1,0:T(8,128)(2,1)S(1)}, u32[]{:S(2)}, u32[]{:S(2)}) collective-permute-start(bf16[1040,256]{1,0:T(8,128)(2,1)S(1)} %pad_maximum_fusion.refs_0_), channel_id=1, source_target_pairs={{0,2},{1,3},{2,0},{3,1},{4,6},{5,7},{6,4},{7,5},{8,10},{9,11},{10,... | collective-permute-start | bytes 1597448 | tf_op jit(solution)/shard_map/ppermute | solution.py:20
  162.8 34.9 %collective-permute-start.22 = (bf16[1040,256]{1,0:T(8,128)(2,1)}, bf16[1040,256]{1,0:T(8,128)(2,1)S(1)}, u32[]{:S(2)}, u32[]{:S(2)}) collective-permute-start(bf16[1040,256]{1,0:T(8,128)(2,1)} %copy-done.21), channel_id=1, source_target_pairs={{0,2},{1,3},{2,0},{3,1},{4,6},{5,7},{6,4},{7,5},{8,10},{9,11},{10,... | collective-permute-start | bytes 1597448 | tf_op jit(solution)/shard_map/ppermute | solution.py:20
  171.5 44.2 %collective-permute-start.33 = (bf16[2,2,32,256]{3,2,1,0:T(8,128)(2,1)}, bf16[2,2,32,256]{3,2,1,0:T(8,128)(2,1)S(1)}, u32[]{:S(2)}, u32[]{:S(2)}) collective-permute-start(bf16[2,2,32,256]{3,2,1,0:T(8,128)(2,1)} %get-tuple-element.40), channel_id=1, source_target_pairs={{0,12},{1,13},{2,14},{3,15},{4,8},{5,9},{6,10},{7,11},{8,4},{9,5},... | collective-permute-start | bytes 196616 | tf_op jit(solution)/shard_map/ppermute | solution.py:20
  173.7 43.6 %collective-permute-start.34 = (bf16[2,2,32,256]{3,2,1,0:T(8,128)(2,1)}, bf16[2,2,32,256]{3,2,1,0:T(8,128)(2,1)S(1)}, u32[]{:S(2)}, u32[]{:S(2)}) collective-permute-start(bf16[2,2,32,256]{3,2,1,0:T(8,128)(2,1)} %get-tuple-element.41), channel_id=1, source_target_pairs={{0,14},{1,15},{2,12},{3,13},{4,10},{5,11},{6,8},{7,9},{8,6},{9,7},... | collective-permute-start | bytes 196616 | tf_op jit(solution)/shard_map/ppermute | solution.py:20
  183.3 34.4 %collective-permute-start.29 = (bf16[2,2,32,256]{3,2,1,0:T(8,128)(2,1)}, bf16[2,2,32,256]{3,2,1,0:T(8,128)(2,1)S(1)}, u32[]{:S(2)}, u32[]{:S(2)}) collective-permute-start(bf16[2,2,32,256]{3,2,1,0:T(8,128)(2,1)} %get-tuple-element.38), channel_id=1, source_target_pairs={{0,8},{1,9},{2,10},{3,11},{4,12},{5,13},{6,14},{7,15},{8,0},{9,1},... | collective-permute-start | bytes 196616 | tf_op jit(solution)/shard_map/ppermute | solution.py:20
  197.8 19.9 %collective-permute-start.30 = (bf16[2,2,32,256]{3,2,1,0:T(8,128)(2,1)}, bf16[2,2,32,256]{3,2,1,0:T(8,128)(2,1)S(1)}, u32[]{:S(2)}, u32[]{:S(2)}) collective-permute-start(bf16[2,2,32,256]{3,2,1,0:T(8,128)(2,1)} %get-tuple-element.39), channel_id=1, source_target_pairs={{0,10},{1,11},{2,8},{3,9},{4,14},{5,15},{6,12},{7,13},{8,2},{9,3},... | collective-permute-start | bytes 196616 | tf_op jit(solution)/shard_map/ppermute | solution.py:20
  207.3 10.4 %collective-permute-start.23 = (bf16[2,2,32,256]{3,2,1,0:T(8,128)(2,1)}, bf16[2,2,32,256]{3,2,1,0:T(8,128)(2,1)S(1)}, u32[]{:S(2)}, u32[]{:S(2)}) collective-permute-start(bf16[2,2,32,256]{3,2,1,0:T(8,128)(2,1)} %get-tuple-element.36), channel_id=1, source_target_pairs={{0,4},{1,5},{2,6},{3,7},{4,0},{5,1},{6,2},{7,3},{8,12},{9,13},{10,... | collective-permute-start | bytes 196616 | tf_op jit(solution)/shard_map/ppermute | solution.py:20
  215.7 4.1 %collective-permute-start.24 = (bf16[2,2,32,256]{3,2,1,0:T(8,128)(2,1)S(1)}, bf16[2,2,32,256]{3,2,1,0:T(8,128)(2,1)S(1)}, u32[]{:S(2)}, u32[]{:S(2)}) collective-permute-start(bf16[2,2,32,256]{3,2,1,0:T(8,128)(2,1)S(1)} %copy-done.28), channel_id=1, source_target_pairs={{0,6},{1,7},{2,4},{3,5},{4,2},{5,3},{6,0},{7,1},{8,14},{9,15},{10,... | collective-permute-start | bytes 196616 | tf_op jit(solution)/shard_map/ppermute | solution.py:20
  217.3 3.3 %collective-permute-start.20 = (bf16[2,2,32,256]{3,2,1,0:T(8,128)(2,1)}, bf16[2,2,32,256]{3,2,1,0:T(8,128)(2,1)S(1)}, u32[]{:S(2)}, u32[]{:S(2)}) collective-permute-start(bf16[2,2,32,256]{3,2,1,0:T(8,128)(2,1)} %get-tuple-element.35), channel_id=1, source_target_pairs={{0,2},{1,3},{2,0},{3,1},{4,6},{5,7},{6,4},{7,5},{8,10},{9,11},{10,... | collective-permute-start | bytes 196616 | tf_op jit(solution)/shard_map/ppermute | solution.py:20
  (17 other events, 54.1 us)
where the time goes:
time: 231 us; the launch traced here: 227 us
  waiting for transfers between devices  108 us (47%)
  Pallas kernels  55 us (24%)
  starting transfers between devices  46.6 us (20%)
  local copies, waits for them, and re-layouts  11 us (5%)
  other arithmetic  6 us (3%)
    ppermute x32, waiting for transfers between devices, permute(): return lax.ppermute(value, AXES, full)  106 us
    ppermute x32, starting transfers between devices, permute(): return lax.ppermute(value, AXES, full)  41.4 us
    pallas_call x4, Pallas kernels, contract_samples(): pl.pallas_call(functools.partial(sample_kernel, groups, many), grid=(loca...  30.3 us
    pallas_call x1, Pallas kernels, contract_stem(): pl.pallas_call(stem_kernel, grid=(local,), in_specs=[piece] * len(arrived...  8.43 us
    pallas_call x1, Pallas kernels, tables(): pl.pallas_call(functools.partial(table_kernel, inner, count_mb, relative)...  6.6 us
    unnamed x63, local copies, waits for them, and re-layouts  6.26 us
    ppermute x3, starting transfers between devices, swap_mb(): return lax.ppermute(value, AXES, [(m, m ^ offset) for m in range(count)])  5.28 us
  transfers between devices with their start and end apart: 35, of which 13 were waited for; matrix products, arithmetic and copies ran while one was open for 5% of the time, Pallas kernels for 21%

commit v1 on v0

v1 whole, which is shorter than its diff:
```python
import functools

import jax
import jax.numpy as jnp
from jax import lax
from jax.experimental import pallas as pl
from jax.experimental.pallas import tpu as pltpu
from jax.sharding import PartitionSpec as P

AXES = ("ma", "mb")
BF16 = jnp.bfloat16
F32 = jnp.float32
VMEM = pl.BlockSpec(memory_space=pltpu.VMEM)
SMEM = pl.BlockSpec(memory_space=pltpu.SMEM)

LIMIT = 24 * 1024 * 1024


def params():
    return pltpu.CompilerParams(vmem_limit_bytes=LIMIT)


def permute(value, pairs):
    count = lax.axis_size("mb")
    full = [(a * count + c, b * count + c) for a, b in pairs for c in range(count)]
    return lax.ppermute(value, AXES, full)


def swap_ma(value, offset):
    return permute(value, [(m, m ^ offset) for m in range(lax.axis_size("ma"))])


def swap_mb(value, offset):
    count = lax.axis_size("ma") * lax.axis_size("mb")
    return lax.ppermute(value, AXES, [(m, m ^ offset) for m in range(count)])


def relay_groups(length):
    owner, groups = {}, {}
    for distance in range(1, length):
        for z in range(length):
            for x in range(1, length):
                if abs((z ^ x) - z) != distance:
                    continue
                sender = z + (1 if (z ^ x) > z else -1)
                held = sender ^ z ^ x
                key = (x, owner.get((sender, held)))
                owner[(z, x)] = key
                groups.setdefault(key, []).append((sender, z))
    return groups


def relay_gather(value):
    length = lax.axis_size("ma") // 2
    sent = {None: value}
    slots = {0: [value]}
    for key, moves in relay_groups(length).items():
        pairs = [(2 * a + y, 2 * b + y) for a, b in moves for y in range(2)]
        sent[key] = permute(sent[key[1]], pairs)
        slots.setdefault(key[0], []).append(sent[key])
    gathered = {}
    for x in sorted(slots):
        whole = functools.reduce(jnp.add, slots[x])
        gathered[2 * x] = whole
        gathered[2 * x + 1] = swap_ma(whole, 1)
    return [gathered[d] for d in range(2 * length)]


def scalars(*values):
    return jnp.stack([jnp.asarray(v, jnp.int32) for v in values])


def pack_kernel(count, place_ref, *refs):
    sources, outs = refs[: -count * refs[0].shape[2]], refs[-count * refs[0].shape[2] :]
    for number, out_ref in enumerate(outs):
        l, d = number // count, number % count
        for s, source in enumerate(sources):
            out_ref[s] = source[place_ref[0] ^ d, :, l]


def pack(here_ma, sources):
    count, parts, local, inner, width = sources[0].shape
    shape = jax.ShapeDtypeStruct((len(sources), parts, inner, width), BF16)
    outs = pl.pallas_call(
        functools.partial(pack_kernel, count),
        in_specs=[SMEM] + [VMEM] * len(sources),
        out_specs=[VMEM] * (count * local),
        out_shape=[shape] * (count * local),
        compiler_params=params(),
        name="pack",
    )(scalars(here_ma), *sources)
    return [outs[l * count : (l + 1) * count] for l in range(local)]


def table_kernel(inner, count_mb, relative, slots, place_ref, relabel_ref, *refs):
    mine, other, refs = refs[:slots], refs[slots : 2 * slots], refs[2 * slots :]
    stem_ref, final_ref, product_ref, first_ref, second_ref, right_ref = refs
    depth = mine[0].shape[2]

    def gather(first, second):
        for d in range(slots):
            start = pl.multiple_of((place_ref[2] ^ d) * depth, depth)
            first_ref[:, :, pl.ds(start, depth), :] = first[d][...]
            second_ref[:, :, pl.ds(start, depth), :] = second[d][...]

    @pl.when(place_ref[3] == 0)
    def _():
        gather(mine, other)

    @pl.when(place_ref[3] != 0)
    def _():
        gather(other, mine)

    size = first_ref.shape[2]
    column = lax.broadcasted_iota(jnp.int32, (size, size), 0)
    seat, rest = column // inner, column % inner
    ma, mb = seat // count_mb, seat % count_mb
    near = (((ma ^ place_ref[0]) * count_mb) + (mb ^ place_ref[1])) * inner + rest
    for r in range(2):
        position = near if relative[r] else column
        selector = jnp.where(relabel_ref[r : r + 1, :] == position, 1.0, 0.0).astype(BF16)
        for p in range(2):
            ordered = jnp.dot(selector, first_ref[r, p], preferred_element_type=F32)
            if r == 0:
                turned = ordered.T.astype(BF16)
                if p == 0:
                    stem_ref[:size, :size] = turned
                    stem_ref[size:, size:] = turned
                else:
                    stem_ref[size:, :size] = turned
                    stem_ref[:size, size:] = -turned
            else:
                ordered = ordered.astype(BF16)
                if p == 0:
                    final_ref[:size, :size] = ordered
                    final_ref[size:, size:] = ordered
                else:
                    final_ref[:size, size:] = ordered
                    final_ref[size:, :size] = -ordered
    width = second_ref.shape[2]
    right_ref[:width, :width] = second_ref[1, 0]
    right_ref[:width, width:] = second_ref[1, 1]
    right_ref[width:, :width] = -second_ref[1, 1]
    right_ref[width:, width:] = second_ref[1, 0]
    both = jnp.dot(second_ref[0, 0], right_ref[:width, :], preferred_element_type=F32)
    both += jnp.dot(second_ref[0, 1], right_ref[width:, :], preferred_element_type=F32)
    both = both.astype(BF16)
    product_ref[:width, :] = both
    product_ref[width:, :width] = -both[:, width:]
    product_ref[width:, width:] = both[:, :width]


def tables(here, relabel, mine, other, inner, count_mb, relative):
    rounds, parts, depth, width = mine[0].shape
    size = depth * len(mine)
    tensors = pltpu.VMEM((rounds, parts, size, width), BF16)
    return pl.pallas_call(
        functools.partial(table_kernel, inner, count_mb, relative, len(mine)),
        in_specs=[SMEM] + [VMEM] * (1 + 2 * len(mine)),
        out_specs=[VMEM] * 3,
        out_shape=[jax.ShapeDtypeStruct((2 * size, 2 * size), BF16)] * 3,
        scratch_shapes=[tensors, tensors, pltpu.VMEM((2 * size, 2 * size), BF16)],
        cost_estimate=pl.CostEstimate(
            flops=16 * size**3, bytes_accessed=40 * size * size, transcendentals=0
        ),
        compiler_params=params(),
        name="tables",
    )(here, relabel, *mine, *other)


def stem_kernel(*refs):
    arrived, (table_ref, product_ref, out_ref, rows_ref, mid_ref) = refs[:-5], refs[-5:]
    seats, parts, inner, _ = arrived[0].shape
    for d, piece in enumerate(arrived):
        for s in range(seats):
            for p in range(parts):
                start = ((p * len(arrived) + d) * seats + s) * inner
                rows_ref[start : start + inner, :] = piece[s, p]
    half = mid_ref.shape[0] // 2
    step = min(256, half)
    for top in range(0, 2 * half, step):
        part = jnp.dot(table_ref[top : top + step, :], rows_ref[...], preferred_element_type=F32)
        mid_ref[top : top + step, :] = part.astype(BF16)
    depth = mid_ref.shape[1]
    for top in range(0, half, step):
        part = jnp.dot(
            mid_ref[top : top + step, :], product_ref[:depth, :], preferred_element_type=F32
        )
        part += jnp.dot(
            mid_ref[half + top : half + top + step, :],
            product_ref[depth:, :],
            preferred_element_type=F32,
        )
        out_ref[top : top + step, :] = part.astype(BF16)


def contract_stem(arrived, table, product):
    width = arrived[0].shape[3]
    size = table.shape[0]
    return pl.pallas_call(
        stem_kernel,
        in_specs=[VMEM] * (len(arrived) + 2),
        out_specs=VMEM,
        out_shape=jax.ShapeDtypeStruct((size // 2, 2 * width), BF16),
        scratch_shapes=[pltpu.VMEM((size, width), BF16), pltpu.VMEM((size, width), BF16)],
        cost_estimate=pl.CostEstimate(
            flops=2 * (size * size * width + 2 * size * width * width),
            bytes_accessed=4 * (size * width + table.size),
            transcendentals=0,
        ),
        compiler_params=params(),
        name="contract_stem",
    )(*arrived, table, product)


def sample_kernel(groups, first, scale, many, seats, *refs):
    states, stems, refs = refs[:many], refs[many : many + seats], refs[many + seats :]
    before, outs = refs[: -2 - many], refs[-2 - many : -2]
    plus_ref, cross_ref = refs[-2:]
    depth = plus_ref.shape[0]
    width = depth // 2
    rows = stems[0].shape[0]
    inner = rows // groups
    step = min(256, rows)
    for m, state_ref in enumerate(states):
        plus_ref[:width, :] = state_ref[:width, :]
        plus_ref[width:, :] = -state_ref[width:depth, :]
        cross_ref[:width, :] = state_ref[width:depth, :]
        cross_ref[width:, :] = state_ref[:width, :]
        named = state_ref[depth : depth + 16, :].astype(F32)[:1, :]
        for s, stem_ref in enumerate(stems):
            for part, weights in enumerate((plus_ref, cross_ref)):
                total = before[m][s, part].astype(F32) if before else 0.0
                for top in range(0, rows, step):
                    value = jnp.dot(
                        stem_ref[top : top + step, :], weights[...], preferred_element_type=F32
                    )
                    for k in range(step // inner):
                        number = float((top // inner + k) * scale + first)
                        part_of = value[k * inner : (k + 1) * inner, :]
                        total += jnp.where(named == number, part_of, 0.0)
                outs[m][s, part] = total.astype(BF16)


def contract_samples(states, stems, groups, first, scale, before):
    many, seats = len(states), len(stems)
    _, samples = states[0].shape
    rows, width = stems[0].shape
    out = (seats, 2, rows // groups, samples)
    return pl.pallas_call(
        functools.partial(sample_kernel, groups, first, scale, many, seats),
        in_specs=[VMEM] * (many + seats + len(before)),
        out_specs=[VMEM] * many,
        out_shape=[jax.ShapeDtypeStruct(out, BF16)] * many,
        scratch_shapes=[pltpu.VMEM((width, samples), BF16)] * 2,
        cost_estimate=pl.CostEstimate(
            flops=2 * many * rows * width * 2 * samples * seats,
            bytes_accessed=2 * (many * states[0].size + seats * stems[0].size),
            transcendentals=0,
        ),
        compiler_params=params(),
        name="contract_samples",
    )(*states, *stems, *before)


def final_kernel(*refs):
    found, (table_ref, out_ref, rows_ref) = refs[:-3], refs[-3:]
    seats, parts, inner, _ = found[0].shape
    for d, piece in enumerate(found):
        for s in range(seats):
            for p in range(parts):
                start = ((p * len(found) + d) * seats + s) * inner
                rows_ref[start : start + inner, :] = piece[s, p]
    out_ref[...] = lax.dot_general(
        rows_ref[...], table_ref[...], (((0,), (0,)), ((), ())), preferred_element_type=F32
    ).astype(BF16)


def contract_final(found, table):
    samples = found[0].shape[3]
    return pl.pallas_call(
        final_kernel,
        in_specs=[VMEM] * (len(found) + 1),
        out_specs=VMEM,
        out_shape=jax.ShapeDtypeStruct((samples, table.shape[1]), BF16),
        scratch_shapes=[pltpu.VMEM((table.shape[0], samples), BF16)],
        cost_estimate=pl.CostEstimate(
            flops=2 * table.size * samples, bytes_accessed=2 * table.size, transcendentals=0
        ),
        compiler_params=params(),
        name="contract_final",
    )(*found, table)


def is_short(count_ma):
    return count_ma // 2 <= 4


def on_device(
    stem_field, first_branch_tensors, second_branch_tensors, relabel, sample_block, sample_state
):
    count_ma, count_mb = lax.axis_size("ma"), lax.axis_size("mb")
    here_ma, here_mb = lax.axis_index("ma"), lax.axis_index("mb")
    groups = count_ma * count_mb
    local, row_count, parts, width = stem_field.shape
    inner = row_count // groups
    samples = sample_state.shape[0]
    short = is_short(count_ma)

    flat = sample_state.reshape(samples, parts * width).T
    named = jnp.broadcast_to(sample_block[:, 0].astype(BF16)[None, :], (16, samples))
    states = jnp.concatenate([flat, named], axis=0)

    pieces = stem_field.reshape(local, count_ma, count_mb, inner, parts, width)
    pieces = jnp.transpose(pieces, (2, 1, 4, 0, 3, 5))

    if short:
        share = jnp.where(here_mb == 0, first_branch_tensors, second_branch_tensors)
        mine = relay_gather(share)
        other = [swap_mb(value, 1) for value in mine]
        held = [
            lax.dynamic_index_in_dim(pieces, here_mb ^ s, keepdims=False) for s in range(count_mb)
        ]
        sources = [held[0]] + [swap_mb(held[s], s) for s in range(1, count_mb)]
        arrived = [
            [swap_ma(piece, d) if d else piece for d, piece in enumerate(packed)]
            for packed in pack(here_ma, sources)
        ]
        every_state = relay_gather(states)
        here = scalars(here_ma, here_mb, here_ma, here_mb)
    else:
        mine = [lax.all_gather(first_branch_tensors, "ma", axis=2, tiled=True)]
        other = [lax.all_gather(second_branch_tensors, "ma", axis=2, tiled=True)]
        sent = jnp.transpose(pieces, (1, 0, 2, 3, 4, 5))
        sent = sent.reshape((groups,) + sent.shape[2:])
        arrived = lax.all_to_all(sent, AXES, split_axis=0, concat_axis=0, tiled=True)
        arrived = arrived.reshape((count_ma, count_mb) + arrived.shape[1:])
        arrived = [[arrived[d, :, :, l] for d in range(count_ma)] for l in range(local)]
        every_state = lax.all_gather(states, "ma", axis=0)
        every_state = [every_state[d] for d in range(count_ma)]
        here = scalars(0, here_mb, 0, 0)

    table, final_table, product = tables(
        here, relabel, mine, other, inner, count_mb, (short, True)
    )
    found = [[] for _ in range(0, count_ma, 2)]
    for l in range(local):
        own = contract_stem(arrived[l], table, product)
        stems = [own] + [swap_mb(own, s) for s in range(1, count_mb)]
        for pair, before in enumerate(found):
            chosen = every_state[2 * pair : 2 * pair + 2]
            found[pair] = contract_samples(chosen, stems, groups, l, local, before)
    found = [value for pair in found for value in pair]
    if short:
        found = [swap_ma(value, d) if d else value for d, value in enumerate(found)]
    else:
        found = lax.all_to_all(jnp.stack(found), "ma", split_axis=0, concat_axis=0, tiled=True)
        found = [found[d] for d in range(count_ma)]
    return contract_final(found, final_table).reshape(samples, parts, -1)


def solution(mesh):
    placed = (
        P(("cuts", "ma", "mb"), None, None, None),
        P(None, None, "ma", None),
        P(None, None, "ma", None),
        P(),
        P(("cuts", "ma", "mb"), None),
        P(("cuts", "ma", "mb"), None, None),
    )
    return jax.shard_map(
        on_device,
        mesh=mesh,
        in_specs=placed,
        out_specs=P(("cuts", "ma", "mb"), None, None),
        check_vma=False,
    )
```

time: 231 us -> 209 us (0.905)
  Pallas kernels: 55 us -> 29.6 us
  starting transfers between devices: 46.6 us -> 55.5 us
  other arithmetic: 6 us -> 2.53 us
    pallas_call x8 -> x12, Pallas kernels: 51.6 us -> 28.9 us  [the longest x8 20 us: contract_samples(): pl.pallas_call(functools.partial(sample_kernel, groups, first, scale, man...]
    ppermute x32 -> x39, starting transfers between devices: 41.4 us -> 46.5 us  [permute(): return lax.ppermute(value, AXES, full)]
    select_n x1 -> x0, other arithmetic: 3.92 us -> none  [on_device(): every_second = jnp.where(here_mb == 0, other, mine)]
    ppermute x3 -> x11, starting transfers between devices: 5.28 us -> 8.93 us  [swap_mb(): return lax.ppermute(value, AXES, [(m, m ^ offset) for m in range(count)])]
    pallas_call x1, Pallas kernels: 3.43 us -> 0.73 us  [contract_final(): pl.pallas_call(final_kernel, in_specs=[VMEM] * (len(found) + 1), out_spec...]
    unnamed x63 -> x21, local copies, waits for them, and re-layouts: 6.26 us -> 4.71 us
    ppermute x32 -> x39, waiting for transfers between devices: 106 us -> 108 us  [permute(): return lax.ppermute(value, AXES, full)]
  transfers between devices with their start and end apart: 35 -> 50, of which waited for: 13 -> 15; matrix products, arithmetic and copies ran while one was open for 5% -> 5% of each run, Pallas kernels for 21% -> 14%
where the time goes in v1:
time: 209 us; the launch traced here: 206 us
  waiting for transfers between devices  108 us (52%)
  starting transfers between devices  55.5 us (27%)
  Pallas kernels  29.6 us (14%)
  local copies, waits for them, and re-layouts  10.5 us (5%)
  other arithmetic  2.53 us (1%)
    ppermute x39, waiting for transfers between devices, permute(): return lax.ppermute(value, AXES, full)  108 us
    ppermute x39, starting transfers between devices, permute(): return lax.ppermute(value, AXES, full)  46.5 us
    pallas_call x8, Pallas kernels, contract_samples(): pl.pallas_call(functools.partial(sample_kernel, groups, first, scale, man...  20 us
    ppermute x11, starting transfers between devices, swap_mb(): return lax.ppermute(value, AXES, [(m, m ^ offset) for m in range(count)])  8.93 us
    unnamed x21, local copies, waits for them, and re-layouts  4.71 us
    pallas_call x2, Pallas kernels, contract_stem(): pl.pallas_call(stem_kernel, in_specs=[VMEM] * (len(arrived) + 2), out_spe...  4.71 us
    another operation x1, local copies, waits for them, and re-layouts  4.58 us
  transfers between devices with their start and end apart: 50, of which 15 were waited for; matrix products, arithmetic and copies ran while one was open for 5% of the time, Pallas kernels for 14%

profile of v1, /device:TPU:1, one launch (start us, length us, event | category | flops | bytes accessed | tf_op | source)
XLA Modules:
  0.0 206.3 jit_solution(9205237002952957295)
XLA Ops:
  1.0 2.2 %collective-permute-start.10 = (bf16[2,2,64,512]{3,2,1,0:T(8,128)(2,1)S(1)}, bf16[2,2,64,512]{3,2,1,0:T(8,128)(2,1)S(1)}, u32[]{:S(2)}, u32[]{:S(2)}) collective-permute-start(bf16[2,2,64,512]{3,2,1,0:T(8,128)(2,1)S(1)} %broadcast_select_fusion.refs_0_), channel_id=1, source_target_pairs={{4,0},{5,1},{6,2},{7,3},{0,4},{1,5},{2,6},{3,7},{12,8},{13,9},{14,... | collective-permute-start | bytes 786440 | tf_op jit(solution)/shard_map/ppermute | solution.py:26
  3.2 4.6 %constant_dynamic-slice_fusion = (bf16[2,8,1,32,2,512]{5,4,3,2,1,0:T(2,128)(2,1)S(1)}, bf16[2,8,1,32,2,512]{5,4,3,2,1,0:T(2,128)(2,1)}) fusion(bf16[2,8,2,32,2,512]{5,4,3,2,1,0:T(2,128)(2,1)} %bitcast.17, s32[]{:T(128)S(6)} %select_n.16, s32[]{:T(128)S(6)} %select_n.15), kind=kLoop, calls=%fused_computation.6 | loop fusion | bytes 4194312 | tf_op jit(solution)/shard_map/dynamic-slice.1
  11.2 1.4 collective-permute-start.12
  13.7 4.1 %collective-permute-done.9.refs_1_ = bf16[2,2,64,512]{3,2,1,0:T(8,128)(2,1)S(1)} collective-permute-done((bf16[2,2,64,512]{3,2,1,0:T(8,128)(2,1)S(1)}, bf16[2,2,64,512]{3,2,1,0:T(8,128)(2,1)S(1)}, u32[]{:S(2)}, u32[]{:S(2)}) %collective-permute-start.9) | collective-permute-done | bytes 262176 | tf_op jit(solution)/shard_map/ppermute | solution.py:26
  20.7 2.8 %collective-permute-done.11.refs_3_ = bf16[2,2,64,512]{3,2,1,0:T(8,128)(2,1)} collective-permute-done((bf16[2,2,64,512]{3,2,1,0:T(8,128)(2,1)S(1)}, bf16[2,2,64,512]{3,2,1,0:T(8,128)(2,1)}, u32[]{:S(2)}, u32[]{:S(2)}) %collective-permute-start.11) | collective-permute-done | bytes 262176 | tf_op jit(solution)/shard_map/ppermute | solution.py:26
  24.4 11.4 %collective-permute-done.13 = bf16[2,2,64,512]{3,2,1,0:T(8,128)(2,1)S(1)} collective-permute-done((bf16[2,2,64,512]{3,2,1,0:T(8,128)(2,1)}, bf16[2,2,64,512]{3,2,1,0:T(8,128)(2,1)S(1)}, u32[]{:S(2)}, u32[]{:S(2)}) %collective-permute-start.13) | collective-permute-done | bytes 262176 | tf_op jit(solution)/shard_map/ppermute | solution.py:26
  35.7 2.2 %collective-permute-start.20 = (bf16[2,2,64,512]{3,2,1,0:T(8,128)(2,1)S(1)}, bf16[2,2,64,512]{3,2,1,0:T(8,128)(2,1)S(1)}, u32[]{:S(2)}, u32[]{:S(2)}) collective-permute-start(bf16[2,2,64,512]{3,2,1,0:T(8,128)(2,1)S(1)} %collective-permute-done.10.refs_2_), channel_id=1, source_target_pairs={{0,1},{1,0},{2,3},{3,2},{4,5},{5,4},{6,7},{7,6},{8,9},{9,8},{10,11... | collective-permute-start | bytes 786440 | tf_op jit(solution)/shard_map/ppermute | solution.py:35
  41.5 6.2 %collective-permute-done.16 = bf16[2,2,64,512]{3,2,1,0:T(8,128)(2,1)S(1)} collective-permute-done((bf16[2,2,64,512]{3,2,1,0:T(8,128)(2,1)S(1)}, bf16[2,2,64,512]{3,2,1,0:T(8,128)(2,1)S(1)}, u32[]{:S(2)}, u32[]{:S(2)}) %collective-permute-start.16) | collective-permute-done | bytes 262176 | tf_op jit(solution)/shard_map/ppermute | solution.py:26
  49.6 1.3 collective-permute-start.17
  51.4 1.5 copy.19
  54.0 3.6 %collective-permute-done.17.refs_7_ = bf16[2,2,64,512]{3,2,1,0:T(8,128)(2,1)} collective-permute-done((bf16[2,2,64,512]{3,2,1,0:T(8,128)(2,1)S(1)}, bf16[2,2,64,512]{3,2,1,0:T(8,128)(2,1)}, u32[]{:S(2)}, u32[]{:S(2)}) %collective-permute-start.17) | collective-permute-done | bytes 262176 | tf_op jit(solution)/shard_map/ppermute | solution.py:26
  57.6 1.3 collective-permute-start.25
  59.1 3.2 %collective-permute-start.5 = (bf16[2,2,32,512]{3,2,1,0:T(8,128)(2,1)S(1)}, bf16[2,2,32,512]{3,2,1,0:T(8,128)(2,1)S(1)}, u32[]{:S(2)}, u32[]{:S(2)}) collective-permute-start(bf16[2,2,32,512]{3,2,1,0:T(8,128)(2,1)S(1)} %get-tuple-element.44), channel_id=1, source_target_pairs={{0,8},{1,9},{2,10},{3,11},{4,12},{5,13},{6,14},{7,15},{8,0},{9,1},... | collective-permute-start | bytes 393224 | tf_op jit(solution)/shard_map/ppermute | solution.py:26
  62.8 4.7 %collective-permute-done.4.refs_3_ = bf16[2,2,32,512]{3,2,1,0:T(8,128)(2,1)S(1)} collective-permute-done((bf16[2,2,32,512]{3,2,1,0:T(8,128)(2,1)S(1)}, bf16[2,2,32,512]{3,2,1,0:T(8,128)(2,1)S(1)}, u32[]{:S(2)}, u32[]{:S(2)}) %collective-permute-start.4) | collective-permute-done | bytes 131104 | tf_op jit(solution)/shard_map/ppermute | solution.py:26
  67.5 1.3 collective-permute-done.5.refs_4_
  68.8 2.0 collective-permute-start.30
  70.8 3.6 %collective-permute-start.32 = (bf16[2,2,32,512]{3,2,1,0:T(8,128)(2,1)S(1)}, bf16[2,2,32,512]{3,2,1,0:T(8,128)(2,1)S(1)}, u32[]{:S(2)}, u32[]{:S(2)}) collective-permute-start(bf16[2,2,32,512]{3,2,1,0:T(8,128)(2,1)S(1)} %get-tuple-element.56), channel_id=1, source_target_pairs={{0,12},{1,13},{2,14},{3,15},{4,8},{5,9},{6,10},{7,11},{8,4},{9,5},... | collective-permute-start | bytes 393224 | tf_op jit(solution)/shard_map/ppermute | solution.py:26
  75.4 4.1 %tables.1 = (bf16[1024,1024]{1,0:T(8,128)(2,1)S(1)}, bf16[1024,1024]{1,0:T(8,128)(2,1)S(1)}, bf16[1024,1024]{1,0:T(8,128)(2,1)S(1)}) custom-call(s32[4]{0:T(128)S(1)} %pad_add_fusion.place_ref, s32[2,512]{1,0:T(2,128)S(1)} %copy-done.6, bf16[2,2,64,512]{3,2,1,0:T(8,128)(2,1)S(1)} %broadcast_select_fusion.refs_0_, ...), custom_call_target="tpu_custom_call" | custom-call | flops 2147483648 | bytes 10485760 | tf_op jit(solution)/shard_map/tables/pallas_call | solution.py:157
  80.2 5.1 %collective-permute-done.30.refs_4_ = bf16[2,2,32,512]{3,2,1,0:T(8,128)(2,1)S(1)} collective-permute-done((bf16[2,2,32,512]{3,2,1,0:T(8,128)(2,1)S(1)}, bf16[2,2,32,512]{3,2,1,0:T(8,128)(2,1)S(1)}, u32[]{:S(2)}, u32[]{:S(2)}) %collective-permute-start.30) | collective-permute-done | bytes 131104 | tf_op jit(solution)/shard_map/ppermute | solution.py:26
  86.0 2.2 %collective-permute-done.31.refs_5_ = bf16[2,2,32,512]{3,2,1,0:T(8,128)(2,1)S(1)} collective-permute-done((bf16[2,2,32,512]{3,2,1,0:T(8,128)(2,1)S(1)}, bf16[2,2,32,512]{3,2,1,0:T(8,128)(2,1)S(1)}, u32[]{:S(2)}, u32[]{:S(2)}) %collective-permute-start.31) | collective-permute-done | bytes 131104 | tf_op jit(solution)/shard_map/ppermute | solution.py:26
  88.2 2.3 %collective-permute-start.7 = (bf16[2,2,32,512]{3,2,1,0:T(8,128)(2,1)S(1)}, bf16[2,2,32,512]{3,2,1,0:T(8,128)(2,1)S(1)}, u32[]{:S(2)}, u32[]{:S(2)}) collective-permute-start(bf16[2,2,32,512]{3,2,1,0:T(8,128)(2,1)S(1)} %get-tuple-element.46), channel_id=1, source_target_pairs={{0,12},{1,13},{2,14},{3,15},{4,8},{5,9},{6,10},{7,11},{8,4},{9,5},... | collective-permute-start | bytes 393224 | tf_op jit(solution)/shard_map/ppermute | solution.py:26
  90.5 1.7 collective-permute-start.8
  92.3 2.4 %contract_stem.3.refs_2_ = bf16[512,1024]{1,0:T(8,128)(2,1)S(1)} custom-call(bf16[2,2,32,512]{3,2,1,0:T(8,128)(2,1)S(1)} %get-tuple-element.50.refs_0_, bf16[2,2,32,512]{3,2,1,0:T(8,128)(2,1)S(1)} %collective-permute-done.27.refs_1_, bf16[2,2,32,512]{3,2,1,0:T(8,128)(2,1)S(1)} %collective-permute-done.28.refs_2_, ...), custom_call_target="tpu_custom_call" | custom-call | flops 2147483648 | bytes 6291456 | tf_op jit(solution)/shard_map/contract_stem/pallas_call | solution.py:200
  94.7 33.2 %collective-permute-done.6.refs_5_ = bf16[2,2,32,512]{3,2,1,0:T(8,128)(2,1)S(1)} collective-permute-done((bf16[2,2,32,512]{3,2,1,0:T(8,128)(2,1)S(1)}, bf16[2,2,32,512]{3,2,1,0:T(8,128)(2,1)S(1)}, u32[]{:S(2)}, u32[]{:S(2)}) %collective-permute-start.6) | collective-permute-done | bytes 131104 | tf_op jit(solution)/shard_map/ppermute | solution.py:26
  127.9 1.7 collective-permute-start.34
  129.6 2.3 %contract_stem.2.refs_2_ = bf16[512,1024]{1,0:T(8,128)(2,1)S(1)} custom-call(bf16[2,2,32,512]{3,2,1,0:T(8,128)(2,1)S(1)} %get-tuple-element.40.refs_0_, bf16[2,2,32,512]{3,2,1,0:T(8,128)(2,1)S(1)} %collective-permute-done.2.refs_1_, bf16[2,2,32,512]{3,2,1,0:T(8,128)(2,1)S(1)} %collective-permute-done.3.refs_2_, ...), custom_call_target="tpu_custom_call" | custom-call | flops 2147483648 | bytes 6291456 | tf_op jit(solution)/shard_map/contract_stem/pallas_call | solution.py:200
  132.0 1.3 collective-permute-start.41
  133.4 1.5 collective-permute-start.46
  134.8 2.2 %collective-permute-start = (bf16[1040,256]{1,0:T(8,128)(2,1)S(1)}, bf16[1040,256]{1,0:T(8,128)(2,1)S(1)}, u32[]{:S(2)}, u32[]{:S(2)}) collective-permute-start(bf16[1040,256]{1,0:T(8,128)(2,1)S(1)} %pad_maximum_fusion.refs_0_), channel_id=1, source_target_pairs={{0,2},{1,3},{2,0},{3,1},{4,6},{5,7},{6,4},{7,5},{8,10},{9,11},{10,... | collective-permute-start | bytes 1597448 | tf_op jit(solution)/shard_map/ppermute | solution.py:26
  137.0 14.0 %collective-permute-done.41 = bf16[1040,256]{1,0:T(8,128)(2,1)S(1)} collective-permute-done((bf16[1040,256]{1,0:T(8,128)(2,1)S(1)}, bf16[1040,256]{1,0:T(8,128)(2,1)S(1)}, u32[]{:S(2)}, u32[]{:S(2)}) %collective-permute-start.41) | collective-permute-done | bytes 532512 | tf_op jit(solution)/shard_map/ppermute | solution.py:26
  151.0 1.6 collective-permute-start.37
  152.7 9.6 %collective-permute-done.46 = bf16[1040,256]{1,0:T(8,128)(2,1)S(1)} collective-permute-done((bf16[1040,256]{1,0:T(8,128)(2,1)S(1)}, bf16[1040,256]{1,0:T(8,128)(2,1)S(1)}, u32[]{:S(2)}, u32[]{:S(2)}) %collective-permute-start.46) | collective-permute-done | bytes 532512 | tf_op jit(solution)/shard_map/ppermute | solution.py:26
  162.4 1.6 collective-permute-start.43
  164.2 2.5 %contract_samples.8 = (bf16[2,2,32,256]{3,2,1,0:T(8,128)(2,1)S(1)}, bf16[2,2,32,256]{3,2,1,0:T(8,128)(2,1)S(1)}) custom-call(bf16[1040,256]{1,0:T(8,128)(2,1)S(1)} %pad_maximum_fusion.refs_0_, bf16[1040,256]{1,0:T(8,128)(2,1)S(1)} %collective-permute-done.refs_1_, bf16[512,1024]{1,0:T(8,128)(2,1)S(1)} %contract_stem.3.refs_2_, ...), custom_call_target="tpu_custom_call" | custom-call | flops 2147483648 | bytes 3162112 | tf_op jit(solution)/shard_map/contract_samples/pallas_call | solution.py:250
  166.8 2.5 %contract_samples.9 = (bf16[2,2,32,256]{3,2,1,0:T(8,128)(2,1)S(1)}, bf16[2,2,32,256]{3,2,1,0:T(8,128)(2,1)S(1)}) custom-call(bf16[1040,256]{1,0:T(8,128)(2,1)S(1)} %pad_maximum_fusion.refs_0_, bf16[1040,256]{1,0:T(8,128)(2,1)S(1)} %collective-permute-done.refs_1_, bf16[512,1024]{1,0:T(8,128)(2,1)S(1)} %contract_stem.2.refs_2_, ...), custom_call_target="tpu_custom_call" | custom-call | flops 2147483648 | bytes 3162112 | tf_op jit(solution)/shard_map/contract_samples/pallas_call | solution.py:250
  169.3 1.5 collective-permute-start.35
  170.8 2.4 %contract_samples.10 = (bf16[2,2,32,256]{3,2,1,0:T(8,128)(2,1)S(1)}, bf16[2,2,32,256]{3,2,1,0:T(8,128)(2,1)S(1)}) custom-call(bf16[1040,256]{1,0:T(8,128)(2,1)S(1)} %collective-permute-done.36.refs_0_, bf16[1040,256]{1,0:T(8,128)(2,1)S(1)} %collective-permute-done.37.refs_1_, bf16[512,1024]{1,0:T(8,128)(2,1)S(1)} %contract_stem.3.refs_2_, ...), custom_call_target="tpu_custom_call" | custom-call | flops 2147483648 | bytes 3162112 | tf_op jit(solution)/shard_map/contract_samples/pallas_call | solution.py:250
  173.2 2.4 %contract_samples.11 = (bf16[2,2,32,256]{3,2,1,0:T(8,128)(2,1)S(1)}, bf16[2,2,32,256]{3,2,1,0:T(8,128)(2,1)S(1)}) custom-call(bf16[1040,256]{1,0:T(8,128)(2,1)S(1)} %collective-permute-done.36.refs_0_, bf16[1040,256]{1,0:T(8,128)(2,1)S(1)} %collective-permute-done.37.refs_1_, bf16[512,1024]{1,0:T(8,128)(2,1)S(1)} %contract_stem.2.refs_2_, ...), custom_call_target="tpu_custom_call" | custom-call | flops 2147483648 | bytes 3162112 | tf_op jit(solution)/shard_map/contract_samples/pallas_call | solution.py:250
  176.9 2.5 %contract_samples.12 = (bf16[2,2,32,256]{3,2,1,0:T(8,128)(2,1)S(1)}, bf16[2,2,32,256]{3,2,1,0:T(8,128)(2,1)S(1)}) custom-call(bf16[1040,256]{1,0:T(8,128)(2,1)S(1)} %add.23.refs_0_, bf16[1040,256]{1,0:T(8,128)(2,1)S(1)} %collective-permute-done.43.refs_1_, bf16[512,1024]{1,0:T(8,128)(2,1)S(1)} %contract_stem.3.refs_2_, ...), custom_call_target="tpu_custom_call" | custom-call | flops 2147483648 | bytes 3162112 | tf_op jit(solution)/shard_map/contract_samples/pallas_call | solution.py:250
  179.4 2.7 %contract_samples.13 = (bf16[2,2,32,256]{3,2,1,0:T(8,128)(2,1)S(1)}, bf16[2,2,32,256]{3,2,1,0:T(8,128)(2,1)S(1)}) custom-call(bf16[1040,256]{1,0:T(8,128)(2,1)S(1)} %add.23.refs_0_, bf16[1040,256]{1,0:T(8,128)(2,1)S(1)} %collective-permute-done.43.refs_1_, bf16[512,1024]{1,0:T(8,128)(2,1)S(1)} %contract_stem.2.refs_2_, ...), custom_call_target="tpu_custom_call" | custom-call | flops 2147483648 | bytes 3162112 | tf_op jit(solution)/shard_map/contract_samples/pallas_call | solution.py:250
  182.1 1.3 collective-permute-start.44
  183.4 5.1 %collective-permute-done.47.refs_1_ = bf16[1040,256]{1,0:T(8,128)(2,1)S(1)} collective-permute-done((bf16[1040,256]{1,0:T(8,128)(2,1)S(1)}, bf16[1040,256]{1,0:T(8,128)(2,1)S(1)}, u32[]{:S(2)}, u32[]{:S(2)}) %collective-permute-start.47) | collective-permute-done | bytes 532512 | tf_op jit(solution)/shard_map/ppermute | solution.py:26
  188.5 2.4 %collective-permute-start.45 = (bf16[2,2,32,256]{3,2,1,0:T(8,128)(2,1)S(1)}, bf16[2,2,32,256]{3,2,1,0:T(8,128)(2,1)S(1)}, u32[]{:S(2)}, u32[]{:S(2)}) collective-permute-start(bf16[2,2,32,256]{3,2,1,0:T(8,128)(2,1)S(1)} %get-tuple-element.69), channel_id=1, source_target_pairs={{0,10},{1,11},{2,8},{3,9},{4,14},{5,15},{6,12},{7,13},{8,2},{9,3},... | collective-permute-start | bytes 196616 | tf_op jit(solution)/shard_map/ppermute | solution.py:26
  190.9 2.5 %contract_samples.14 = (bf16[2,2,32,256]{3,2,1,0:T(8,128)(2,1)S(1)}, bf16[2,2,32,256]{3,2,1,0:T(8,128)(2,1)S(1)}) custom-call(bf16[1040,256]{1,0:T(8,128)(2,1)S(1)} %add.24.refs_0_, bf16[1040,256]{1,0:T(8,128)(2,1)S(1)} %collective-permute-done.47.refs_1_, bf16[512,1024]{1,0:T(8,128)(2,1)S(1)} %contract_stem.3.refs_2_, ...), custom_call_target="tpu_custom_call" | custom-call | flops 2147483648 | bytes 3162112 | tf_op jit(solution)/shard_map/contract_samples/pallas_call | solution.py:250
  193.4 2.5 %contract_samples.15 = (bf16[2,2,32,256]{3,2,1,0:T(8,128)(2,1)S(1)}, bf16[2,2,32,256]{3,2,1,0:T(8,128)(2,1)S(1)}) custom-call(bf16[1040,256]{1,0:T(8,128)(2,1)S(1)} %add.24.refs_0_, bf16[1040,256]{1,0:T(8,128)(2,1)S(1)} %collective-permute-done.47.refs_1_, bf16[512,1024]{1,0:T(8,128)(2,1)S(1)} %contract_stem.2.refs_2_, ...), custom_call_target="tpu_custom_call" | custom-call | flops 2147483648 | bytes 3162112 | tf_op jit(solution)/shard_map/contract_samples/pallas_call | solution.py:250
  195.8 2.0 collective-permute-start.48
  197.8 2.1 %collective-permute-start.49 = (bf16[2,2,32,256]{3,2,1,0:T(8,128)(2,1)S(1)}, bf16[2,2,32,256]{3,2,1,0:T(8,128)(2,1)S(1)}, u32[]{:S(2)}, u32[]{:S(2)}) collective-permute-start(bf16[2,2,32,256]{3,2,1,0:T(8,128)(2,1)S(1)} %get-tuple-element.73), channel_id=1, source_target_pairs={{0,14},{1,15},{2,12},{3,13},{4,10},{5,11},{6,8},{7,9},{8,6},{9,7},... | collective-permute-start | bytes 196616 | tf_op jit(solution)/shard_map/ppermute | solution.py:26
  200.8 3.6 %collective-permute-done.49.refs_7_ = bf16[2,2,32,256]{3,2,1,0:T(8,128)(2,1)S(1)} collective-permute-done((bf16[2,2,32,256]{3,2,1,0:T(8,128)(2,1)S(1)}, bf16[2,2,32,256]{3,2,1,0:T(8,128)(2,1)S(1)}, u32[]{:S(2)}, u32[]{:S(2)}) %collective-permute-start.49) | collective-permute-done | bytes 65568 | tf_op jit(solution)/shard_map/ppermute | solution.py:26
  (97 shorter events, 23.9 us)
Async XLA Ops:
  1.0 12.4 %collective-permute-start.10 = (bf16[2,2,64,512]{3,2,1,0:T(8,128)(2,1)S(1)}, bf16[2,2,64,512]{3,2,1,0:T(8,128)(2,1)S(1)}, u32[]{:S(2)}, u32[]{:S(2)}) collective-permute-start(bf16[2,2,64,512]{3,2,1,0:T(8,128)(2,1)S(1)} %broadcast_select_fusion.refs_0_), channel_id=1, source_target_pairs={{4,0},{5,1},{6,2},{7,3},{0,4},{1,5},{2,6},{3,7},{12,8},{13,9},{14,... | collective-permute-start | bytes 786440 | tf_op jit(solution)/shard_map/ppermute | solution.py:26
  9.0 42.2 %collective-permute-start.1 = (bf16[8,2,2,32,512]{4,3,2,1,0:T(8,128)(2,1)}, bf16[8,2,2,32,512]{4,3,2,1,0:T(8,128)(2,1)S(1)}, u32[]{:S(2)}, u32[]{:S(2)}) collective-permute-start(bf16[8,2,2,32,512]{4,3,2,1,0:T(8,128)(2,1)} %bitcast.14), channel_id=1, source_target_pairs={{0,1},{1,0},{2,3},{3,2},{4,5},{5,4},{6,7},{7,6},{8,9},{9,8},{10,11... | collective-permute-start | bytes 3145736 | tf_op jit(solution)/shard_map/ppermute | solution.py:35
  9.9 7.9 %collective-permute-start.9 = (bf16[2,2,64,512]{3,2,1,0:T(8,128)(2,1)S(1)}, bf16[2,2,64,512]{3,2,1,0:T(8,128)(2,1)S(1)}, u32[]{:S(2)}, u32[]{:S(2)}) collective-permute-start(bf16[2,2,64,512]{3,2,1,0:T(8,128)(2,1)S(1)} %broadcast_select_fusion.refs_0_), channel_id=1, source_target_pairs={{0,2},{1,3},{2,0},{3,1},{4,6},{5,7},{6,4},{7,5},{8,10},{9,11},{10,... | collective-permute-start | bytes 786440 | tf_op jit(solution)/shard_map/ppermute | solution.py:26
  11.2 6.9 %collective-permute-start.12 = (bf16[2,2,64,512]{3,2,1,0:T(8,128)(2,1)S(1)}, bf16[2,2,64,512]{3,2,1,0:T(8,128)(2,1)}, u32[]{:S(2)}, u32[]{:S(2)}) collective-permute-start(bf16[2,2,64,512]{3,2,1,0:T(8,128)(2,1)S(1)} %broadcast_select_fusion.refs_0_), channel_id=1, source_target_pairs={{8,4},{9,5},{10,6},{11,7},{4,8},{5,9},{6,10},{7,11},{24,20},{25,21... | collective-permute-start | bytes 786440 | tf_op jit(solution)/shard_map/ppermute | solution.py:26
  12.5 6.8 %collective-permute-start.18 = (bf16[2,2,64,512]{3,2,1,0:T(8,128)(2,1)S(1)}, bf16[2,2,64,512]{3,2,1,0:T(8,128)(2,1)S(1)}, u32[]{:S(2)}, u32[]{:S(2)}) collective-permute-start(bf16[2,2,64,512]{3,2,1,0:T(8,128)(2,1)S(1)} %broadcast_select_fusion.refs_0_), channel_id=1, source_target_pairs={{0,1},{1,0},{2,3},{3,2},{4,5},{5,4},{6,7},{7,6},{8,9},{9,8},{10,11... | collective-permute-start | bytes 786440 | tf_op jit(solution)/shard_map/ppermute | solution.py:35
  13.4 10.1 %collective-permute-start.11 = (bf16[2,2,64,512]{3,2,1,0:T(8,128)(2,1)S(1)}, bf16[2,2,64,512]{3,2,1,0:T(8,128)(2,1)}, u32[]{:S(2)}, u32[]{:S(2)}) collective-permute-start(bf16[2,2,64,512]{3,2,1,0:T(8,128)(2,1)S(1)} %collective-permute-done.10.refs_2_), channel_id=1, source_target_pairs={{0,2},{1,3},{2,0},{3,1},{4,6},{5,7},{6,4},{7,5},{8,10},{9,11},{10,... | collective-permute-start | bytes 786440 | tf_op jit(solution)/shard_map/ppermute | solution.py:26
  17.8 31.8 %collective-permute-start.36 = (bf16[1040,256]{1,0:T(8,128)(2,1)S(1)}, bf16[1040,256]{1,0:T(8,128)(2,1)S(1)}, u32[]{:S(2)}, u32[]{:S(2)}) collective-permute-start(bf16[1040,256]{1,0:T(8,128)(2,1)S(1)} %pad_maximum_fusion.refs_0_), channel_id=1, source_target_pairs={{4,0},{5,1},{6,2},{7,3},{0,4},{1,5},{2,6},{3,7},{12,8},{13,9},{14,... | collective-permute-start | bytes 1597448 | tf_op jit(solution)/shard_map/ppermute | solution.py:26
  18.0 17.7 %collective-permute-start.13 = (bf16[2,2,64,512]{3,2,1,0:T(8,128)(2,1)}, bf16[2,2,64,512]{3,2,1,0:T(8,128)(2,1)S(1)}, u32[]{:S(2)}, u32[]{:S(2)}) collective-permute-start(bf16[2,2,64,512]{3,2,1,0:T(8,128)(2,1)} %collective-permute-done.12), channel_id=1, source_target_pairs={{4,0},{5,1},{6,2},{7,3},{8,12},{9,13},{10,14},{11,15},{20,16},{21,... | collective-permute-start | bytes 786440 | tf_op jit(solution)/shard_map/ppermute | solution.py:26
  20.1 17.9 %collective-permute-start.14 = (bf16[2,2,64,512]{3,2,1,0:T(8,128)(2,1)S(1)}, bf16[2,2,64,512]{3,2,1,0:T(8,128)(2,1)S(1)}, u32[]{:S(2)}, u32[]{:S(2)}) collective-permute-start(bf16[2,2,64,512]{3,2,1,0:T(8,128)(2,1)S(1)} %collective-permute-done.10.refs_2_), channel_id=1, source_target_pairs={{8,4},{9,5},{10,6},{11,7},{4,8},{5,9},{6,10},{7,11},{24,20},{25,21... | collective-permute-start | bytes 786440 | tf_op jit(solution)/shard_map/ppermute | solution.py:26
  23.5 15.8 %collective-permute-start.19 = (bf16[2,2,64,512]{3,2,1,0:T(8,128)(2,1)S(1)}, bf16[2,2,64,512]{3,2,1,0:T(8,128)(2,1)S(1)}, u32[]{:S(2)}, u32[]{:S(2)}) collective-permute-start(bf16[2,2,64,512]{3,2,1,0:T(8,128)(2,1)S(1)} %collective-permute-done.9.refs_1_), channel_id=1, source_target_pairs={{0,1},{1,0},{2,3},{3,2},{4,5},{5,4},{6,7},{7,6},{8,9},{9,8},{10,11... | collective-permute-start | bytes 786440 | tf_op jit(solution)/shard_map/ppermute | solution.py:35
  37.9 9.8 %collective-permute-start.16 = (bf16[2,2,64,512]{3,2,1,0:T(8,128)(2,1)S(1)}, bf16[2,2,64,512]{3,2,1,0:T(8,128)(2,1)S(1)}, u32[]{:S(2)}, u32[]{:S(2)}) collective-permute-start(bf16[2,2,64,512]{3,2,1,0:T(8,128)(2,1)S(1)} %collective-permute-done.14), channel_id=1, source_target_pairs={{4,0},{5,1},{6,2},{7,3},{8,12},{9,13},{10,14},{11,15},{20,16},{21,... | collective-permute-start | bytes 786440 | tf_op jit(solution)/shard_map/ppermute | solution.py:26
  40.0 10.9 %collective-permute-start.15 = (bf16[2,2,64,512]{3,2,1,0:T(8,128)(2,1)S(1)}, bf16[2,2,64,512]{3,2,1,0:T(8,128)(2,1)}, u32[]{:S(2)}, u32[]{:S(2)}) collective-permute-start(bf16[2,2,64,512]{3,2,1,0:T(8,128)(2,1)S(1)} %add.21.refs_4_), channel_id=1, source_target_pairs={{0,2},{1,3},{2,0},{3,1},{4,6},{5,7},{6,4},{7,5},{8,10},{9,11},{10,... | collective-permute-start | bytes 786440 | tf_op jit(solution)/shard_map/ppermute | solution.py:26
  41.3 11.8 %collective-permute-start.21 = (bf16[2,2,64,512]{3,2,1,0:T(8,128)(2,1)}, bf16[2,2,64,512]{3,2,1,0:T(8,128)(2,1)}, u32[]{:S(2)}, u32[]{:S(2)}) collective-permute-start(bf16[2,2,64,512]{3,2,1,0:T(8,128)(2,1)} %collective-permute-done.11.refs_3_), channel_id=1, source_target_pairs={{0,1},{1,0},{2,3},{3,2},{4,5},{5,4},{6,7},{7,6},{8,9},{9,8},{10,11... | collective-permute-start | bytes 786440 | tf_op jit(solution)/shard_map/ppermute | solution.py:35
  47.8 5.6 %collective-permute-start.22 = (bf16[2,2,64,512]{3,2,1,0:T(8,128)(2,1)S(1)}, bf16[2,2,64,512]{3,2,1,0:T(8,128)(2,1)}, u32[]{:S(2)}, u32[]{:S(2)}) collective-permute-start(bf16[2,2,64,512]{3,2,1,0:T(8,128)(2,1)S(1)} %add.21.refs_4_), channel_id=1, source_target_pairs={{0,1},{1,0},{2,3},{3,2},{4,5},{5,4},{6,7},{7,6},{8,9},{9,8},{10,11... | collective-permute-start | bytes 786440 | tf_op jit(solution)/shard_map/ppermute | solution.py:35
  49.6 8.0 %collective-permute-start.17 = (bf16[2,2,64,512]{3,2,1,0:T(8,128)(2,1)S(1)}, bf16[2,2,64,512]{3,2,1,0:T(8,128)(2,1)}, u32[]{:S(2)}, u32[]{:S(2)}) collective-permute-start(bf16[2,2,64,512]{3,2,1,0:T(8,128)(2,1)S(1)} %add.22.refs_6_), channel_id=1, source_target_pairs={{0,2},{1,3},{2,0},{3,1},{4,6},{5,7},{6,4},{7,5},{8,10},{9,11},{10,... | collective-permute-start | bytes 786440 | tf_op jit(solution)/shard_map/ppermute | solution.py:26
  50.9 8.0 %collective-permute-start.23 = (bf16[2,2,64,512]{3,2,1,0:T(8,128)(2,1)}, bf16[2,2,64,512]{3,2,1,0:T(8,128)(2,1)}, u32[]{:S(2)}, u32[]{:S(2)}) collective-permute-start(bf16[2,2,64,512]{3,2,1,0:T(8,128)(2,1)} %collective-permute-done.15.refs_5_), channel_id=1, source_target_pairs={{0,1},{1,0},{2,3},{3,2},{4,5},{5,4},{6,7},{7,6},{8,9},{9,8},{10,11... | collective-permute-start | bytes 786440 | tf_op jit(solution)/shard_map/ppermute | solution.py:35
  51.2 8.0 %collective-permute-start.24 = (bf16[2,2,64,512]{3,2,1,0:T(8,128)(2,1)S(1)}, bf16[2,2,64,512]{3,2,1,0:T(8,128)(2,1)}, u32[]{:S(2)}, u32[]{:S(2)}) collective-permute-start(bf16[2,2,64,512]{3,2,1,0:T(8,128)(2,1)S(1)} %add.22.refs_6_), channel_id=1, source_target_pairs={{0,1},{1,0},{2,3},{3,2},{4,5},{5,4},{6,7},{7,6},{8,9},{9,8},{10,11... | collective-permute-start | bytes 786440 | tf_op jit(solution)/shard_map/ppermute | solution.py:35
  53.1 9.3 %collective-permute-start.2 = (bf16[2,2,32,512]{3,2,1,0:T(8,128)(2,1)S(1)}, bf16[2,2,32,512]{3,2,1,0:T(8,128)(2,1)S(1)}, u32[]{:S(2)}, u32[]{:S(2)}) collective-permute-start(bf16[2,2,32,512]{3,2,1,0:T(8,128)(2,1)S(1)} %get-tuple-element.41), channel_id=1, source_target_pairs={{0,2},{1,3},{2,0},{3,1},{4,6},{5,7},{6,4},{7,5},{8,10},{9,11},{10,... | collective-permute-start | bytes 393224 | tf_op jit(solution)/shard_map/ppermute | solution.py:26
  53.4 9.2 %collective-permute-start.3 = (bf16[2,2,32,512]{3,2,1,0:T(8,128)(2,1)S(1)}, bf16[2,2,32,512]{3,2,1,0:T(8,128)(2,1)S(1)}, u32[]{:S(2)}, u32[]{:S(2)}) collective-permute-start(bf16[2,2,32,512]{3,2,1,0:T(8,128)(2,1)S(1)} %get-tuple-element.42), channel_id=1, source_target_pairs={{0,4},{1,5},{2,6},{3,7},{4,0},{5,1},{6,2},{7,3},{8,12},{9,13},{10,... | collective-permute-start | bytes 393224 | tf_op jit(solution)/shard_map/ppermute | solution.py:26
  57.6 16.8 %collective-permute-start.25 = (bf16[2,2,64,512]{3,2,1,0:T(8,128)(2,1)}, bf16[2,2,64,512]{3,2,1,0:T(8,128)(2,1)S(1)}, u32[]{:S(2)}, u32[]{:S(2)}) collective-permute-start(bf16[2,2,64,512]{3,2,1,0:T(8,128)(2,1)} %collective-permute-done.17.refs_7_), channel_id=1, source_target_pairs={{0,1},{1,0},{2,3},{3,2},{4,5},{5,4},{6,7},{7,6},{8,9},{9,8},{10,11... | collective-permute-start | bytes 786440 | tf_op jit(solution)/shard_map/ppermute | solution.py:35
  58.9 8.6 %collective-permute-start.4 = (bf16[2,2,32,512]{3,2,1,0:T(8,128)(2,1)S(1)}, bf16[2,2,32,512]{3,2,1,0:T(8,128)(2,1)S(1)}, u32[]{:S(2)}, u32[]{:S(2)}) collective-permute-start(bf16[2,2,32,512]{3,2,1,0:T(8,128)(2,1)S(1)} %get-tuple-element.43), channel_id=1, source_target_pairs={{0,6},{1,7},{2,4},{3,5},{4,2},{5,3},{6,0},{7,1},{8,14},{9,15},{10,... | collective-permute-start | bytes 393224 | tf_op jit(solution)/shard_map/ppermute | solution.py:26
  59.1 9.7 %collective-permute-start.5 = (bf16[2,2,32,512]{3,2,1,0:T(8,128)(2,1)S(1)}, bf16[2,2,32,512]{3,2,1,0:T(8,128)(2,1)S(1)}, u32[]{:S(2)}, u32[]{:S(2)}) collective-permute-start(bf16[2,2,32,512]{3,2,1,0:T(8,128)(2,1)S(1)} %get-tuple-element.44), channel_id=1, source_target_pairs={{0,8},{1,9},{2,10},{3,11},{4,12},{5,13},{6,14},{7,15},{8,0},{9,1},... | collective-permute-start | bytes 393224 | tf_op jit(solution)/shard_map/ppermute | solution.py:26
  62.4 8.4 %collective-permute-start.27 = (bf16[2,2,32,512]{3,2,1,0:T(8,128)(2,1)S(1)}, bf16[2,2,32,512]{3,2,1,0:T(8,128)(2,1)S(1)}, u32[]{:S(2)}, u32[]{:S(2)}) collective-permute-start(bf16[2,2,32,512]{3,2,1,0:T(8,128)(2,1)S(1)} %get-tuple-element.51), channel_id=1, source_target_pairs={{0,2},{1,3},{2,0},{3,1},{4,6},{5,7},{6,4},{7,5},{8,10},{9,11},{10,... | collective-permute-start | bytes 393224 | tf_op jit(solution)/shard_map/ppermute | solution.py:26
  62.6 8.2 %collective-permute-start.28 = (bf16[2,2,32,512]{3,2,1,0:T(8,128)(2,1)S(1)}, bf16[2,2,32,512]{3,2,1,0:T(8,128)(2,1)S(1)}, u32[]{:S(2)}, u32[]{:S(2)}) collective-permute-start(bf16[2,2,32,512]{3,2,1,0:T(8,128)(2,1)S(1)} %get-tuple-element.52), channel_id=1, source_target_pairs={{0,4},{1,5},{2,6},{3,7},{4,0},{5,1},{6,2},{7,3},{8,12},{9,13},{10,... | collective-permute-start | bytes 393224 | tf_op jit(solution)/shard_map/ppermute | solution.py:26
  67.5 12.0 %collective-permute-start.29 = (bf16[2,2,32,512]{3,2,1,0:T(8,128)(2,1)S(1)}, bf16[2,2,32,512]{3,2,1,0:T(8,128)(2,1)S(1)}, u32[]{:S(2)}, u32[]{:S(2)}) collective-permute-start(bf16[2,2,32,512]{3,2,1,0:T(8,128)(2,1)S(1)} %get-tuple-element.53), channel_id=1, source_target_pairs={{0,6},{1,7},{2,4},{3,5},{4,2},{5,3},{6,0},{7,1},{8,14},{9,15},{10,... | collective-permute-start | bytes 393224 | tf_op jit(solution)/shard_map/ppermute | solution.py:26
  68.8 16.5 %collective-permute-start.30 = (bf16[2,2,32,512]{3,2,1,0:T(8,128)(2,1)S(1)}, bf16[2,2,32,512]{3,2,1,0:T(8,128)(2,1)S(1)}, u32[]{:S(2)}, u32[]{:S(2)}) collective-permute-start(bf16[2,2,32,512]{3,2,1,0:T(8,128)(2,1)S(1)} %get-tuple-element.54), channel_id=1, source_target_pairs={{0,8},{1,9},{2,10},{3,11},{4,12},{5,13},{6,14},{7,15},{8,0},{9,1},... | collective-permute-start | bytes 393224 | tf_op jit(solution)/shard_map/ppermute | solution.py:26
  70.8 17.5 %collective-permute-start.31 = (bf16[2,2,32,512]{3,2,1,0:T(8,128)(2,1)S(1)}, bf16[2,2,32,512]{3,2,1,0:T(8,128)(2,1)S(1)}, u32[]{:S(2)}, u32[]{:S(2)}) collective-permute-start(bf16[2,2,32,512]{3,2,1,0:T(8,128)(2,1)S(1)} %get-tuple-element.55), channel_id=1, source_target_pairs={{0,10},{1,11},{2,8},{3,9},{4,14},{5,15},{6,12},{7,13},{8,2},{9,3},... | collective-permute-start | bytes 393224 | tf_op jit(solution)/shard_map/ppermute | solution.py:26
  70.8 17.4 %collective-permute-start.32 = (bf16[2,2,32,512]{3,2,1,0:T(8,128)(2,1)S(1)}, bf16[2,2,32,512]{3,2,1,0:T(8,128)(2,1)S(1)}, u32[]{:S(2)}, u32[]{:S(2)}) collective-permute-start(bf16[2,2,32,512]{3,2,1,0:T(8,128)(2,1)S(1)} %get-tuple-element.56), channel_id=1, source_target_pairs={{0,12},{1,13},{2,14},{3,15},{4,8},{5,9},{6,10},{7,11},{8,4},{9,5},... | collective-permute-start | bytes 393224 | tf_op jit(solution)/shard_map/ppermute | solution.py:26
  74.4 16.2 %collective-permute-start.33 = (bf16[2,2,32,512]{3,2,1,0:T(8,128)(2,1)S(1)}, bf16[2,2,32,512]{3,2,1,0:T(8,128)(2,1)S(1)}, u32[]{:S(2)}, u32[]{:S(2)}) collective-permute-start(bf16[2,2,32,512]{3,2,1,0:T(8,128)(2,1)S(1)} %get-tuple-element.57), channel_id=1, source_target_pairs={{0,14},{1,15},{2,12},{3,13},{4,10},{5,11},{6,8},{7,9},{8,6},{9,7},... | collective-permute-start | bytes 393224 | tf_op jit(solution)/shard_map/ppermute | solution.py:26
  79.5 52.6 %collective-permute-start.40 = (bf16[1040,256]{1,0:T(8,128)(2,1)S(1)}, bf16[1040,256]{1,0:T(8,128)(2,1)S(1)}, u32[]{:S(2)}, u32[]{:S(2)}) collective-permute-start(bf16[1040,256]{1,0:T(8,128)(2,1)S(1)} %pad_maximum_fusion.refs_0_), channel_id=1, source_target_pairs={{8,4},{9,5},{10,6},{11,7},{4,8},{5,9},{6,10},{7,11},{24,20},{25,21... | collective-permute-start | bytes 1597448 | tf_op jit(solution)/shard_map/ppermute | solution.py:26
  85.3 48.0 %collective-permute-start.42 = (bf16[1040,256]{1,0:T(8,128)(2,1)S(1)}, bf16[1040,256]{1,0:T(8,128)(2,1)S(1)}, u32[]{:S(2)}, u32[]{:S(2)}) collective-permute-start(bf16[1040,256]{1,0:T(8,128)(2,1)S(1)} %collective-permute-done.36.refs_0_), channel_id=1, source_target_pairs={{8,4},{9,5},{10,6},{11,7},{4,8},{5,9},{6,10},{7,11},{24,20},{25,21... | collective-permute-start | bytes 1597448 | tf_op jit(solution)/shard_map/ppermute | solution.py:26
  88.2 39.7 %collective-permute-start.6 = (bf16[2,2,32,512]{3,2,1,0:T(8,128)(2,1)S(1)}, bf16[2,2,32,512]{3,2,1,0:T(8,128)(2,1)S(1)}, u32[]{:S(2)}, u32[]{:S(2)}) collective-permute-start(bf16[2,2,32,512]{3,2,1,0:T(8,128)(2,1)S(1)} %get-tuple-element.45), channel_id=1, source_target_pairs={{0,10},{1,11},{2,8},{3,9},{4,14},{5,15},{6,12},{7,13},{8,2},{9,3},... | collective-permute-start | bytes 393224 | tf_op jit(solution)/shard_map/ppermute | solution.py:26
  88.2 41.4 %collective-permute-start.7 = (bf16[2,2,32,512]{3,2,1,0:T(8,128)(2,1)S(1)}, bf16[2,2,32,512]{3,2,1,0:T(8,128)(2,1)S(1)}, u32[]{:S(2)}, u32[]{:S(2)}) collective-permute-start(bf16[2,2,32,512]{3,2,1,0:T(8,128)(2,1)S(1)} %get-tuple-element.46), channel_id=1, source_target_pairs={{0,12},{1,13},{2,14},{3,15},{4,8},{5,9},{6,10},{7,11},{8,4},{9,5},... | collective-permute-start | bytes 393224 | tf_op jit(solution)/shard_map/ppermute | solution.py:26
  90.5 39.1 %collective-permute-start.8 = (bf16[2,2,32,512]{3,2,1,0:T(8,128)(2,1)S(1)}, bf16[2,2,32,512]{3,2,1,0:T(8,128)(2,1)S(1)}, u32[]{:S(2)}, u32[]{:S(2)}) collective-permute-start(bf16[2,2,32,512]{3,2,1,0:T(8,128)(2,1)S(1)} %get-tuple-element.47), channel_id=1, source_target_pairs={{0,14},{1,15},{2,12},{3,13},{4,10},{5,11},{6,8},{7,9},{8,6},{9,7},... | collective-permute-start | bytes 393224 | tf_op jit(solution)/shard_map/ppermute | solution.py:26
  127.9 36.3 %collective-permute-start.34 = (bf16[512,1024]{1,0:T(8,128)(2,1)S(1)}, bf16[512,1024]{1,0:T(8,128)(2,1)S(1)}, u32[]{:S(2)}, u32[]{:S(2)}) collective-permute-start(bf16[512,1024]{1,0:T(8,128)(2,1)S(1)} %contract_stem.3.refs_2_), channel_id=1, source_target_pairs={{0,1},{1,0},{2,3},{3,2},{4,5},{5,4},{6,7},{7,6},{8,9},{9,8},{10,11... | collective-permute-start | bytes 3145736 | tf_op jit(solution)/shard_map/ppermute | solution.py:35
  132.0 34.8 %collective-permute-start.26 = (bf16[512,1024]{1,0:T(8,128)(2,1)S(1)}, bf16[512,1024]{1,0:T(8,128)(2,1)S(1)}, u32[]{:S(2)}, u32[]{:S(2)}) collective-permute-start(bf16[512,1024]{1,0:T(8,128)(2,1)S(1)} %contract_stem.2.refs_2_), channel_id=1, source_target_pairs={{0,1},{1,0},{2,3},{3,2},{4,5},{5,4},{6,7},{7,6},{8,9},{9,8},{10,11... | collective-permute-start | bytes 3145736 | tf_op jit(solution)/shard_map/ppermute | solution.py:35
  132.0 18.9 %collective-permute-start.41 = (bf16[1040,256]{1,0:T(8,128)(2,1)S(1)}, bf16[1040,256]{1,0:T(8,128)(2,1)S(1)}, u32[]{:S(2)}, u32[]{:S(2)}) collective-permute-start(bf16[1040,256]{1,0:T(8,128)(2,1)S(1)} %collective-permute-done.40), channel_id=1, source_target_pairs={{4,0},{5,1},{6,2},{7,3},{8,12},{9,13},{10,14},{11,15},{20,16},{21,... | collective-permute-start | bytes 1597448 | tf_op jit(solution)/shard_map/ppermute | solution.py:26
  133.4 29.0 %collective-permute-start.46 = (bf16[1040,256]{1,0:T(8,128)(2,1)S(1)}, bf16[1040,256]{1,0:T(8,128)(2,1)S(1)}, u32[]{:S(2)}, u32[]{:S(2)}) collective-permute-start(bf16[1040,256]{1,0:T(8,128)(2,1)S(1)} %collective-permute-done.42), channel_id=1, source_target_pairs={{4,0},{5,1},{6,2},{7,3},{8,12},{9,13},{10,14},{11,15},{20,16},{21,... | collective-permute-start | bytes 1597448 | tf_op jit(solution)/shard_map/ppermute | solution.py:26
  134.8 29.3 %collective-permute-start = (bf16[1040,256]{1,0:T(8,128)(2,1)S(1)}, bf16[1040,256]{1,0:T(8,128)(2,1)S(1)}, u32[]{:S(2)}, u32[]{:S(2)}) collective-permute-start(bf16[1040,256]{1,0:T(8,128)(2,1)S(1)} %pad_maximum_fusion.refs_0_), channel_id=1, source_target_pairs={{0,2},{1,3},{2,0},{3,1},{4,6},{5,7},{6,4},{7,5},{8,10},{9,11},{10,... | collective-permute-start | bytes 1597448 | tf_op jit(solution)/shard_map/ppermute | solution.py:26
  151.0 19.8 %collective-permute-start.37 = (bf16[1040,256]{1,0:T(8,128)(2,1)S(1)}, bf16[1040,256]{1,0:T(8,128)(2,1)S(1)}, u32[]{:S(2)}, u32[]{:S(2)}) collective-permute-start(bf16[1040,256]{1,0:T(8,128)(2,1)S(1)} %collective-permute-done.36.refs_0_), channel_id=1, source_target_pairs={{0,2},{1,3},{2,0},{3,1},{4,6},{5,7},{6,4},{7,5},{8,10},{9,11},{10,... | collective-permute-start | bytes 1597448 | tf_op jit(solution)/shard_map/ppermute | solution.py:26
  162.4 14.6 %collective-permute-start.43 = (bf16[1040,256]{1,0:T(8,128)(2,1)S(1)}, bf16[1040,256]{1,0:T(8,128)(2,1)S(1)}, u32[]{:S(2)}, u32[]{:S(2)}) collective-permute-start(bf16[1040,256]{1,0:T(8,128)(2,1)S(1)} %add.23.refs_0_), channel_id=1, source_target_pairs={{0,2},{1,3},{2,0},{3,1},{4,6},{5,7},{6,4},{7,5},{8,10},{9,11},{10,... | collective-permute-start | bytes 1597448 | tf_op jit(solution)/shard_map/ppermute | solution.py:26
  164.2 24.3 %collective-permute-start.47 = (bf16[1040,256]{1,0:T(8,128)(2,1)S(1)}, bf16[1040,256]{1,0:T(8,128)(2,1)S(1)}, u32[]{:S(2)}, u32[]{:S(2)}) collective-permute-start(bf16[1040,256]{1,0:T(8,128)(2,1)S(1)} %add.24.refs_0_), channel_id=1, source_target_pairs={{0,2},{1,3},{2,0},{3,1},{4,6},{5,7},{6,4},{7,5},{8,10},{9,11},{10,... | collective-permute-start | bytes 1597448 | tf_op jit(solution)/shard_map/ppermute | solution.py:26
  169.3 26.6 %collective-permute-start.35 = (bf16[2,2,32,256]{3,2,1,0:T(8,128)(2,1)S(1)}, bf16[2,2,32,256]{3,2,1,0:T(8,128)(2,1)S(1)}, u32[]{:S(2)}, u32[]{:S(2)}) collective-permute-start(bf16[2,2,32,256]{3,2,1,0:T(8,128)(2,1)S(1)} %get-tuple-element.61), channel_id=1, source_target_pairs={{0,2},{1,3},{2,0},{3,1},{4,6},{5,7},{6,4},{7,5},{8,10},{9,11},{10,... | collective-permute-start | bytes 196616 | tf_op jit(solution)/shard_map/ppermute | solution.py:26
  175.7 22.2 %collective-permute-start.38 = (bf16[2,2,32,256]{3,2,1,0:T(8,128)(2,1)S(1)}, bf16[2,2,32,256]{3,2,1,0:T(8,128)(2,1)S(1)}, u32[]{:S(2)}, u32[]{:S(2)}) collective-permute-start(bf16[2,2,32,256]{3,2,1,0:T(8,128)(2,1)S(1)} %get-tuple-element.64), channel_id=1, source_target_pairs={{0,4},{1,5},{2,6},{3,7},{4,0},{5,1},{6,2},{7,3},{8,12},{9,13},{10,... | collective-permute-start | bytes 196616 | tf_op jit(solution)/shard_map/ppermute | solution.py:26
  175.7 24.2 %collective-permute-start.39 = (bf16[2,2,32,256]{3,2,1,0:T(8,128)(2,1)S(1)}, bf16[2,2,32,256]{3,2,1,0:T(8,128)(2,1)S(1)}, u32[]{:S(2)}, u32[]{:S(2)}) collective-permute-start(bf16[2,2,32,256]{3,2,1,0:T(8,128)(2,1)S(1)} %get-tuple-element.65), channel_id=1, source_target_pairs={{0,6},{1,7},{2,4},{3,5},{4,2},{5,3},{6,0},{7,1},{8,14},{9,15},{10,... | collective-permute-start | bytes 196616 | tf_op jit(solution)/shard_map/ppermute | solution.py:26
  182.1 17.8 %collective-permute-start.44 = (bf16[2,2,32,256]{3,2,1,0:T(8,128)(2,1)S(1)}, bf16[2,2,32,256]{3,2,1,0:T(8,128)(2,1)S(1)}, u32[]{:S(2)}, u32[]{:S(2)}) collective-permute-start(bf16[2,2,32,256]{3,2,1,0:T(8,128)(2,1)S(1)} %get-tuple-element.68), channel_id=1, source_target_pairs={{0,8},{1,9},{2,10},{3,11},{4,12},{5,13},{6,14},{7,15},{8,0},{9,1},... | collective-permute-start | bytes 196616 | tf_op jit(solution)/shard_map/ppermute | solution.py:26
  188.5 11.5 %collective-permute-start.45 = (bf16[2,2,32,256]{3,2,1,0:T(8,128)(2,1)S(1)}, bf16[2,2,32,256]{3,2,1,0:T(8,128)(2,1)S(1)}, u32[]{:S(2)}, u32[]{:S(2)}) collective-permute-start(bf16[2,2,32,256]{3,2,1,0:T(8,128)(2,1)S(1)} %get-tuple-element.69), channel_id=1, source_target_pairs={{0,10},{1,11},{2,8},{3,9},{4,14},{5,15},{6,12},{7,13},{8,2},{9,3},... | collective-permute-start | bytes 196616 | tf_op jit(solution)/shard_map/ppermute | solution.py:26
  197.8 6.5 %collective-permute-start.49 = (bf16[2,2,32,256]{3,2,1,0:T(8,128)(2,1)S(1)}, bf16[2,2,32,256]{3,2,1,0:T(8,128)(2,1)S(1)}, u32[]{:S(2)}, u32[]{:S(2)}) collective-permute-start(bf16[2,2,32,256]{3,2,1,0:T(8,128)(2,1)S(1)} %get-tuple-element.73), channel_id=1, source_target_pairs={{0,14},{1,15},{2,12},{3,13},{4,10},{5,11},{6,8},{7,9},{8,6},{9,7},... | collective-permute-start | bytes 196616 | tf_op jit(solution)/shard_map/ppermute | solution.py:26
  (11 other events, 127.8 us)

commit v2 on v1

--- a/solution.py
+++ b/solution.py
@@ -33,6 +33,13 @@
 def swap_mb(value, offset):
     count = lax.axis_size("ma") * lax.axis_size("mb")
     return lax.ppermute(value, AXES, [(m, m ^ offset) for m in range(count)])
+
+
+def swap_cuts(value):
+    shape = [lax.axis_size(name) for name in ("cuts",) + AXES]
+    count, inner = shape[0], shape[1] * shape[2]
+    pairs = [(c * inner + m, (c ^ 1) * inner + m) for c in range(count) for m in range(inner)]
+    return lax.ppermute(value, ("cuts",) + AXES, pairs)
 
 
 def relay_groups(length):
@@ -60,36 +67,93 @@
         slots.setdefault(key[0], []).append(sent[key])
     gathered = {}
     for x in sorted(slots):
-        whole = functools.reduce(jnp.add, slots[x])
+        whole = slots[x][0] if len(slots[x]) == 1 else merge(slots[x])
         gathered[2 * x] = whole
         gathered[2 * x + 1] = swap_ma(whole, 1)
     return [gathered[d] for d in range(2 * length)]
 
 
+def merge_kernel(*refs):
+    total = refs[0][...]
+    for ref in refs[1:-1]:
+        total = total + ref[...]
+    refs[-1][...] = total
+
+
+def merge(values):
+    return pl.pallas_call(
+        merge_kernel,
+        in_specs=[VMEM] * len(values),
+        out_specs=VMEM,
+        out_shape=jax.ShapeDtypeStruct(values[0].shape, BF16),
+        compiler_params=params(),
+        name="merge",
+    )(*values)
+
+
 def scalars(*values):
     return jnp.stack([jnp.asarray(v, jnp.int32) for v in values])
 
 
-def pack_kernel(count, place_ref, *refs):
-    sources, outs = refs[: -count * refs[0].shape[2]], refs[-count * refs[0].shape[2] :]
-    for number, out_ref in enumerate(outs):
-        l, d = number // count, number % count
+def pack_kernel(offsets, blocks, place_ref, *refs):
+    sources, outs = refs[: -len(offsets)], refs[-len(offsets) :]
+    for d, out_ref in zip(offsets, outs):
         for s, source in enumerate(sources):
-            out_ref[s] = source[place_ref[0] ^ d, :, l]
-
-
-def pack(here_ma, sources):
-    count, parts, local, inner, width = sources[0].shape
-    shape = jax.ShapeDtypeStruct((len(sources), parts, inner, width), BF16)
-    outs = pl.pallas_call(
-        functools.partial(pack_kernel, count),
+            seat = (place_ref[1],) if s == 0 else ()
+            for number, l in enumerate(blocks):
+                out_ref[number, s] = source[(l, place_ref[0] ^ d) + seat]
+
+
+def pack(here, sources, offsets, blocks):
+    shape = (len(blocks), len(sources)) + sources[0].shape[3:]
+    return pl.pallas_call(
+        functools.partial(pack_kernel, offsets, blocks),
         in_specs=[SMEM] + [VMEM] * len(sources),
-        out_specs=[VMEM] * (count * local),
-        out_shape=[shape] * (count * local),
+        out_specs=[VMEM] * len(offsets),
+        out_shape=[jax.ShapeDtypeStruct(shape, BF16)] * len(offsets),
         compiler_params=params(),
         name="pack",
-    )(scalars(here_ma), *sources)
-    return [outs[l * count : (l + 1) * count] for l in range(local)]
+    )(here, *sources)
+
+
+def stack_kernel(*refs):
+    for d, ref in enumerate(refs[:-1]):
+        refs[-1][d] = ref[...]
+
+
+def stack(values):
+    return pl.pallas_call(
+        stack_kernel,
+        in_specs=[VMEM] * len(values),
+        out_specs=VMEM,
+        out_shape=jax.ShapeDtypeStruct((len(values),) + values[0].shape, BF16),
+        compiler_params=params(),
+        name="stack",
+    )(*values)
+
+
+def collect_kernel(place_ref, *refs):
+    out_ref = refs[-1]
+    stacks = len(refs) // 2
+    count, _, depth, _ = refs[0].shape
+    for number, ref in enumerate(refs[:-1]):
+        turn = place_ref[1] if number < stacks else 1 - place_ref[1]
+        for d in range(count):
+            slot = (number % stacks) * count + d
+            start = pl.multiple_of((place_ref[0] ^ slot) * depth, depth)
+            out_ref[turn, :, pl.ds(start, depth), :] = ref[d]
+
+
+def collect(here, own, far):
+    count, parts, depth, width = own[0].shape
+    return pl.pallas_call(
+        collect_kernel,
+        in_specs=[SMEM] + [VMEM] * (2 * len(own)),
+        out_specs=VMEM,
+        out_shape=jax.ShapeDtypeStruct((2, parts, depth * count * len(own), width), BF16),
+        compiler_params=params(),
+        name="collect",
+    )(here, *own, *far)
 
 
 def table_kernel(inner, count_mb, relative, slots, place_ref, relabel_ref, *refs):
@@ -112,31 +176,29 @@
         gather(other, mine)
 
     size = first_ref.shape[2]
-    column = lax.broadcasted_iota(jnp.int32, (size, size), 0)
-    seat, rest = column // inner, column % inner
-    ma, mb = seat // count_mb, seat % count_mb
-    near = (((ma ^ place_ref[0]) * count_mb) + (mb ^ place_ref[1])) * inner + rest
-    for r in range(2):
-        position = near if relative[r] else column
-        selector = jnp.where(relabel_ref[r : r + 1, :] == position, 1.0, 0.0).astype(BF16)
-        for p in range(2):
-            ordered = jnp.dot(selector, first_ref[r, p], preferred_element_type=F32)
-            if r == 0:
-                turned = ordered.T.astype(BF16)
-                if p == 0:
-                    stem_ref[:size, :size] = turned
-                    stem_ref[size:, size:] = turned
-                else:
-                    stem_ref[size:, :size] = turned
-                    stem_ref[:size, size:] = -turned
-            else:
-                ordered = ordered.astype(BF16)
-                if p == 0:
-                    final_ref[:size, :size] = ordered
-                    final_ref[size:, size:] = ordered
-                else:
-                    final_ref[:size, size:] = ordered
-                    final_ref[size:, :size] = -ordered
+
+    def select(near, relabel, repeat):
+        column = lax.broadcasted_iota(jnp.int32, (repeat * size, size), 0) // repeat
+        seat, rest = column // inner, column % inner
+        ma, mb = seat // count_mb, seat % count_mb
+        if near:
+            ma, mb = ma ^ place_ref[0], mb ^ place_ref[1]
+        position = (ma * count_mb + mb) * inner + rest
+        return jnp.where(relabel == position, 1.0, 0.0).astype(BF16)
+
+    selector = select(relative[0], relabel_ref[0:1, :], 2)
+    real = jnp.dot(selector, first_ref[0, 0], preferred_element_type=F32)
+    imag = jnp.dot(selector, first_ref[0, 1], preferred_element_type=F32)
+    even = lax.broadcasted_iota(jnp.int32, real.shape, 0) % 2 == 0
+    stem_ref[:size, :] = jnp.where(even, real, -imag).T.astype(BF16)
+    stem_ref[size:, :] = jnp.where(even, imag, real).T.astype(BF16)
+    selector = select(relative[1], relabel_ref[1:2, :], 1)
+    real = jnp.dot(selector, first_ref[1, 0], preferred_element_type=F32).astype(BF16)
+    imag = jnp.dot(selector, first_ref[1, 1], preferred_element_type=F32).astype(BF16)
+    final_ref[:size, :size] = real
+    final_ref[size:, size:] = real
+    final_ref[:size, size:] = imag
+    final_ref[size:, :size] = -imag
     width = second_ref.shape[2]
     right_ref[:width, :width] = second_ref[1, 0]
     right_ref[:width, width:] = second_ref[1, 1]
@@ -168,14 +230,13 @@
     )(here, relabel, *mine, *other)
 
 
-def stem_kernel(*refs):
+def stem_kernel(blocks, *refs):
     arrived, (table_ref, product_ref, out_ref, rows_ref, mid_ref) = refs[:-5], refs[-5:]
-    seats, parts, inner, _ = arrived[0].shape
+    _, seats, depth, _ = arrived[0].shape
     for d, piece in enumerate(arrived):
         for s in range(seats):
-            for p in range(parts):
-                start = ((p * len(arrived) + d) * seats + s) * inner
-                rows_ref[start : start + inner, :] = piece[s, p]
+            start = (d * seats + s) * depth
+            rows_ref[start : start + depth, :] = piece[blocks[d], s]
     half = mid_ref.shape[0] // 2
     step = min(256, half)
     for top in range(0, 2 * half, step):
@@ -195,10 +256,11 @@
 
 
 def contract_stem(arrived, table, product):
+    arrived, blocks = zip(*arrived)
     width = arrived[0].shape[3]
     size = table.shape[0]
     return pl.pallas_call(
-        stem_kernel,
+        functools.partial(stem_kernel, blocks),
         in_specs=[VMEM] * (len(arrived) + 2),
         out_specs=VMEM,
         out_shape=jax.ShapeDtypeStruct((size // 2, 2 * width), BF16),
@@ -271,18 +333,21 @@
             for p in range(parts):
                 start = ((p * len(found) + d) * seats + s) * inner
                 rows_ref[start : start + inner, :] = piece[s, p]
-    out_ref[...] = lax.dot_general(
+    result = lax.dot_general(
         rows_ref[...], table_ref[...], (((0,), (0,)), ((), ())), preferred_element_type=F32
     ).astype(BF16)
+    width = out_ref.shape[2]
+    for p in range(parts):
+        out_ref[:, p, :] = result[:, p * width : (p + 1) * width]
 
 
 def contract_final(found, table):
-    samples = found[0].shape[3]
+    parts, _, samples = found[0].shape[1:]
     return pl.pallas_call(
         final_kernel,
         in_specs=[VMEM] * (len(found) + 1),
         out_specs=VMEM,
-        out_shape=jax.ShapeDtypeStruct((samples, table.shape[1]), BF16),
+        out_shape=jax.ShapeDtypeStruct((samples, parts, table.shape[1] // parts), BF16),
         scratch_shapes=[pltpu.VMEM((table.shape[0], samples), BF16)],
         cost_estimate=pl.CostEstimate(
             flops=2 * table.size * samples, bytes_accessed=2 * table.size, transcendentals=0
@@ -292,8 +357,8 @@
     )(*found, table)
 
 
-def is_short(count_ma):
-    return count_ma // 2 <= 4
+def is_short(count_cuts, count_ma, rounds):
+    return count_ma // 2 <= 4 and count_cuts == rounds == 2
 
 
 def on_device(
@@ -305,37 +370,49 @@
     local, row_count, parts, width = stem_field.shape
     inner = row_count // groups
     samples = sample_state.shape[0]
-    short = is_short(count_ma)
+    short = is_short(lax.axis_size("cuts"), count_ma, first_branch_tensors.shape[0])
+    here_cuts = lax.axis_index("cuts")
 
     flat = sample_state.reshape(samples, parts * width).T
     named = jnp.broadcast_to(sample_block[:, 0].astype(BF16)[None, :], (16, samples))
     states = jnp.concatenate([flat, named], axis=0)
 
-    pieces = stem_field.reshape(local, count_ma, count_mb, inner, parts, width)
-    pieces = jnp.transpose(pieces, (2, 1, 4, 0, 3, 5))
+    pieces = stem_field.reshape(local, count_ma, count_mb, inner * parts, width)
 
     if short:
         share = jnp.where(here_mb == 0, first_branch_tensors, second_branch_tensors)
-        mine = relay_gather(share)
-        other = [swap_mb(value, 1) for value in mine]
-        held = [
-            lax.dynamic_index_in_dim(pieces, here_mb ^ s, keepdims=False) for s in range(count_mb)
-        ]
-        sources = [held[0]] + [swap_mb(held[s], s) for s in range(1, count_mb)]
-        arrived = [
-            [swap_ma(piece, d) if d else piece for d, piece in enumerate(packed)]
-            for packed in pack(here_ma, sources)
-        ]
+        share = lax.dynamic_index_in_dim(share, here_cuts, keepdims=False)
+        own = [swap_ma(share, d) if d else share for d in range(count_ma)]
+        half = count_ma // 2
+        own = [stack(own[:half]), stack(own[half:])]
+        far = [swap_cuts(value) for value in own]
+        mine = collect(scalars(here_ma, here_cuts), own, far)
+        other = swap_mb(mine, 1)
+        mine, other = [mine], [other]
+        sources = [pieces]
+        for s in range(1, count_mb):
+            held = lax.dynamic_index_in_dim(pieces, here_mb ^ s, 2, keepdims=False)
+            sources.append(swap_mb(held, s))
+        place = scalars(here_ma, here_mb)
+        near, distant = tuple(range(half)), tuple(range(half, count_ma))
+        arrived = [[] for _ in range(local)]
+        for d, piece in zip(near, pack(place, sources, near, tuple(range(local)))):
+            piece = swap_ma(piece, d) if d else piece
+            for l in range(local):
+                arrived[l].append((piece, l))
+        for l in range(local):
+            for d, piece in zip(distant, pack(place, sources, distant, (l,))):
+                arrived[l].append((swap_ma(piece, d), 0))
         every_state = relay_gather(states)
-        here = scalars(here_ma, here_mb, here_ma, here_mb)
+        here = scalars(here_ma, here_mb, 0, here_mb)
     else:
         mine = [lax.all_gather(first_branch_tensors, "ma", axis=2, tiled=True)]
         other = [lax.all_gather(second_branch_tensors, "ma", axis=2, tiled=True)]
-        sent = jnp.transpose(pieces, (1, 0, 2, 3, 4, 5))
+        sent = jnp.transpose(pieces, (1, 2, 0, 3, 4))
         sent = sent.reshape((groups,) + sent.shape[2:])
         arrived = lax.all_to_all(sent, AXES, split_axis=0, concat_axis=0, tiled=True)
         arrived = arrived.reshape((count_ma, count_mb) + arrived.shape[1:])
-        arrived = [[arrived[d, :, :, l] for d in range(count_ma)] for l in range(local)]
+        arrived = [[(arrived[d, :, l][None], 0) for d in range(count_ma)] for l in range(local)]
         every_state = lax.all_gather(states, "ma", axis=0)
         every_state = [every_state[d] for d in range(count_ma)]
         here = scalars(0, here_mb, 0, 0)
@@ -356,7 +433,7 @@
     else:
         found = lax.all_to_all(jnp.stack(found), "ma", split_axis=0, concat_axis=0, tiled=True)
         found = [found[d] for d in range(count_ma)]
-    return contract_final(found, final_table).reshape(samples, parts, -1)
+    return contract_final(found, final_table)
 
 
 def solution(mesh):
@@ -368,10 +445,13 @@
         P(("cuts", "ma", "mb"), None),
         P(("cuts", "ma", "mb"), None, None),
     )
-    return jax.shard_map(
+    step = jax.shard_map(
         on_device,
         mesh=mesh,
         in_specs=placed,
         out_specs=P(("cuts", "ma", "mb"), None, None),
         check_vma=False,
     )
+    if not is_short(mesh.shape["cuts"], mesh.shape["ma"], 2):
+        return step
+    return step

time: 209 us -> 210 us (level)
  Pallas kernels: 29.6 us -> 36.1 us
  local copies, waits for them, and re-layouts: 10.5 us -> 5.86 us
    ppermute x39 -> x34, waiting for transfers between devices: 108 us -> 96.8 us  [permute(): return lax.ppermute(value, AXES, full)]
    ppermute x0 -> x2, waiting for transfers between devices: none -> 9.58 us  [swap_cuts(): return lax.ppermute(value, ('cuts',) + AXES, pairs)]
    another operation x1 -> x0, local copies, waits for them, and re-layouts: 4.58 us -> none
    pallas_call x3 -> x10, Pallas kernels: 4.86 us -> 8.65 us  [the longest x2 4.68 us: contract_stem(): pl.pallas_call(functools.partial(stem_kernel, blocks), in_specs=[VMEM] *...]
    ppermute x0 -> x2, starting transfers between devices: none -> 3.19 us  [swap_cuts(): return lax.ppermute(value, ('cuts',) + AXES, pairs)]
    unnamed x21 -> x5, local copies, waits for them, and re-layouts: 4.71 us -> 1.99 us
    ppermute x11 -> x4, starting transfers between devices: 8.93 us -> 6.38 us  [swap_mb(): return lax.ppermute(value, AXES, [(m, m ^ offset) for m in range(count)])]
    ppermute x39 -> x34, starting transfers between devices: 46.5 us -> 46.4 us  [permute(): return lax.ppermute(value, AXES, full)]
  transfers between devices with their start and end apart: 50 -> 40, of which waited for: 15 -> 12; matrix products, arithmetic and copies ran while one was open for 5% -> 3% of each run, Pallas kernels for 14% -> 16%
where the time goes in v2:
time: 210 us; the launch traced here: 207 us
  waiting for transfers between devices  106 us (50%)
  starting transfers between devices  55.9 us (27%)
  Pallas kernels  36.1 us (17%)
  local copies, waits for them, and re-layouts  5.86 us (3%)
  other arithmetic  2.31 us (1%)
    ppermute x34, waiting for transfers between devices, permute(): return lax.ppermute(value, AXES, full)  96.8 us
    ppermute x34, starting transfers between devices, permute(): return lax.ppermute(value, AXES, full)  46.4 us
    pallas_call x8, Pallas kernels, contract_samples(): pl.pallas_call(functools.partial(sample_kernel, groups, first, scale, man...  20 us
    ppermute x2, waiting for transfers between devices, swap_cuts(): return lax.ppermute(value, ('cuts',) + AXES, pairs)  9.58 us
    ppermute x4, starting transfers between devices, swap_mb(): return lax.ppermute(value, AXES, [(m, m ^ offset) for m in range(count)])  6.38 us
    pallas_call x1, Pallas kernels, tables(): pl.pallas_call(functools.partial(table_kernel, inner, count_mb, relative,...  5.83 us
    pallas_call x2, Pallas kernels, contract_stem(): pl.pallas_call(functools.partial(stem_kernel, blocks), in_specs=[VMEM] *...  4.68 us
  transfers between devices with their start and end apart: 40, of which 12 were waited for; matrix products, arithmetic and copies ran while one was open for 3% of the time, Pallas kernels for 16%

profile of v2, /device:TPU:1, one launch (start us, length us, event | category | flops | bytes accessed | tf_op | source)
XLA Modules:
  0.0 206.9 jit_solution(295525036637111509)
XLA Ops:
  1.0 2.1 %collective-permute-start.9 = (bf16[2,64,512]{2,1,0:T(8,128)(2,1)S(1)}, bf16[2,64,512]{2,1,0:T(8,128)(2,1)S(1)}, u32[]{:S(2)}, u32[]{:S(2)}) collective-permute-start(bf16[2,64,512]{2,1,0:T(8,128)(2,1)S(1)} %fusion.refs_0_), channel_id=1, source_target_pairs={{0,2},{1,3},{2,0},{3,1},{4,6},{5,7},{6,4},{7,5},{8,10},{9,11},{10,... | collective-permute-start | bytes 393224 | tf_op jit(solution)/shard_map/ppermute | solution.py:26
  3.1 1.3 collective-permute-start.10
  4.4 2.4 %collective-permute-start.12 = (bf16[2,64,512]{2,1,0:T(8,128)(2,1)S(1)}, bf16[2,64,512]{2,1,0:T(8,128)(2,1)S(1)}, u32[]{:S(2)}, u32[]{:S(2)}) collective-permute-start(bf16[2,64,512]{2,1,0:T(8,128)(2,1)S(1)} %fusion.refs_0_), channel_id=1, source_target_pairs={{0,8},{1,9},{2,10},{3,11},{4,12},{5,13},{6,14},{7,15},{8,0},{9,1},... | collective-permute-start | bytes 393224 | tf_op jit(solution)/shard_map/ppermute | solution.py:26
  7.8 3.3 %collective-permute-start.14 = (bf16[2,64,512]{2,1,0:T(8,128)(2,1)S(1)}, bf16[2,64,512]{2,1,0:T(8,128)(2,1)S(1)}, u32[]{:S(2)}, u32[]{:S(2)}) collective-permute-start(bf16[2,64,512]{2,1,0:T(8,128)(2,1)S(1)} %fusion.refs_0_), channel_id=1, source_target_pairs={{0,12},{1,13},{2,14},{3,15},{4,8},{5,9},{6,10},{7,11},{8,4},{9,5},... | collective-permute-start | bytes 393224 | tf_op jit(solution)/shard_map/ppermute | solution.py:26
  11.2 2.6 %collective-permute-done.11.refs_3_ = bf16[2,64,512]{2,1,0:T(8,128)(2,1)S(1)} collective-permute-done((bf16[2,64,512]{2,1,0:T(8,128)(2,1)S(1)}, bf16[2,64,512]{2,1,0:T(8,128)(2,1)S(1)}, u32[]{:S(2)}, u32[]{:S(2)}) %collective-permute-start.11) | collective-permute-done | bytes 131104 | tf_op jit(solution)/shard_map/ppermute | solution.py:26
  13.9 1.9 collective-permute-start.16
  15.8 9.6 %collective-permute-done.13.refs_1_ = bf16[2,64,512]{2,1,0:T(8,128)(2,1)S(1)} collective-permute-done((bf16[2,64,512]{2,1,0:T(8,128)(2,1)S(1)}, bf16[2,64,512]{2,1,0:T(8,128)(2,1)S(1)}, u32[]{:S(2)}, u32[]{:S(2)}) %collective-permute-start.13) | collective-permute-done | bytes 131104 | tf_op jit(solution)/shard_map/ppermute | solution.py:26
  25.5 1.3 collective-permute-start.17
  26.8 9.6 %collective-permute-done.17.refs_3_ = bf16[4,2,64,512]{3,2,1,0:T(8,128)(2,1)S(1)} collective-permute-done((bf16[4,2,64,512]{3,2,1,0:T(8,128)(2,1)S(1)}, bf16[4,2,64,512]{3,2,1,0:T(8,128)(2,1)S(1)}, u32[]{:S(2)}, u32[]{:S(2)}) %collective-permute-start.17) | collective-permute-done | bytes 524320 | tf_op jit(solution)/shard_map/ppermute | solution.py:42
  36.4 2.0 collect.1.refs_0_
  38.4 3.5 %collective-permute-start.18 = (bf16[2,2,512,512]{3,2,1,0:T(8,128)(2,1)}, bf16[2,2,512,512]{3,2,1,0:T(8,128)(2,1)}, u32[]{:S(2)}, u32[]{:S(2)}) collective-permute-start(bf16[2,2,512,512]{3,2,1,0:T(8,128)(2,1)} %collect.1.refs_0_), channel_id=1, source_target_pairs={{0,1},{1,0},{2,3},{3,2},{4,5},{5,4},{6,7},{7,6},{8,9},{9,8},{10,11... | collective-permute-start | bytes 6291464 | tf_op jit(solution)/shard_map/ppermute | solution.py:35
  41.9 2.7 %reshape.13.refs_0_ = bf16[2,8,2,64,512]{4,3,2,1,0:T(8,128)(2,1)S(1)} reshape(bf16[2,512,2,512]{3,2,1,0:T(2,128)(2,1)} %param.6) | data formatting | bytes 4194304 | tf_op jit(solution)/shard_map/reshape | solution.py:380
  44.7 1.1 dynamic-slice_bitcast_fusion
  45.8 2.0 copy.7
  48.9 5.9 %collective-permute-start.26 = (bf16[1040,256]{1,0:T(8,128)(2,1)S(1)}, bf16[1040,256]{1,0:T(8,128)(2,1)S(1)}, u32[]{:S(2)}, u32[]{:S(2)}) collective-permute-start(bf16[1040,256]{1,0:T(8,128)(2,1)S(1)} %pad_maximum_fusion.refs_0_), channel_id=1, source_target_pairs={{4,0},{5,1},{6,2},{7,3},{0,4},{1,5},{2,6},{3,7},{12,8},{13,9},{14,... | collective-permute-start | bytes 1597448 | tf_op jit(solution)/shard_map/ppermute | solution.py:26
  55.5 1.4 collective-permute-start.5
  57.5 1.1 collective-permute-start.20
  59.8 15.4 %collective-permute-done.26.refs_0_ = bf16[1040,256]{1,0:T(8,128)(2,1)S(1)} collective-permute-done((bf16[1040,256]{1,0:T(8,128)(2,1)S(1)}, bf16[1040,256]{1,0:T(8,128)(2,1)S(1)}, u32[]{:S(2)}, u32[]{:S(2)}) %collective-permute-start.26) | collective-permute-done | bytes 532512 | tf_op jit(solution)/shard_map/ppermute | solution.py:26
  75.3 2.6 %collective-permute-start.4 = (bf16[2,2,64,512]{3,2,1,0:T(8,128)(2,1)S(1)}, bf16[2,2,64,512]{3,2,1,0:T(8,128)(2,1)S(1)}, u32[]{:S(2)}, u32[]{:S(2)}) collective-permute-start(bf16[2,2,64,512]{3,2,1,0:T(8,128)(2,1)S(1)} %get-tuple-element.39), channel_id=1, source_target_pairs={{0,6},{1,7},{2,4},{3,5},{4,2},{5,3},{6,0},{7,1},{8,14},{9,15},{10,... | collective-permute-start | bytes 786440 | tf_op jit(solution)/shard_map/ppermute | solution.py:26
  78.0 2.5 %collective-permute-start.22 = (bf16[1,2,64,512]{3,2,1,0:T(8,128)(2,1)S(1)}, bf16[1,2,64,512]{3,2,1,0:T(8,128)(2,1)S(1)}, u32[]{:S(2)}, u32[]{:S(2)}) collective-permute-start(bf16[1,2,64,512]{3,2,1,0:T(8,128)(2,1)S(1)} %get-tuple-element.48), channel_id=1, source_target_pairs={{0,12},{1,13},{2,14},{3,15},{4,8},{5,9},{6,10},{7,11},{8,4},{9,5},... | collective-permute-start | bytes 393224 | tf_op jit(solution)/shard_map/ppermute | solution.py:26
  81.0 5.8 %tables.1 = (bf16[1024,1024]{1,0:T(8,128)(2,1)S(1)}, bf16[1024,1024]{1,0:T(8,128)(2,1)S(1)}, bf16[1024,1024]{1,0:T(8,128)(2,1)S(1)}) custom-call(s32[4]{0:T(128)S(1)} %pad_add_fusion.1.place_ref, s32[2,512]{1,0:T(2,128)S(1)} %copy-done, bf16[2,2,512,512]{3,2,1,0:T(8,128)(2,1)} %collect.1.refs_0_, bf16[2,2,512,512]{3,2,1,0:T(8,128)(2,1)} %collective-permute-done.18.refs_1_), custom_call_target="tpu_custom_call" | custom-call | flops 2147483648 | bytes 10485760 | tf_op jit(solution)/shard_map/tables/pallas_call | solution.py:219
  86.8 6.4 %collective-permute-done.22.refs_6_ = bf16[1,2,64,512]{3,2,1,0:T(8,128)(2,1)S(1)} collective-permute-done((bf16[1,2,64,512]{3,2,1,0:T(8,128)(2,1)S(1)}, bf16[1,2,64,512]{3,2,1,0:T(8,128)(2,1)S(1)}, u32[]{:S(2)}, u32[]{:S(2)}) %collective-permute-start.22) | collective-permute-done | bytes 131104 | tf_op jit(solution)/shard_map/ppermute | solution.py:26
  93.9 2.0 collective-permute-done.23.refs_7_
  96.7 1.5 collective-permute-start.7
  98.2 2.9 %collective-permute-start.8 = (bf16[1,2,64,512]{3,2,1,0:T(8,128)(2,1)S(1)}, bf16[1,2,64,512]{3,2,1,0:T(8,128)(2,1)S(1)}, u32[]{:S(2)}, u32[]{:S(2)}) collective-permute-start(bf16[1,2,64,512]{3,2,1,0:T(8,128)(2,1)S(1)} %get-tuple-element.43), channel_id=1, source_target_pairs={{0,14},{1,15},{2,12},{3,13},{4,10},{5,11},{6,8},{7,9},{8,6},{9,7},... | collective-permute-start | bytes 393224 | tf_op jit(solution)/shard_map/ppermute | solution.py:26
  101.1 2.3 %contract_stem.3.refs_2_ = bf16[512,1024]{1,0:T(8,128)(2,1)S(1)} custom-call(bf16[2,2,64,512]{3,2,1,0:T(8,128)(2,1)S(1)} %get-tuple-element.36.refs_0_, bf16[2,2,64,512]{3,2,1,0:T(8,128)(2,1)S(1)} %collective-permute-done.2.refs_1_, bf16[2,2,64,512]{3,2,1,0:T(8,128)(2,1)S(1)} %collective-permute-done.3.refs_2_, ...), custom_call_target="tpu_custom_call" | custom-call | flops 2147483648 | bytes 6291456 | tf_op jit(solution)/shard_map/contract_stem/pallas_call | solution.py:262
  103.4 25.7 %collective-permute-done.6.refs_5_ = bf16[1,2,64,512]{3,2,1,0:T(8,128)(2,1)S(1)} collective-permute-done((bf16[1,2,64,512]{3,2,1,0:T(8,128)(2,1)S(1)}, bf16[1,2,64,512]{3,2,1,0:T(8,128)(2,1)S(1)}, u32[]{:S(2)}, u32[]{:S(2)}) %collective-permute-start.6) | collective-permute-done | bytes 131104 | tf_op jit(solution)/shard_map/ppermute | solution.py:26
  129.1 2.8 %collective-permute-start.24 = (bf16[512,1024]{1,0:T(8,128)(2,1)S(1)}, bf16[512,1024]{1,0:T(8,128)(2,1)S(1)}, u32[]{:S(2)}, u32[]{:S(2)}) collective-permute-start(bf16[512,1024]{1,0:T(8,128)(2,1)S(1)} %contract_stem.3.refs_2_), channel_id=1, source_target_pairs={{0,1},{1,0},{2,3},{3,2},{4,5},{5,4},{6,7},{7,6},{8,9},{9,8},{10,11... | collective-permute-start | bytes 3145736 | tf_op jit(solution)/shard_map/ppermute | solution.py:35
  132.0 2.3 %contract_stem.2.refs_2_ = bf16[512,1024]{1,0:T(8,128)(2,1)S(1)} custom-call(bf16[2,2,64,512]{3,2,1,0:T(8,128)(2,1)S(1)} %get-tuple-element.36.refs_0_, bf16[2,2,64,512]{3,2,1,0:T(8,128)(2,1)S(1)} %collective-permute-done.2.refs_1_, bf16[2,2,64,512]{3,2,1,0:T(8,128)(2,1)S(1)} %collective-permute-done.3.refs_2_, ...), custom_call_target="tpu_custom_call" | custom-call | flops 2147483648 | bytes 6291456 | tf_op jit(solution)/shard_map/contract_stem/pallas_call | solution.py:262
  134.4 1.3 collective-permute-start.31
  135.7 1.5 collective-permute-start.36
  138.1 14.6 %collective-permute-done.31.refs_0_ = bf16[1040,256]{1,0:T(8,128)(2,1)S(1)} collective-permute-done((bf16[1040,256]{1,0:T(8,128)(2,1)S(1)}, bf16[1040,256]{1,0:T(8,128)(2,1)S(1)}, u32[]{:S(2)}, u32[]{:S(2)}) %collective-permute-start.31) | collective-permute-done | bytes 532512 | tf_op jit(solution)/shard_map/ppermute | solution.py:26
  153.6 10.6 %collective-permute-done.36.refs_1_ = bf16[1040,256]{1,0:T(8,128)(2,1)S(1)} collective-permute-done((bf16[1040,256]{1,0:T(8,128)(2,1)S(1)}, bf16[1040,256]{1,0:T(8,128)(2,1)S(1)}, u32[]{:S(2)}, u32[]{:S(2)}) %collective-permute-start.36) | collective-permute-done | bytes 532512 | tf_op jit(solution)/shard_map/ppermute | solution.py:26
  165.8 2.5 %contract_samples.8 = (bf16[2,2,32,256]{3,2,1,0:T(8,128)(2,1)S(1)}, bf16[2,2,32,256]{3,2,1,0:T(8,128)(2,1)S(1)}) custom-call(bf16[1040,256]{1,0:T(8,128)(2,1)S(1)} %pad_maximum_fusion.refs_0_, bf16[1040,256]{1,0:T(8,128)(2,1)S(1)} %collective-permute-done.refs_1_, bf16[512,1024]{1,0:T(8,128)(2,1)S(1)} %contract_stem.3.refs_2_, ...), custom_call_target="tpu_custom_call" | custom-call | flops 2147483648 | bytes 3162112 | tf_op jit(solution)/shard_map/contract_samples/pallas_call | solution.py:312
  168.3 2.5 %contract_samples.9 = (bf16[2,2,32,256]{3,2,1,0:T(8,128)(2,1)S(1)}, bf16[2,2,32,256]{3,2,1,0:T(8,128)(2,1)S(1)}) custom-call(bf16[1040,256]{1,0:T(8,128)(2,1)S(1)} %pad_maximum_fusion.refs_0_, bf16[1040,256]{1,0:T(8,128)(2,1)S(1)} %collective-permute-done.refs_1_, bf16[512,1024]{1,0:T(8,128)(2,1)S(1)} %contract_stem.2.refs_2_, ...), custom_call_target="tpu_custom_call" | custom-call | flops 2147483648 | bytes 3162112 | tf_op jit(solution)/shard_map/contract_samples/pallas_call | solution.py:312
  171.6 2.5 %contract_samples.10 = (bf16[2,2,32,256]{3,2,1,0:T(8,128)(2,1)S(1)}, bf16[2,2,32,256]{3,2,1,0:T(8,128)(2,1)S(1)}) custom-call(bf16[1040,256]{1,0:T(8,128)(2,1)S(1)} %collective-permute-done.26.refs_0_, bf16[1040,256]{1,0:T(8,128)(2,1)S(1)} %collective-permute-done.27.refs_1_, bf16[512,1024]{1,0:T(8,128)(2,1)S(1)} %contract_stem.3.refs_2_, ...), custom_call_target="tpu_custom_call" | custom-call | flops 2147483648 | bytes 3162112 | tf_op jit(solution)/shard_map/contract_samples/pallas_call | solution.py:312
  174.1 2.5 %contract_samples.11 = (bf16[2,2,32,256]{3,2,1,0:T(8,128)(2,1)S(1)}, bf16[2,2,32,256]{3,2,1,0:T(8,128)(2,1)S(1)}) custom-call(bf16[1040,256]{1,0:T(8,128)(2,1)S(1)} %collective-permute-done.26.refs_0_, bf16[1040,256]{1,0:T(8,128)(2,1)S(1)} %collective-permute-done.27.refs_1_, bf16[512,1024]{1,0:T(8,128)(2,1)S(1)} %contract_stem.2.refs_2_, ...), custom_call_target="tpu_custom_call" | custom-call | flops 2147483648 | bytes 3162112 | tf_op jit(solution)/shard_map/contract_samples/pallas_call | solution.py:312
  176.6 1.8 collective-permute-start.29
  178.5 2.5 %contract_samples.12 = (bf16[2,2,32,256]{3,2,1,0:T(8,128)(2,1)S(1)}, bf16[2,2,32,256]{3,2,1,0:T(8,128)(2,1)S(1)}) custom-call(bf16[1040,256]{1,0:T(8,128)(2,1)S(1)} %merge.2.refs_0_, bf16[1040,256]{1,0:T(8,128)(2,1)S(1)} %collective-permute-done.33.refs_1_, bf16[512,1024]{1,0:T(8,128)(2,1)S(1)} %contract_stem.3.refs_2_, ...), custom_call_target="tpu_custom_call" | custom-call | flops 2147483648 | bytes 3162112 | tf_op jit(solution)/shard_map/contract_samples/pallas_call | solution.py:312
  180.9 2.7 %contract_samples.13 = (bf16[2,2,32,256]{3,2,1,0:T(8,128)(2,1)S(1)}, bf16[2,2,32,256]{3,2,1,0:T(8,128)(2,1)S(1)}) custom-call(bf16[1040,256]{1,0:T(8,128)(2,1)S(1)} %merge.2.refs_0_, bf16[1040,256]{1,0:T(8,128)(2,1)S(1)} %collective-permute-done.33.refs_1_, bf16[512,1024]{1,0:T(8,128)(2,1)S(1)} %contract_stem.2.refs_2_, ...), custom_call_target="tpu_custom_call" | custom-call | flops 2147483648 | bytes 3162112 | tf_op jit(solution)/shard_map/contract_samples/pallas_call | solution.py:312
  184.5 5.6 %collective-permute-done.37.refs_1_ = bf16[1040,256]{1,0:T(8,128)(2,1)S(1)} collective-permute-done((bf16[1040,256]{1,0:T(8,128)(2,1)S(1)}, bf16[1040,256]{1,0:T(8,128)(2,1)S(1)}, u32[]{:S(2)}, u32[]{:S(2)}) %collective-permute-start.37) | collective-permute-done | bytes 532512 | tf_op jit(solution)/shard_map/ppermute | solution.py:26
  190.0 1.9 collective-permute-start.35
  191.9 2.5 %contract_samples.14 = (bf16[2,2,32,256]{3,2,1,0:T(8,128)(2,1)S(1)}, bf16[2,2,32,256]{3,2,1,0:T(8,128)(2,1)S(1)}) custom-call(bf16[1040,256]{1,0:T(8,128)(2,1)S(1)} %merge.3.refs_0_, bf16[1040,256]{1,0:T(8,128)(2,1)S(1)} %collective-permute-done.37.refs_1_, bf16[512,1024]{1,0:T(8,128)(2,1)S(1)} %contract_stem.3.refs_2_, ...), custom_call_target="tpu_custom_call" | custom-call | flops 2147483648 | bytes 3162112 | tf_op jit(solution)/shard_map/contract_samples/pallas_call | solution.py:312
  194.4 2.5 %contract_samples.15 = (bf16[2,2,32,256]{3,2,1,0:T(8,128)(2,1)S(1)}, bf16[2,2,32,256]{3,2,1,0:T(8,128)(2,1)S(1)}) custom-call(bf16[1040,256]{1,0:T(8,128)(2,1)S(1)} %merge.3.refs_0_, bf16[1040,256]{1,0:T(8,128)(2,1)S(1)} %collective-permute-done.37.refs_1_, bf16[512,1024]{1,0:T(8,128)(2,1)S(1)} %contract_stem.2.refs_2_, ...), custom_call_target="tpu_custom_call" | custom-call | flops 2147483648 | bytes 3162112 | tf_op jit(solution)/shard_map/contract_samples/pallas_call | solution.py:312
  196.9 2.0 collective-permute-start.38
  198.8 2.2 %collective-permute-start.39 = (bf16[2,2,32,256]{3,2,1,0:T(8,128)(2,1)S(1)}, bf16[2,2,32,256]{3,2,1,0:T(8,128)(2,1)S(1)}, u32[]{:S(2)}, u32[]{:S(2)}) collective-permute-start(bf16[2,2,32,256]{3,2,1,0:T(8,128)(2,1)S(1)} %get-tuple-element.65), channel_id=1, source_target_pairs={{0,14},{1,15},{2,12},{3,13},{4,10},{5,11},{6,8},{7,9},{8,6},{9,7},... | collective-permute-start | bytes 196616 | tf_op jit(solution)/shard_map/ppermute | solution.py:26
  202.0 3.3 %collective-permute-done.39.refs_7_ = bf16[2,2,32,256]{3,2,1,0:T(8,128)(2,1)S(1)} collective-permute-done((bf16[2,2,32,256]{3,2,1,0:T(8,128)(2,1)S(1)}, bf16[2,2,32,256]{3,2,1,0:T(8,128)(2,1)S(1)}, u32[]{:S(2)}, u32[]{:S(2)}) %collective-permute-start.39) | collective-permute-done | bytes 65568 | tf_op jit(solution)/shard_map/ppermute | solution.py:26
  205.2 1.7 contract_final.1
  (66 shorter events, 13.8 us)
Async XLA Ops:
  1.0 6.9 %collective-permute-start.9 = (bf16[2,64,512]{2,1,0:T(8,128)(2,1)S(1)}, bf16[2,64,512]{2,1,0:T(8,128)(2,1)S(1)}, u32[]{:S(2)}, u32[]{:S(2)}) collective-permute-start(bf16[2,64,512]{2,1,0:T(8,128)(2,1)S(1)} %fusion.refs_0_), channel_id=1, source_target_pairs={{0,2},{1,3},{2,0},{3,1},{4,6},{5,7},{6,4},{7,5},{8,10},{9,11},{10,... | collective-permute-start | bytes 393224 | tf_op jit(solution)/shard_map/ppermute | solution.py:26
  3.1 8.1 %collective-permute-start.10 = (bf16[2,64,512]{2,1,0:T(8,128)(2,1)S(1)}, bf16[2,64,512]{2,1,0:T(8,128)(2,1)S(1)}, u32[]{:S(2)}, u32[]{:S(2)}) collective-permute-start(bf16[2,64,512]{2,1,0:T(8,128)(2,1)S(1)} %fusion.refs_0_), channel_id=1, source_target_pairs={{0,4},{1,5},{2,6},{3,7},{4,0},{5,1},{6,2},{7,3},{8,12},{9,13},{10,... | collective-permute-start | bytes 393224 | tf_op jit(solution)/shard_map/ppermute | solution.py:26
  4.4 9.4 %collective-permute-start.11 = (bf16[2,64,512]{2,1,0:T(8,128)(2,1)S(1)}, bf16[2,64,512]{2,1,0:T(8,128)(2,1)S(1)}, u32[]{:S(2)}, u32[]{:S(2)}) collective-permute-start(bf16[2,64,512]{2,1,0:T(8,128)(2,1)S(1)} %fusion.refs_0_), channel_id=1, source_target_pairs={{0,6},{1,7},{2,4},{3,5},{4,2},{5,3},{6,0},{7,1},{8,14},{9,15},{10,... | collective-permute-start | bytes 393224 | tf_op jit(solution)/shard_map/ppermute | solution.py:26
  4.4 11.4 %collective-permute-start.12 = (bf16[2,64,512]{2,1,0:T(8,128)(2,1)S(1)}, bf16[2,64,512]{2,1,0:T(8,128)(2,1)S(1)}, u32[]{:S(2)}, u32[]{:S(2)}) collective-permute-start(bf16[2,64,512]{2,1,0:T(8,128)(2,1)S(1)} %fusion.refs_0_), channel_id=1, source_target_pairs={{0,8},{1,9},{2,10},{3,11},{4,12},{5,13},{6,14},{7,15},{8,0},{9,1},... | collective-permute-start | bytes 393224 | tf_op jit(solution)/shard_map/ppermute | solution.py:26
  6.8 18.6 %collective-permute-start.13 = (bf16[2,64,512]{2,1,0:T(8,128)(2,1)S(1)}, bf16[2,64,512]{2,1,0:T(8,128)(2,1)S(1)}, u32[]{:S(2)}, u32[]{:S(2)}) collective-permute-start(bf16[2,64,512]{2,1,0:T(8,128)(2,1)S(1)} %fusion.refs_0_), channel_id=1, source_target_pairs={{0,10},{1,11},{2,8},{3,9},{4,14},{5,15},{6,12},{7,13},{8,2},{9,3},... | collective-permute-start | bytes 393224 | tf_op jit(solution)/shard_map/ppermute | solution.py:26
  7.8 17.6 %collective-permute-start.14 = (bf16[2,64,512]{2,1,0:T(8,128)(2,1)S(1)}, bf16[2,64,512]{2,1,0:T(8,128)(2,1)S(1)}, u32[]{:S(2)}, u32[]{:S(2)}) collective-permute-start(bf16[2,64,512]{2,1,0:T(8,128)(2,1)S(1)} %fusion.refs_0_), channel_id=1, source_target_pairs={{0,12},{1,13},{2,14},{3,15},{4,8},{5,9},{6,10},{7,11},{8,4},{9,5},... | collective-permute-start | bytes 393224 | tf_op jit(solution)/shard_map/ppermute | solution.py:26
  11.2 14.3 %collective-permute-start.15 = (bf16[2,64,512]{2,1,0:T(8,128)(2,1)S(1)}, bf16[2,64,512]{2,1,0:T(8,128)(2,1)S(1)}, u32[]{:S(2)}, u32[]{:S(2)}) collective-permute-start(bf16[2,64,512]{2,1,0:T(8,128)(2,1)S(1)} %fusion.refs_0_), channel_id=1, source_target_pairs={{0,14},{1,15},{2,12},{3,13},{4,10},{5,11},{6,8},{7,9},{8,6},{9,7},... | collective-permute-start | bytes 393224 | tf_op jit(solution)/shard_map/ppermute | solution.py:26
  13.9 13.0 %collective-permute-start.16 = (bf16[4,2,64,512]{3,2,1,0:T(8,128)(2,1)S(1)}, bf16[4,2,64,512]{3,2,1,0:T(8,128)(2,1)S(1)}, u32[]{:S(2)}, u32[]{:S(2)}) collective-permute-start(bf16[4,2,64,512]{3,2,1,0:T(8,128)(2,1)S(1)} %stack.30.refs_0_), channel_id=1, source_target_pairs={{0,16},{1,17},{2,18},{3,19},{4,20},{5,21},{6,22},{7,23},{8,24},{9,... | collective-permute-start | bytes 1572872 | tf_op jit(solution)/shard_map/ppermute | solution.py:42
  25.5 10.9 %collective-permute-start.17 = (bf16[4,2,64,512]{3,2,1,0:T(8,128)(2,1)S(1)}, bf16[4,2,64,512]{3,2,1,0:T(8,128)(2,1)S(1)}, u32[]{:S(2)}, u32[]{:S(2)}) collective-permute-start(bf16[4,2,64,512]{3,2,1,0:T(8,128)(2,1)S(1)} %stack.31.refs_1_), channel_id=1, source_target_pairs={{0,16},{1,17},{2,18},{3,19},{4,20},{5,21},{6,22},{7,23},{8,24},{9,... | collective-permute-start | bytes 1572872 | tf_op jit(solution)/shard_map/ppermute | solution.py:42
  38.4 42.1 %collective-permute-start.18 = (bf16[2,2,512,512]{3,2,1,0:T(8,128)(2,1)}, bf16[2,2,512,512]{3,2,1,0:T(8,128)(2,1)}, u32[]{:S(2)}, u32[]{:S(2)}) collective-permute-start(bf16[2,2,512,512]{3,2,1,0:T(8,128)(2,1)} %collect.1.refs_0_), channel_id=1, source_target_pairs={{0,1},{1,0},{2,3},{3,2},{4,5},{5,4},{6,7},{7,6},{8,9},{9,8},{10,11... | collective-permute-start | bytes 6291464 | tf_op jit(solution)/shard_map/ppermute | solution.py:35
  44.7 3.1 %copy-start.1 = (s32[256,1]{0,1:T(1,128)S(1)}, s32[256,1]{0,1:T(1,128)}, u32[]{:S(2)}) copy-start(s32[256,1]{0,1:T(1,128)} %param.10) | copy-start | bytes 3076
  45.8 9.1 %collective-permute-start.1 = (bf16[2,8,64,512]{3,2,1,0:T(8,128)(2,1)}, bf16[2,8,64,512]{3,2,1,0:T(8,128)(2,1)S(1)}, u32[]{:S(2)}, u32[]{:S(2)}) collective-permute-start(bf16[2,8,64,512]{3,2,1,0:T(8,128)(2,1)} %dynamic-slice_bitcast_fusion), channel_id=1, source_target_pairs={{0,1},{1,0},{2,3},{3,2},{4,5},{5,4},{6,7},{7,6},{8,9},{9,8},{10,11... | collective-permute-start | bytes 3145736 | tf_op jit(solution)/shard_map/ppermute | solution.py:35
  48.9 26.3 %collective-permute-start.26 = (bf16[1040,256]{1,0:T(8,128)(2,1)S(1)}, bf16[1040,256]{1,0:T(8,128)(2,1)S(1)}, u32[]{:S(2)}, u32[]{:S(2)}) collective-permute-start(bf16[1040,256]{1,0:T(8,128)(2,1)S(1)} %pad_maximum_fusion.refs_0_), channel_id=1, source_target_pairs={{4,0},{5,1},{6,2},{7,3},{0,4},{1,5},{2,6},{3,7},{12,8},{13,9},{14,... | collective-permute-start | bytes 1597448 | tf_op jit(solution)/shard_map/ppermute | solution.py:26
  55.5 19.7 %collective-permute-start.5 = (bf16[1,2,64,512]{3,2,1,0:T(8,128)(2,1)S(1)}, bf16[1,2,64,512]{3,2,1,0:T(8,128)(2,1)S(1)}, u32[]{:S(2)}, u32[]{:S(2)}) collective-permute-start(bf16[1,2,64,512]{3,2,1,0:T(8,128)(2,1)S(1)} %get-tuple-element.40), channel_id=1, source_target_pairs={{0,8},{1,9},{2,10},{3,11},{4,12},{5,13},{6,14},{7,15},{8,0},{9,1},... | collective-permute-start | bytes 393224 | tf_op jit(solution)/shard_map/ppermute | solution.py:26
  57.5 23.5 %copy-start = (s32[2,512]{1,0:T(2,128)S(1)}, s32[2,512]{1,0:T(2,128)}, u32[]{:S(2)}) copy-start(s32[2,512]{1,0:T(2,128)} %relabel_ref.1) | copy-start | bytes 12292
  57.5 17.7 %collective-permute-start.20 = (bf16[1,2,64,512]{3,2,1,0:T(8,128)(2,1)S(1)}, bf16[1,2,64,512]{3,2,1,0:T(8,128)(2,1)S(1)}, u32[]{:S(2)}, u32[]{:S(2)}) collective-permute-start(bf16[1,2,64,512]{3,2,1,0:T(8,128)(2,1)S(1)} %get-tuple-element.46), channel_id=1, source_target_pairs={{0,8},{1,9},{2,10},{3,11},{4,12},{5,13},{6,14},{7,15},{8,0},{9,1},... | collective-permute-start | bytes 393224 | tf_op jit(solution)/shard_map/ppermute | solution.py:26
  58.6 19.4 %collective-permute-start.21 = (bf16[1,2,64,512]{3,2,1,0:T(8,128)(2,1)S(1)}, bf16[1,2,64,512]{3,2,1,0:T(8,128)(2,1)S(1)}, u32[]{:S(2)}, u32[]{:S(2)}) collective-permute-start(bf16[1,2,64,512]{3,2,1,0:T(8,128)(2,1)S(1)} %get-tuple-element.47), channel_id=1, source_target_pairs={{0,10},{1,11},{2,8},{3,9},{4,14},{5,15},{6,12},{7,13},{8,2},{9,3},... | collective-permute-start | bytes 393224 | tf_op jit(solution)/shard_map/ppermute | solution.py:26
  75.2 21.4 %collective-permute-start.2 = (bf16[2,2,64,512]{3,2,1,0:T(8,128)(2,1)S(1)}, bf16[2,2,64,512]{3,2,1,0:T(8,128)(2,1)S(1)}, u32[]{:S(2)}, u32[]{:S(2)}) collective-permute-start(bf16[2,2,64,512]{3,2,1,0:T(8,128)(2,1)S(1)} %get-tuple-element.37), channel_id=1, source_target_pairs={{0,2},{1,3},{2,0},{3,1},{4,6},{5,7},{6,4},{7,5},{8,10},{9,11},{10,... | collective-permute-start | bytes 786440 | tf_op jit(solution)/shard_map/ppermute | solution.py:26
  75.2 21.5 %collective-permute-start.3 = (bf16[2,2,64,512]{3,2,1,0:T(8,128)(2,1)S(1)}, bf16[2,2,64,512]{3,2,1,0:T(8,128)(2,1)S(1)}, u32[]{:S(2)}, u32[]{:S(2)}) collective-permute-start(bf16[2,2,64,512]{3,2,1,0:T(8,128)(2,1)S(1)} %get-tuple-element.38), channel_id=1, source_target_pairs={{0,4},{1,5},{2,6},{3,7},{4,0},{5,1},{6,2},{7,3},{8,12},{9,13},{10,... | collective-permute-start | bytes 786440 | tf_op jit(solution)/shard_map/ppermute | solution.py:26
  75.3 23.0 %collective-permute-start.4 = (bf16[2,2,64,512]{3,2,1,0:T(8,128)(2,1)S(1)}, bf16[2,2,64,512]{3,2,1,0:T(8,128)(2,1)S(1)}, u32[]{:S(2)}, u32[]{:S(2)}) collective-permute-start(bf16[2,2,64,512]{3,2,1,0:T(8,128)(2,1)S(1)} %get-tuple-element.39), channel_id=1, source_target_pairs={{0,6},{1,7},{2,4},{3,5},{4,2},{5,3},{6,0},{7,1},{8,14},{9,15},{10,... | collective-permute-start | bytes 786440 | tf_op jit(solution)/shard_map/ppermute | solution.py:26
  78.0 15.3 %collective-permute-start.22 = (bf16[1,2,64,512]{3,2,1,0:T(8,128)(2,1)S(1)}, bf16[1,2,64,512]{3,2,1,0:T(8,128)(2,1)S(1)}, u32[]{:S(2)}, u32[]{:S(2)}) collective-permute-start(bf16[1,2,64,512]{3,2,1,0:T(8,128)(2,1)S(1)} %get-tuple-element.48), channel_id=1, source_target_pairs={{0,12},{1,13},{2,14},{3,15},{4,8},{5,9},{6,10},{7,11},{8,4},{9,5},... | collective-permute-start | bytes 393224 | tf_op jit(solution)/shard_map/ppermute | solution.py:26
  80.5 15.5 %collective-permute-start.23 = (bf16[1,2,64,512]{3,2,1,0:T(8,128)(2,1)S(1)}, bf16[1,2,64,512]{3,2,1,0:T(8,128)(2,1)S(1)}, u32[]{:S(2)}, u32[]{:S(2)}) collective-permute-start(bf16[1,2,64,512]{3,2,1,0:T(8,128)(2,1)S(1)} %get-tuple-element.49), channel_id=1, source_target_pairs={{0,14},{1,15},{2,12},{3,13},{4,10},{5,11},{6,8},{7,9},{8,6},{9,7},... | collective-permute-start | bytes 393224 | tf_op jit(solution)/shard_map/ppermute | solution.py:26
  93.2 41.2 %collective-permute-start.30 = (bf16[1040,256]{1,0:T(8,128)(2,1)S(1)}, bf16[1040,256]{1,0:T(8,128)(2,1)S(1)}, u32[]{:S(2)}, u32[]{:S(2)}) collective-permute-start(bf16[1040,256]{1,0:T(8,128)(2,1)S(1)} %pad_maximum_fusion.refs_0_), channel_id=1, source_target_pairs={{8,4},{9,5},{10,6},{11,7},{4,8},{5,9},{6,10},{7,11},{24,20},{25,21... | collective-permute-start | bytes 1597448 | tf_op jit(solution)/shard_map/ppermute | solution.py:26
  95.9 39.8 %collective-permute-start.32 = (bf16[1040,256]{1,0:T(8,128)(2,1)S(1)}, bf16[1040,256]{1,0:T(8,128)(2,1)S(1)}, u32[]{:S(2)}, u32[]{:S(2)}) collective-permute-start(bf16[1040,256]{1,0:T(8,128)(2,1)S(1)} %collective-permute-done.26.refs_0_), channel_id=1, source_target_pairs={{8,4},{9,5},{10,6},{11,7},{4,8},{5,9},{6,10},{7,11},{24,20},{25,21... | collective-permute-start | bytes 1597448 | tf_op jit(solution)/shard_map/ppermute | solution.py:26
  96.6 32.5 %collective-permute-start.6 = (bf16[1,2,64,512]{3,2,1,0:T(8,128)(2,1)S(1)}, bf16[1,2,64,512]{3,2,1,0:T(8,128)(2,1)S(1)}, u32[]{:S(2)}, u32[]{:S(2)}) collective-permute-start(bf16[1,2,64,512]{3,2,1,0:T(8,128)(2,1)S(1)} %get-tuple-element.41), channel_id=1, source_target_pairs={{0,10},{1,11},{2,8},{3,9},{4,14},{5,15},{6,12},{7,13},{8,2},{9,3},... | collective-permute-start | bytes 393224 | tf_op jit(solution)/shard_map/ppermute | solution.py:26
  96.7 35.2 %collective-permute-start.7 = (bf16[1,2,64,512]{3,2,1,0:T(8,128)(2,1)S(1)}, bf16[1,2,64,512]{3,2,1,0:T(8,128)(2,1)S(1)}, u32[]{:S(2)}, u32[]{:S(2)}) collective-permute-start(bf16[1,2,64,512]{3,2,1,0:T(8,128)(2,1)S(1)} %get-tuple-element.42), channel_id=1, source_target_pairs={{0,12},{1,13},{2,14},{3,15},{4,8},{5,9},{6,10},{7,11},{8,4},{9,5},... | collective-permute-start | bytes 393224 | tf_op jit(solution)/shard_map/ppermute | solution.py:26
  98.2 33.7 %collective-permute-start.8 = (bf16[1,2,64,512]{3,2,1,0:T(8,128)(2,1)S(1)}, bf16[1,2,64,512]{3,2,1,0:T(8,128)(2,1)S(1)}, u32[]{:S(2)}, u32[]{:S(2)}) collective-permute-start(bf16[1,2,64,512]{3,2,1,0:T(8,128)(2,1)S(1)} %get-tuple-element.43), channel_id=1, source_target_pairs={{0,14},{1,15},{2,12},{3,13},{4,10},{5,11},{6,8},{7,9},{8,6},{9,7},... | collective-permute-start | bytes 393224 | tf_op jit(solution)/shard_map/ppermute | solution.py:26
  129.1 36.6 %collective-permute-start.24 = (bf16[512,1024]{1,0:T(8,128)(2,1)S(1)}, bf16[512,1024]{1,0:T(8,128)(2,1)S(1)}, u32[]{:S(2)}, u32[]{:S(2)}) collective-permute-start(bf16[512,1024]{1,0:T(8,128)(2,1)S(1)} %contract_stem.3.refs_2_), channel_id=1, source_target_pairs={{0,1},{1,0},{2,3},{3,2},{4,5},{5,4},{6,7},{7,6},{8,9},{9,8},{10,11... | collective-permute-start | bytes 3145736 | tf_op jit(solution)/shard_map/ppermute | solution.py:35
  134.3 34.0 %collective-permute-start.19 = (bf16[512,1024]{1,0:T(8,128)(2,1)S(1)}, bf16[512,1024]{1,0:T(8,128)(2,1)S(1)}, u32[]{:S(2)}, u32[]{:S(2)}) collective-permute-start(bf16[512,1024]{1,0:T(8,128)(2,1)S(1)} %contract_stem.2.refs_2_), channel_id=1, source_target_pairs={{0,1},{1,0},{2,3},{3,2},{4,5},{5,4},{6,7},{7,6},{8,9},{9,8},{10,11... | collective-permute-start | bytes 3145736 | tf_op jit(solution)/shard_map/ppermute | solution.py:35
  134.4 18.4 %collective-permute-start.31 = (bf16[1040,256]{1,0:T(8,128)(2,1)S(1)}, bf16[1040,256]{1,0:T(8,128)(2,1)S(1)}, u32[]{:S(2)}, u32[]{:S(2)}) collective-permute-start(bf16[1040,256]{1,0:T(8,128)(2,1)S(1)} %collective-permute-done.30.refs_0_), channel_id=1, source_target_pairs={{4,0},{5,1},{6,2},{7,3},{8,12},{9,13},{10,14},{11,15},{20,16},{21,... | collective-permute-start | bytes 1597448 | tf_op jit(solution)/shard_map/ppermute | solution.py:26
  135.7 28.5 %collective-permute-start.36 = (bf16[1040,256]{1,0:T(8,128)(2,1)S(1)}, bf16[1040,256]{1,0:T(8,128)(2,1)S(1)}, u32[]{:S(2)}, u32[]{:S(2)}) collective-permute-start(bf16[1040,256]{1,0:T(8,128)(2,1)S(1)} %collective-permute-done.32.refs_1_), channel_id=1, source_target_pairs={{4,0},{5,1},{6,2},{7,3},{8,12},{9,13},{10,14},{11,15},{20,16},{21,... | collective-permute-start | bytes 1597448 | tf_op jit(solution)/shard_map/ppermute | solution.py:26
  137.2 27.8 %collective-permute-start = (bf16[1040,256]{1,0:T(8,128)(2,1)S(1)}, bf16[1040,256]{1,0:T(8,128)(2,1)S(1)}, u32[]{:S(2)}, u32[]{:S(2)}) collective-permute-start(bf16[1040,256]{1,0:T(8,128)(2,1)S(1)} %pad_maximum_fusion.refs_0_), channel_id=1, source_target_pairs={{0,2},{1,3},{2,0},{3,1},{4,6},{5,7},{6,4},{7,5},{8,10},{9,11},{10,... | collective-permute-start | bytes 1597448 | tf_op jit(solution)/shard_map/ppermute | solution.py:26
  152.8 18.8 %collective-permute-start.27 = (bf16[1040,256]{1,0:T(8,128)(2,1)S(1)}, bf16[1040,256]{1,0:T(8,128)(2,1)S(1)}, u32[]{:S(2)}, u32[]{:S(2)}) collective-permute-start(bf16[1040,256]{1,0:T(8,128)(2,1)S(1)} %collective-permute-done.26.refs_0_), channel_id=1, source_target_pairs={{0,2},{1,3},{2,0},{3,1},{4,6},{5,7},{6,4},{7,5},{8,10},{9,11},{10,... | collective-permute-start | bytes 1597448 | tf_op jit(solution)/shard_map/ppermute | solution.py:26
  164.2 14.3 %collective-permute-start.33 = (bf16[1040,256]{1,0:T(8,128)(2,1)S(1)}, bf16[1040,256]{1,0:T(8,128)(2,1)S(1)}, u32[]{:S(2)}, u32[]{:S(2)}) collective-permute-start(bf16[1040,256]{1,0:T(8,128)(2,1)S(1)} %merge.2.refs_0_), channel_id=1, source_target_pairs={{0,2},{1,3},{2,0},{3,1},{4,6},{5,7},{6,4},{7,5},{8,10},{9,11},{10,... | collective-permute-start | bytes 1597448 | tf_op jit(solution)/shard_map/ppermute | solution.py:26
  165.0 25.0 %collective-permute-start.37 = (bf16[1040,256]{1,0:T(8,128)(2,1)S(1)}, bf16[1040,256]{1,0:T(8,128)(2,1)S(1)}, u32[]{:S(2)}, u32[]{:S(2)}) collective-permute-start(bf16[1040,256]{1,0:T(8,128)(2,1)S(1)} %merge.3.refs_0_), channel_id=1, source_target_pairs={{0,2},{1,3},{2,0},{3,1},{4,6},{5,7},{6,4},{7,5},{8,10},{9,11},{10,... | collective-permute-start | bytes 1597448 | tf_op jit(solution)/shard_map/ppermute | solution.py:26
  170.7 26.1 %collective-permute-start.25 = (bf16[2,2,32,256]{3,2,1,0:T(8,128)(2,1)S(1)}, bf16[2,2,32,256]{3,2,1,0:T(8,128)(2,1)S(1)}, u32[]{:S(2)}, u32[]{:S(2)}) collective-permute-start(bf16[2,2,32,256]{3,2,1,0:T(8,128)(2,1)S(1)} %get-tuple-element.53), channel_id=1, source_target_pairs={{0,2},{1,3},{2,0},{3,1},{4,6},{5,7},{6,4},{7,5},{8,10},{9,11},{10,... | collective-permute-start | bytes 196616 | tf_op jit(solution)/shard_map/ppermute | solution.py:26
  176.5 22.3 %collective-permute-start.28 = (bf16[2,2,32,256]{3,2,1,0:T(8,128)(2,1)S(1)}, bf16[2,2,32,256]{3,2,1,0:T(8,128)(2,1)S(1)}, u32[]{:S(2)}, u32[]{:S(2)}) collective-permute-start(bf16[2,2,32,256]{3,2,1,0:T(8,128)(2,1)S(1)} %get-tuple-element.56), channel_id=1, source_target_pairs={{0,4},{1,5},{2,6},{3,7},{4,0},{5,1},{6,2},{7,3},{8,12},{9,13},{10,... | collective-permute-start | bytes 196616 | tf_op jit(solution)/shard_map/ppermute | solution.py:26
  176.6 24.5 %collective-permute-start.29 = (bf16[2,2,32,256]{3,2,1,0:T(8,128)(2,1)S(1)}, bf16[2,2,32,256]{3,2,1,0:T(8,128)(2,1)S(1)}, u32[]{:S(2)}, u32[]{:S(2)}) collective-permute-start(bf16[2,2,32,256]{3,2,1,0:T(8,128)(2,1)S(1)} %get-tuple-element.57), channel_id=1, source_target_pairs={{0,6},{1,7},{2,4},{3,5},{4,2},{5,3},{6,0},{7,1},{8,14},{9,15},{10,... | collective-permute-start | bytes 196616 | tf_op jit(solution)/shard_map/ppermute | solution.py:26
  183.7 17.4 %collective-permute-start.34 = (bf16[2,2,32,256]{3,2,1,0:T(8,128)(2,1)S(1)}, bf16[2,2,32,256]{3,2,1,0:T(8,128)(2,1)S(1)}, u32[]{:S(2)}, u32[]{:S(2)}) collective-permute-start(bf16[2,2,32,256]{3,2,1,0:T(8,128)(2,1)S(1)} %get-tuple-element.60), channel_id=1, source_target_pairs={{0,8},{1,9},{2,10},{3,11},{4,12},{5,13},{6,14},{7,15},{8,0},{9,1},... | collective-permute-start | bytes 196616 | tf_op jit(solution)/shard_map/ppermute | solution.py:26
  190.0 11.0 %collective-permute-start.35 = (bf16[2,2,32,256]{3,2,1,0:T(8,128)(2,1)S(1)}, bf16[2,2,32,256]{3,2,1,0:T(8,128)(2,1)S(1)}, u32[]{:S(2)}, u32[]{:S(2)}) collective-permute-start(bf16[2,2,32,256]{3,2,1,0:T(8,128)(2,1)S(1)} %get-tuple-element.61), channel_id=1, source_target_pairs={{0,10},{1,11},{2,8},{3,9},{4,14},{5,15},{6,12},{7,13},{8,2},{9,3},... | collective-permute-start | bytes 196616 | tf_op jit(solution)/shard_map/ppermute | solution.py:26
  196.9 5.1 %collective-permute-start.38 = (bf16[2,2,32,256]{3,2,1,0:T(8,128)(2,1)S(1)}, bf16[2,2,32,256]{3,2,1,0:T(8,128)(2,1)S(1)}, u32[]{:S(2)}, u32[]{:S(2)}) collective-permute-start(bf16[2,2,32,256]{3,2,1,0:T(8,128)(2,1)S(1)} %get-tuple-element.64), channel_id=1, source_target_pairs={{0,12},{1,13},{2,14},{3,15},{4,8},{5,9},{6,10},{7,11},{8,4},{9,5},... | collective-permute-start | bytes 196616 | tf_op jit(solution)/shard_map/ppermute | solution.py:26
  198.8 6.4 %collective-permute-start.39 = (bf16[2,2,32,256]{3,2,1,0:T(8,128)(2,1)S(1)}, bf16[2,2,32,256]{3,2,1,0:T(8,128)(2,1)S(1)}, u32[]{:S(2)}, u32[]{:S(2)}) collective-permute-start(bf16[2,2,32,256]{3,2,1,0:T(8,128)(2,1)S(1)} %get-tuple-element.65), channel_id=1, source_target_pairs={{0,14},{1,15},{2,12},{3,13},{4,10},{5,11},{6,8},{7,9},{8,6},{9,7},... | collective-permute-start | bytes 196616 | tf_op jit(solution)/shard_map/ppermute | solution.py:26

commit v3 on v2

--- a/solution.py
+++ b/solution.py
@@ -325,36 +325,54 @@
     )(*states, *stems, *before)
 
 
-def final_kernel(*refs):
-    found, (table_ref, out_ref, rows_ref) = refs[:-3], refs[-3:]
+def final_kernel(first, count, *refs):
+    found, table_ref = refs[:count], refs[count]
+    before, (out_ref, rows_ref) = refs[count + 1 : -2], refs[-2:]
     seats, parts, inner, _ = found[0].shape
+    block = len(found) * seats * inner
     for d, piece in enumerate(found):
         for s in range(seats):
             for p in range(parts):
-                start = ((p * len(found) + d) * seats + s) * inner
+                start = p * block + (d * seats + s) * inner
                 rows_ref[start : start + inner, :] = piece[s, p]
-    result = lax.dot_general(
-        rows_ref[...], table_ref[...], (((0,), (0,)), ((), ())), preferred_element_type=F32
-    ).astype(BF16)
-    width = out_ref.shape[2]
+    total = before[0][...] if before else 0.0
+    half = table_ref.shape[0] // parts
+    offset = first * seats * inner
     for p in range(parts):
-        out_ref[:, p, :] = result[:, p * width : (p + 1) * width]
-
-
-def contract_final(found, table):
-    parts, _, samples = found[0].shape[1:]
-    return pl.pallas_call(
-        final_kernel,
-        in_specs=[VMEM] * (len(found) + 1),
+        total += lax.dot_general(
+            rows_ref[p * block : (p + 1) * block, :],
+            table_ref[p * half + offset : p * half + offset + block, :],
+            (((0,), (0,)), ((), ())),
+            preferred_element_type=F32,
+        )
+    if out_ref.ndim == 2:
+        out_ref[...] = total
+    else:
+        result = total.astype(BF16)
+        width = out_ref.shape[2]
+        for p in range(parts):
+            out_ref[:, p, :] = result[:, p * width : (p + 1) * width]
+
+
+def contract_final(found, table, first, before):
+    seats, parts, inner, samples = found[0].shape
+    last = (first + len(found)) * seats * inner * parts == table.shape[0]
+    shape = (samples, parts, table.shape[1] // parts) if last else (samples, table.shape[1])
+    rows = len(found) * seats * parts * inner
+    return pl.pallas_call(
+        functools.partial(final_kernel, first, len(found)),
+        in_specs=[VMEM] * (len(found) + 1 + len(before)),
         out_specs=VMEM,
-        out_shape=jax.ShapeDtypeStruct((samples, parts, table.shape[1] // parts), BF16),
-        scratch_shapes=[pltpu.VMEM((table.shape[0], samples), BF16)],
+        out_shape=jax.ShapeDtypeStruct(shape, BF16 if last else F32),
+        scratch_shapes=[pltpu.VMEM((rows, samples), BF16)],
         cost_estimate=pl.CostEstimate(
-            flops=2 * table.size * samples, bytes_accessed=2 * table.size, transcendentals=0
+            flops=2 * rows * samples * table.shape[1],
+            bytes_accessed=2 * rows * table.shape[1],
+            transcendentals=0,
         ),
         compiler_params=params(),
         name="contract_final",
-    )(*found, table)
+    )(*found, table, *before)
 
 
 def is_short(count_cuts, count_ma, rounds):
@@ -433,7 +451,9 @@
     else:
         found = lax.all_to_all(jnp.stack(found), "ma", split_axis=0, concat_axis=0, tiled=True)
         found = [found[d] for d in range(count_ma)]
-    return contract_final(found, final_table)
+    cut = count_ma - 2
+    sums = contract_final(found[:cut], final_table, 0, [])
+    return contract_final(found[cut:], final_table, cut, [sums])
 
 
 def solution(mesh):

time: 210 us -> 215 us (1.024)
  starting transfers between devices: 55.9 us -> 66.9 us
  waiting for transfers between devices: 106 us -> 99.7 us
    ppermute x34, waiting for transfers between devices: 96.8 us -> 81.6 us  [permute(): return lax.ppermute(value, AXES, full)]
    ppermute x34, starting transfers between devices: 46.4 us -> 55.6 us  [permute(): return lax.ppermute(value, AXES, full)]
    ppermute x2, waiting for transfers between devices: 9.58 us -> 18.1 us  [swap_cuts(): return lax.ppermute(value, ('cuts',) + AXES, pairs)]
    ppermute x4, starting transfers between devices: 6.38 us -> 8.79 us  [swap_mb(): return lax.ppermute(value, AXES, [(m, m ^ offset) for m in range(count)])]
  transfers between devices with their start and end apart: 40 -> 40, of which waited for: 12 -> 16; matrix products, arithmetic and copies ran while one was open for 3% -> 3% of each run, Pallas kernels for 16% -> 16%
where the time goes in v3:
time: 215 us; the launch traced here: 212 us
  waiting for transfers between devices  99.7 us (46%)
  starting transfers between devices  66.9 us (31%)
  Pallas kernels  36.7 us (17%)
  local copies, waits for them, and re-layouts  5.86 us (3%)
  other arithmetic  2.31 us (1%)
    ppermute x34, waiting for transfers between devices, permute(): return lax.ppermute(value, AXES, full)  81.6 us
    ppermute x34, starting transfers between devices, permute(): return lax.ppermute(value, AXES, full)  55.6 us
    pallas_call x8, Pallas kernels, contract_samples(): pl.pallas_call(functools.partial(sample_kernel, groups, first, scale, man...  20 us
    ppermute x2, waiting for transfers between devices, swap_cuts(): return lax.ppermute(value, ('cuts',) + AXES, pairs)  18.1 us
    ppermute x4, starting transfers between devices, swap_mb(): return lax.ppermute(value, AXES, [(m, m ^ offset) for m in range(count)])  8.79 us
    pallas_call x1, Pallas kernels, tables(): pl.pallas_call(functools.partial(table_kernel, inner, count_mb, relative,...  5.84 us
    pallas_call x2, Pallas kernels, contract_stem(): pl.pallas_call(functools.partial(stem_kernel, blocks), in_specs=[VMEM] *...  4.66 us
  transfers between devices with their start and end apart: 40, of which 16 were waited for; matrix products, arithmetic and copies ran while one was open for 3% of the time, Pallas kernels for 16%

profile of v3, /device:TPU:1, one launch (start us, length us, event | category | flops | bytes accessed | tf_op | source)
XLA Modules:
  0.0 211.8 jit_solution(9491447865858334065)
XLA Ops:
  1.0 3.2 %collective-permute-start.16 = (bf16[2,64,512]{2,1,0:T(8,128)(2,1)S(1)}, bf16[2,64,512]{2,1,0:T(8,128)(2,1)S(1)}, u32[]{:S(2)}, u32[]{:S(2)}) collective-permute-start(bf16[2,64,512]{2,1,0:T(8,128)(2,1)S(1)} %fusion.refs_0_), channel_id=1, source_target_pairs={{0,8},{1,9},{2,10},{3,11},{4,12},{5,13},{6,14},{7,15},{8,0},{9,1},... | collective-permute-start | bytes 393224 | tf_op jit(solution)/shard_map/ppermute | solution.py:26
  5.2 3.3 %collective-permute-start.18 = (bf16[2,64,512]{2,1,0:T(8,128)(2,1)S(1)}, bf16[2,64,512]{2,1,0:T(8,128)(2,1)S(1)}, u32[]{:S(2)}, u32[]{:S(2)}) collective-permute-start(bf16[2,64,512]{2,1,0:T(8,128)(2,1)S(1)} %fusion.refs_0_), channel_id=1, source_target_pairs={{0,12},{1,13},{2,14},{3,15},{4,8},{5,9},{6,10},{7,11},{8,4},{9,5},... | collective-permute-start | bytes 393224 | tf_op jit(solution)/shard_map/ppermute | solution.py:26
  9.7 8.9 %collective-permute-done.16.refs_0_ = bf16[2,64,512]{2,1,0:T(8,128)(2,1)S(1)} collective-permute-done((bf16[2,64,512]{2,1,0:T(8,128)(2,1)S(1)}, bf16[2,64,512]{2,1,0:T(8,128)(2,1)S(1)}, u32[]{:S(2)}, u32[]{:S(2)}) %collective-permute-start.16) | collective-permute-done | bytes 131104 | tf_op jit(solution)/shard_map/ppermute | solution.py:26
  19.8 2.4 %collective-permute-done.17.refs_1_ = bf16[2,64,512]{2,1,0:T(8,128)(2,1)S(1)} collective-permute-done((bf16[2,64,512]{2,1,0:T(8,128)(2,1)S(1)}, bf16[2,64,512]{2,1,0:T(8,128)(2,1)S(1)}, u32[]{:S(2)}, u32[]{:S(2)}) %collective-permute-start.17) | collective-permute-done | bytes 131104 | tf_op jit(solution)/shard_map/ppermute | solution.py:26
  22.2 1.4 collective-permute-start.15
  24.9 2.8 %collective-permute-done.15.refs_3_ = bf16[2,64,512]{2,1,0:T(8,128)(2,1)S(1)} collective-permute-done((bf16[2,64,512]{2,1,0:T(8,128)(2,1)S(1)}, bf16[2,64,512]{2,1,0:T(8,128)(2,1)S(1)}, u32[]{:S(2)}, u32[]{:S(2)}) %collective-permute-start.15) | collective-permute-done | bytes 131104 | tf_op jit(solution)/shard_map/ppermute | solution.py:26
  29.1 6.9 %collective-permute-done.21.refs_3_ = bf16[4,2,64,512]{3,2,1,0:T(8,128)(2,1)S(1)} collective-permute-done((bf16[4,2,64,512]{3,2,1,0:T(8,128)(2,1)S(1)}, bf16[4,2,64,512]{3,2,1,0:T(8,128)(2,1)S(1)}, u32[]{:S(2)}, u32[]{:S(2)}) %collective-permute-start.21) | collective-permute-done | bytes 524320 | tf_op jit(solution)/shard_map/ppermute | solution.py:42
  36.0 11.2 %collective-permute-done.20.refs_2_ = bf16[4,2,64,512]{3,2,1,0:T(8,128)(2,1)S(1)} collective-permute-done((bf16[4,2,64,512]{3,2,1,0:T(8,128)(2,1)S(1)}, bf16[4,2,64,512]{3,2,1,0:T(8,128)(2,1)S(1)}, u32[]{:S(2)}, u32[]{:S(2)}) %collective-permute-start.20) | collective-permute-done | bytes 524320 | tf_op jit(solution)/shard_map/ppermute | solution.py:42
  47.2 2.0 collect.1.refs_0_
  49.2 2.1 collective-permute-start.22
  51.3 2.7 %reshape.13.refs_0_ = bf16[2,8,2,64,512]{4,3,2,1,0:T(8,128)(2,1)S(1)} reshape(bf16[2,512,2,512]{3,2,1,0:T(2,128)(2,1)} %param.6) | data formatting | bytes 4194304 | tf_op jit(solution)/shard_map/reshape | solution.py:398
  55.2 2.0 copy.7
  58.3 5.9 %collective-permute-start.1 = (bf16[1040,256]{1,0:T(8,128)(2,1)S(1)}, bf16[1040,256]{1,0:T(8,128)(2,1)S(1)}, u32[]{:S(2)}, u32[]{:S(2)}) collective-permute-start(bf16[1040,256]{1,0:T(8,128)(2,1)S(1)} %pad_maximum_fusion.refs_0_), channel_id=1, source_target_pairs={{4,0},{5,1},{6,2},{7,3},{0,4},{1,5},{2,6},{3,7},{12,8},{13,9},{14,... | collective-permute-start | bytes 1597448 | tf_op jit(solution)/shard_map/ppermute | solution.py:26
  65.6 5.0 %collective-permute-start.24 = (bf16[1,2,64,512]{3,2,1,0:T(8,128)(2,1)S(1)}, bf16[1,2,64,512]{3,2,1,0:T(8,128)(2,1)S(1)}, u32[]{:S(2)}, u32[]{:S(2)}) collective-permute-start(bf16[1,2,64,512]{3,2,1,0:T(8,128)(2,1)S(1)} %get-tuple-element.46), channel_id=1, source_target_pairs={{0,8},{1,9},{2,10},{3,11},{4,12},{5,13},{6,14},{7,15},{8,0},{9,1},... | collective-permute-start | bytes 393224 | tf_op jit(solution)/shard_map/ppermute | solution.py:26
  70.6 5.6 %collective-permute-done.1.refs_0_ = bf16[1040,256]{1,0:T(8,128)(2,1)S(1)} collective-permute-done((bf16[1040,256]{1,0:T(8,128)(2,1)S(1)}, bf16[1040,256]{1,0:T(8,128)(2,1)S(1)}, u32[]{:S(2)}, u32[]{:S(2)}) %collective-permute-start.1) | collective-permute-done | bytes 532512 | tf_op jit(solution)/shard_map/ppermute | solution.py:26
  76.2 4.9 %collective-permute-start.26 = (bf16[1,2,64,512]{3,2,1,0:T(8,128)(2,1)S(1)}, bf16[1,2,64,512]{3,2,1,0:T(8,128)(2,1)S(1)}, u32[]{:S(2)}, u32[]{:S(2)}) collective-permute-start(bf16[1,2,64,512]{3,2,1,0:T(8,128)(2,1)S(1)} %get-tuple-element.48), channel_id=1, source_target_pairs={{0,12},{1,13},{2,14},{3,15},{4,8},{5,9},{6,10},{7,11},{8,4},{9,5},... | collective-permute-start | bytes 393224 | tf_op jit(solution)/shard_map/ppermute | solution.py:26
  81.9 11.1 %collective-permute-done.24.refs_4_ = bf16[1,2,64,512]{3,2,1,0:T(8,128)(2,1)S(1)} collective-permute-done((bf16[1,2,64,512]{3,2,1,0:T(8,128)(2,1)S(1)}, bf16[1,2,64,512]{3,2,1,0:T(8,128)(2,1)S(1)}, u32[]{:S(2)}, u32[]{:S(2)}) %collective-permute-start.24) | collective-permute-done | bytes 131104 | tf_op jit(solution)/shard_map/ppermute | solution.py:26
  93.0 2.7 %collective-permute-done.25.refs_5_ = bf16[1,2,64,512]{3,2,1,0:T(8,128)(2,1)S(1)} collective-permute-done((bf16[1,2,64,512]{3,2,1,0:T(8,128)(2,1)S(1)}, bf16[1,2,64,512]{3,2,1,0:T(8,128)(2,1)S(1)}, u32[]{:S(2)}, u32[]{:S(2)}) %collective-permute-start.25) | collective-permute-done | bytes 131104 | tf_op jit(solution)/shard_map/ppermute | solution.py:26
  96.3 3.2 %collective-permute-start.27 = (bf16[1,2,64,512]{3,2,1,0:T(8,128)(2,1)S(1)}, bf16[1,2,64,512]{3,2,1,0:T(8,128)(2,1)S(1)}, u32[]{:S(2)}, u32[]{:S(2)}) collective-permute-start(bf16[1,2,64,512]{3,2,1,0:T(8,128)(2,1)S(1)} %get-tuple-element.49), channel_id=1, source_target_pairs={{0,14},{1,15},{2,12},{3,13},{4,10},{5,11},{6,8},{7,9},{8,6},{9,7},... | collective-permute-start | bytes 393224 | tf_op jit(solution)/shard_map/ppermute | solution.py:26
  99.5 1.5 collective-permute-start.10
  101.0 5.8 %tables.1 = (bf16[1024,1024]{1,0:T(8,128)(2,1)S(1)}, bf16[1024,1024]{1,0:T(8,128)(2,1)S(1)}, bf16[1024,1024]{1,0:T(8,128)(2,1)S(1)}) custom-call(s32[4]{0:T(128)S(1)} %pad_add_fusion.1.place_ref, s32[2,512]{1,0:T(2,128)S(1)} %copy-done, bf16[2,2,512,512]{3,2,1,0:T(8,128)(2,1)} %collect.1.refs_0_, bf16[2,2,512,512]{3,2,1,0:T(8,128)(2,1)} %collective-permute-done.22.refs_1_), custom_call_target="tpu_custom_call" | custom-call | flops 2147483648 | bytes 10485760 | tf_op jit(solution)/shard_map/tables/pallas_call | solution.py:219
  106.9 2.5 %collective-permute-done.27.refs_7_ = bf16[1,2,64,512]{3,2,1,0:T(8,128)(2,1)S(1)} collective-permute-done((bf16[1,2,64,512]{3,2,1,0:T(8,128)(2,1)S(1)}, bf16[1,2,64,512]{3,2,1,0:T(8,128)(2,1)S(1)}, u32[]{:S(2)}, u32[]{:S(2)}) %collective-permute-start.27) | collective-permute-done | bytes 131104 | tf_op jit(solution)/shard_map/ppermute | solution.py:26
  111.4 1.3 collective-permute-start.11
  112.7 1.6 collective-permute-start.12
  115.4 2.3 %contract_stem.3.refs_2_ = bf16[512,1024]{1,0:T(8,128)(2,1)S(1)} custom-call(bf16[2,2,64,512]{3,2,1,0:T(8,128)(2,1)S(1)} %get-tuple-element.36.refs_0_, bf16[2,2,64,512]{3,2,1,0:T(8,128)(2,1)S(1)} %collective-permute-done.6.refs_1_, bf16[2,2,64,512]{3,2,1,0:T(8,128)(2,1)S(1)} %collective-permute-done.7.refs_2_, ...), custom_call_target="tpu_custom_call" | custom-call | flops 2147483648 | bytes 6291456 | tf_op jit(solution)/shard_map/contract_stem/pallas_call | solution.py:262
  117.8 5.7 %collective-permute-start.28 = (bf16[512,1024]{1,0:T(8,128)(2,1)S(1)}, bf16[512,1024]{1,0:T(8,128)(2,1)S(1)}, u32[]{:S(2)}, u32[]{:S(2)}) collective-permute-start(bf16[512,1024]{1,0:T(8,128)(2,1)S(1)} %contract_stem.3.refs_2_), channel_id=1, source_target_pairs={{0,1},{1,0},{2,3},{3,2},{4,5},{5,4},{6,7},{7,6},{8,9},{9,8},{10,11... | collective-permute-start | bytes 3145736 | tf_op jit(solution)/shard_map/ppermute | solution.py:35
  123.5 17.6 %collective-permute-done.9.refs_4_ = bf16[1,2,64,512]{3,2,1,0:T(8,128)(2,1)S(1)} collective-permute-done((bf16[1,2,64,512]{3,2,1,0:T(8,128)(2,1)S(1)}, bf16[1,2,64,512]{3,2,1,0:T(8,128)(2,1)S(1)}, u32[]{:S(2)}, u32[]{:S(2)}) %collective-permute-start.9) | collective-permute-done | bytes 131104 | tf_op jit(solution)/shard_map/ppermute | solution.py:26
  141.0 2.3 %contract_stem.2.refs_2_ = bf16[512,1024]{1,0:T(8,128)(2,1)S(1)} custom-call(bf16[2,2,64,512]{3,2,1,0:T(8,128)(2,1)S(1)} %get-tuple-element.36.refs_0_, bf16[2,2,64,512]{3,2,1,0:T(8,128)(2,1)S(1)} %collective-permute-done.6.refs_1_, bf16[2,2,64,512]{3,2,1,0:T(8,128)(2,1)S(1)} %collective-permute-done.7.refs_2_, ...), custom_call_target="tpu_custom_call" | custom-call | flops 2147483648 | bytes 6291456 | tf_op jit(solution)/shard_map/contract_stem/pallas_call | solution.py:262
  144.4 1.5 collective-permute-start.3
  147.5 12.4 %collective-permute-done.3.refs_1_ = bf16[1040,256]{1,0:T(8,128)(2,1)S(1)} collective-permute-done((bf16[1040,256]{1,0:T(8,128)(2,1)S(1)}, bf16[1040,256]{1,0:T(8,128)(2,1)S(1)}, u32[]{:S(2)}, u32[]{:S(2)}) %collective-permute-start.3) | collective-permute-done | bytes 532512 | tf_op jit(solution)/shard_map/ppermute | solution.py:26
  161.5 2.5 %contract_samples.14 = (bf16[2,2,32,256]{3,2,1,0:T(8,128)(2,1)S(1)}, bf16[2,2,32,256]{3,2,1,0:T(8,128)(2,1)S(1)}) custom-call(bf16[1040,256]{1,0:T(8,128)(2,1)S(1)} %merge.3.refs_0_, bf16[1040,256]{1,0:T(8,128)(2,1)S(1)} %collective-permute-done.37.refs_1_, bf16[512,1024]{1,0:T(8,128)(2,1)S(1)} %contract_stem.3.refs_2_, ...), custom_call_target="tpu_custom_call" | custom-call | flops 2147483648 | bytes 3162112 | tf_op jit(solution)/shard_map/contract_samples/pallas_call | solution.py:312
  164.0 2.5 %contract_samples.15 = (bf16[2,2,32,256]{3,2,1,0:T(8,128)(2,1)S(1)}, bf16[2,2,32,256]{3,2,1,0:T(8,128)(2,1)S(1)}) custom-call(bf16[1040,256]{1,0:T(8,128)(2,1)S(1)} %merge.3.refs_0_, bf16[1040,256]{1,0:T(8,128)(2,1)S(1)} %collective-permute-done.37.refs_1_, bf16[512,1024]{1,0:T(8,128)(2,1)S(1)} %contract_stem.2.refs_2_, ...), custom_call_target="tpu_custom_call" | custom-call | flops 2147483648 | bytes 3162112 | tf_op jit(solution)/shard_map/contract_samples/pallas_call | solution.py:312
  166.5 1.6 collective-permute-start.38
  168.2 1.6 collective-permute-start.39
  171.1 2.5 %contract_samples.12 = (bf16[2,2,32,256]{3,2,1,0:T(8,128)(2,1)S(1)}, bf16[2,2,32,256]{3,2,1,0:T(8,128)(2,1)S(1)}) custom-call(bf16[1040,256]{1,0:T(8,128)(2,1)S(1)} %collective-permute-done.1.refs_0_, bf16[1040,256]{1,0:T(8,128)(2,1)S(1)} %collective-permute-done.33.refs_1_, bf16[512,1024]{1,0:T(8,128)(2,1)S(1)} %contract_stem.3.refs_2_, ...), custom_call_target="tpu_custom_call" | custom-call | flops 2147483648 | bytes 3162112 | tf_op jit(solution)/shard_map/contract_samples/pallas_call | solution.py:312
  173.6 2.5 %contract_samples.13 = (bf16[2,2,32,256]{3,2,1,0:T(8,128)(2,1)S(1)}, bf16[2,2,32,256]{3,2,1,0:T(8,128)(2,1)S(1)}) custom-call(bf16[1040,256]{1,0:T(8,128)(2,1)S(1)} %collective-permute-done.1.refs_0_, bf16[1040,256]{1,0:T(8,128)(2,1)S(1)} %collective-permute-done.33.refs_1_, bf16[512,1024]{1,0:T(8,128)(2,1)S(1)} %contract_stem.2.refs_2_, ...), custom_call_target="tpu_custom_call" | custom-call | flops 2147483648 | bytes 3162112 | tf_op jit(solution)/shard_map/contract_samples/pallas_call | solution.py:312
  176.0 1.9 collective-permute-start.34
  178.0 5.9 %collective-permute-done.31.refs_1_ = bf16[1040,256]{1,0:T(8,128)(2,1)S(1)} collective-permute-done((bf16[1040,256]{1,0:T(8,128)(2,1)S(1)}, bf16[1040,256]{1,0:T(8,128)(2,1)S(1)}, u32[]{:S(2)}, u32[]{:S(2)}) %collective-permute-start.31) | collective-permute-done | bytes 532512 | tf_op jit(solution)/shard_map/ppermute | solution.py:26
  183.9 2.7 %collective-permute-start.35 = (bf16[2,2,32,256]{3,2,1,0:T(8,128)(2,1)S(1)}, bf16[2,2,32,256]{3,2,1,0:T(8,128)(2,1)S(1)}, u32[]{:S(2)}, u32[]{:S(2)}) collective-permute-start(bf16[2,2,32,256]{3,2,1,0:T(8,128)(2,1)S(1)} %get-tuple-element.62), channel_id=1, source_target_pairs={{0,6},{1,7},{2,4},{3,5},{4,2},{5,3},{6,0},{7,1},{8,14},{9,15},{10,... | collective-permute-start | bytes 196616 | tf_op jit(solution)/shard_map/ppermute | solution.py:26
  186.5 2.5 %contract_samples.10 = (bf16[2,2,32,256]{3,2,1,0:T(8,128)(2,1)S(1)}, bf16[2,2,32,256]{3,2,1,0:T(8,128)(2,1)S(1)}) custom-call(bf16[1040,256]{1,0:T(8,128)(2,1)S(1)} %pad_maximum_fusion.refs_0_, bf16[1040,256]{1,0:T(8,128)(2,1)S(1)} %collective-permute-done.31.refs_1_, bf16[512,1024]{1,0:T(8,128)(2,1)S(1)} %contract_stem.3.refs_2_, ...), custom_call_target="tpu_custom_call" | custom-call | flops 2147483648 | bytes 3162112 | tf_op jit(solution)/shard_map/contract_samples/pallas_call | solution.py:312
  189.0 2.7 %contract_samples.11 = (bf16[2,2,32,256]{3,2,1,0:T(8,128)(2,1)S(1)}, bf16[2,2,32,256]{3,2,1,0:T(8,128)(2,1)S(1)}) custom-call(bf16[1040,256]{1,0:T(8,128)(2,1)S(1)} %pad_maximum_fusion.refs_0_, bf16[1040,256]{1,0:T(8,128)(2,1)S(1)} %collective-permute-done.31.refs_1_, bf16[512,1024]{1,0:T(8,128)(2,1)S(1)} %contract_stem.2.refs_2_, ...), custom_call_target="tpu_custom_call" | custom-call | flops 2147483648 | bytes 3162112 | tf_op jit(solution)/shard_map/contract_samples/pallas_call | solution.py:312
  191.7 5.0 %collective-permute-done.4.refs_1_ = bf16[1040,256]{1,0:T(8,128)(2,1)S(1)} collective-permute-done((bf16[1040,256]{1,0:T(8,128)(2,1)S(1)}, bf16[1040,256]{1,0:T(8,128)(2,1)S(1)}, u32[]{:S(2)}, u32[]{:S(2)}) %collective-permute-start.4) | collective-permute-done | bytes 532512 | tf_op jit(solution)/shard_map/ppermute | solution.py:26
  197.8 2.5 %contract_samples.8 = (bf16[2,2,32,256]{3,2,1,0:T(8,128)(2,1)S(1)}, bf16[2,2,32,256]{3,2,1,0:T(8,128)(2,1)S(1)}) custom-call(bf16[1040,256]{1,0:T(8,128)(2,1)S(1)} %merge.2.refs_0_, bf16[1040,256]{1,0:T(8,128)(2,1)S(1)} %collective-permute-done.4.refs_1_, bf16[512,1024]{1,0:T(8,128)(2,1)S(1)} %contract_stem.3.refs_2_, ...), custom_call_target="tpu_custom_call" | custom-call | flops 2147483648 | bytes 3162112 | tf_op jit(solution)/shard_map/contract_samples/pallas_call | solution.py:312
  200.3 2.5 %contract_samples.9 = (bf16[2,2,32,256]{3,2,1,0:T(8,128)(2,1)S(1)}, bf16[2,2,32,256]{3,2,1,0:T(8,128)(2,1)S(1)}) custom-call(bf16[1040,256]{1,0:T(8,128)(2,1)S(1)} %merge.2.refs_0_, bf16[1040,256]{1,0:T(8,128)(2,1)S(1)} %collective-permute-done.4.refs_1_, bf16[512,1024]{1,0:T(8,128)(2,1)S(1)} %contract_stem.2.refs_2_, ...), custom_call_target="tpu_custom_call" | custom-call | flops 2147483648 | bytes 3162112 | tf_op jit(solution)/shard_map/contract_samples/pallas_call | solution.py:312
  202.8 1.8 collective-permute-start.29
  204.6 1.6 collective-permute-start.30
  207.9 2.5 %collective-permute-done.30.refs_1_ = bf16[2,2,32,256]{3,2,1,0:T(8,128)(2,1)S(1)} collective-permute-done((bf16[2,2,32,256]{3,2,1,0:T(8,128)(2,1)S(1)}, bf16[2,2,32,256]{3,2,1,0:T(8,128)(2,1)S(1)}, u32[]{:S(2)}, u32[]{:S(2)}) %collective-permute-start.30) | collective-permute-done | bytes 65568 | tf_op jit(solution)/shard_map/ppermute | solution.py:26
  210.4 1.4 contract_final.3
  (67 shorter events, 23.7 us)
Async XLA Ops:
  1.0 17.6 %collective-permute-start.16 = (bf16[2,64,512]{2,1,0:T(8,128)(2,1)S(1)}, bf16[2,64,512]{2,1,0:T(8,128)(2,1)S(1)}, u32[]{:S(2)}, u32[]{:S(2)}) collective-permute-start(bf16[2,64,512]{2,1,0:T(8,128)(2,1)S(1)} %fusion.refs_0_), channel_id=1, source_target_pairs={{0,8},{1,9},{2,10},{3,11},{4,12},{5,13},{6,14},{7,15},{8,0},{9,1},... | collective-permute-start | bytes 393224 | tf_op jit(solution)/shard_map/ppermute | solution.py:26
  4.2 18.0 %collective-permute-start.17 = (bf16[2,64,512]{2,1,0:T(8,128)(2,1)S(1)}, bf16[2,64,512]{2,1,0:T(8,128)(2,1)S(1)}, u32[]{:S(2)}, u32[]{:S(2)}) collective-permute-start(bf16[2,64,512]{2,1,0:T(8,128)(2,1)S(1)} %fusion.refs_0_), channel_id=1, source_target_pairs={{0,10},{1,11},{2,8},{3,9},{4,14},{5,15},{6,12},{7,13},{8,2},{9,3},... | collective-permute-start | bytes 393224 | tf_op jit(solution)/shard_map/ppermute | solution.py:26
  5.2 18.4 %collective-permute-start.18 = (bf16[2,64,512]{2,1,0:T(8,128)(2,1)S(1)}, bf16[2,64,512]{2,1,0:T(8,128)(2,1)S(1)}, u32[]{:S(2)}, u32[]{:S(2)}) collective-permute-start(bf16[2,64,512]{2,1,0:T(8,128)(2,1)S(1)} %fusion.refs_0_), channel_id=1, source_target_pairs={{0,12},{1,13},{2,14},{3,15},{4,8},{5,9},{6,10},{7,11},{8,4},{9,5},... | collective-permute-start | bytes 393224 | tf_op jit(solution)/shard_map/ppermute | solution.py:26
  8.5 15.1 %collective-permute-start.19 = (bf16[2,64,512]{2,1,0:T(8,128)(2,1)S(1)}, bf16[2,64,512]{2,1,0:T(8,128)(2,1)S(1)}, u32[]{:S(2)}, u32[]{:S(2)}) collective-permute-start(bf16[2,64,512]{2,1,0:T(8,128)(2,1)S(1)} %fusion.refs_0_), channel_id=1, source_target_pairs={{0,14},{1,15},{2,12},{3,13},{4,10},{5,11},{6,8},{7,9},{8,6},{9,7},... | collective-permute-start | bytes 393224 | tf_op jit(solution)/shard_map/ppermute | solution.py:26
  8.5 16.4 %collective-permute-start.13 = (bf16[2,64,512]{2,1,0:T(8,128)(2,1)S(1)}, bf16[2,64,512]{2,1,0:T(8,128)(2,1)S(1)}, u32[]{:S(2)}, u32[]{:S(2)}) collective-permute-start(bf16[2,64,512]{2,1,0:T(8,128)(2,1)S(1)} %fusion.refs_0_), channel_id=1, source_target_pairs={{0,2},{1,3},{2,0},{3,1},{4,6},{5,7},{6,4},{7,5},{8,10},{9,11},{10,... | collective-permute-start | bytes 393224 | tf_op jit(solution)/shard_map/ppermute | solution.py:26
  18.6 6.3 %collective-permute-start.14 = (bf16[2,64,512]{2,1,0:T(8,128)(2,1)S(1)}, bf16[2,64,512]{2,1,0:T(8,128)(2,1)S(1)}, u32[]{:S(2)}, u32[]{:S(2)}) collective-permute-start(bf16[2,64,512]{2,1,0:T(8,128)(2,1)S(1)} %fusion.refs_0_), channel_id=1, source_target_pairs={{0,4},{1,5},{2,6},{3,7},{4,0},{5,1},{6,2},{7,3},{8,12},{9,13},{10,... | collective-permute-start | bytes 393224 | tf_op jit(solution)/shard_map/ppermute | solution.py:26
  22.2 5.5 %collective-permute-start.15 = (bf16[2,64,512]{2,1,0:T(8,128)(2,1)S(1)}, bf16[2,64,512]{2,1,0:T(8,128)(2,1)S(1)}, u32[]{:S(2)}, u32[]{:S(2)}) collective-permute-start(bf16[2,64,512]{2,1,0:T(8,128)(2,1)S(1)} %fusion.refs_0_), channel_id=1, source_target_pairs={{0,6},{1,7},{2,4},{3,5},{4,2},{5,3},{6,0},{7,1},{8,14},{9,15},{10,... | collective-permute-start | bytes 393224 | tf_op jit(solution)/shard_map/ppermute | solution.py:26
  23.6 12.3 %collective-permute-start.21 = (bf16[4,2,64,512]{3,2,1,0:T(8,128)(2,1)S(1)}, bf16[4,2,64,512]{3,2,1,0:T(8,128)(2,1)S(1)}, u32[]{:S(2)}, u32[]{:S(2)}) collective-permute-start(bf16[4,2,64,512]{3,2,1,0:T(8,128)(2,1)S(1)} %stack.31.refs_1_), channel_id=1, source_target_pairs={{0,16},{1,17},{2,18},{3,19},{4,20},{5,21},{6,22},{7,23},{8,24},{9,... | collective-permute-start | bytes 1572872 | tf_op jit(solution)/shard_map/ppermute | solution.py:42
  27.7 19.5 %collective-permute-start.20 = (bf16[4,2,64,512]{3,2,1,0:T(8,128)(2,1)S(1)}, bf16[4,2,64,512]{3,2,1,0:T(8,128)(2,1)S(1)}, u32[]{:S(2)}, u32[]{:S(2)}) collective-permute-start(bf16[4,2,64,512]{3,2,1,0:T(8,128)(2,1)S(1)} %stack.30.refs_0_), channel_id=1, source_target_pairs={{0,16},{1,17},{2,18},{3,19},{4,20},{5,21},{6,22},{7,23},{8,24},{9,... | collective-permute-start | bytes 1572872 | tf_op jit(solution)/shard_map/ppermute | solution.py:42
  49.2 50.3 %collective-permute-start.22 = (bf16[2,2,512,512]{3,2,1,0:T(8,128)(2,1)}, bf16[2,2,512,512]{3,2,1,0:T(8,128)(2,1)}, u32[]{:S(2)}, u32[]{:S(2)}) collective-permute-start(bf16[2,2,512,512]{3,2,1,0:T(8,128)(2,1)} %collect.1.refs_0_), channel_id=1, source_target_pairs={{0,1},{1,0},{2,3},{3,2},{4,5},{5,4},{6,7},{7,6},{8,9},{9,8},{10,11... | collective-permute-start | bytes 6291464 | tf_op jit(solution)/shard_map/ppermute | solution.py:35
  54.0 3.1 %copy-start.1 = (s32[256,1]{0,1:T(1,128)S(1)}, s32[256,1]{0,1:T(1,128)}, u32[]{:S(2)}) copy-start(s32[256,1]{0,1:T(1,128)} %param.10) | copy-start | bytes 3076
  55.2 9.8 %collective-permute-start.5 = (bf16[2,8,64,512]{3,2,1,0:T(8,128)(2,1)}, bf16[2,8,64,512]{3,2,1,0:T(8,128)(2,1)S(1)}, u32[]{:S(2)}, u32[]{:S(2)}) collective-permute-start(bf16[2,8,64,512]{3,2,1,0:T(8,128)(2,1)} %dynamic-slice_bitcast_fusion), channel_id=1, source_target_pairs={{0,1},{1,0},{2,3},{3,2},{4,5},{5,4},{6,7},{7,6},{8,9},{9,8},{10,11... | collective-permute-start | bytes 3145736 | tf_op jit(solution)/shard_map/ppermute | solution.py:35
  58.3 17.9 %collective-permute-start.1 = (bf16[1040,256]{1,0:T(8,128)(2,1)S(1)}, bf16[1040,256]{1,0:T(8,128)(2,1)S(1)}, u32[]{:S(2)}, u32[]{:S(2)}) collective-permute-start(bf16[1040,256]{1,0:T(8,128)(2,1)S(1)} %pad_maximum_fusion.refs_0_), channel_id=1, source_target_pairs={{4,0},{5,1},{6,2},{7,3},{0,4},{1,5},{2,6},{3,7},{12,8},{13,9},{14,... | collective-permute-start | bytes 1597448 | tf_op jit(solution)/shard_map/ppermute | solution.py:26
  64.2 17.5 %collective-permute-start = (bf16[1040,256]{1,0:T(8,128)(2,1)S(1)}, bf16[1040,256]{1,0:T(8,128)(2,1)S(1)}, u32[]{:S(2)}, u32[]{:S(2)}) collective-permute-start(bf16[1040,256]{1,0:T(8,128)(2,1)S(1)} %pad_maximum_fusion.refs_0_), channel_id=1, source_target_pairs={{8,4},{9,5},{10,6},{11,7},{4,8},{5,9},{6,10},{7,11},{24,20},{25,21... | collective-permute-start | bytes 1597448 | tf_op jit(solution)/shard_map/ppermute | solution.py:26
  65.6 27.4 %collective-permute-start.24 = (bf16[1,2,64,512]{3,2,1,0:T(8,128)(2,1)S(1)}, bf16[1,2,64,512]{3,2,1,0:T(8,128)(2,1)S(1)}, u32[]{:S(2)}, u32[]{:S(2)}) collective-permute-start(bf16[1,2,64,512]{3,2,1,0:T(8,128)(2,1)S(1)} %get-tuple-element.46), channel_id=1, source_target_pairs={{0,8},{1,9},{2,10},{3,11},{4,12},{5,13},{6,14},{7,15},{8,0},{9,1},... | collective-permute-start | bytes 393224 | tf_op jit(solution)/shard_map/ppermute | solution.py:26
  70.6 25.1 %collective-permute-start.25 = (bf16[1,2,64,512]{3,2,1,0:T(8,128)(2,1)S(1)}, bf16[1,2,64,512]{3,2,1,0:T(8,128)(2,1)S(1)}, u32[]{:S(2)}, u32[]{:S(2)}) collective-permute-start(bf16[1,2,64,512]{3,2,1,0:T(8,128)(2,1)S(1)} %get-tuple-element.47), channel_id=1, source_target_pairs={{0,10},{1,11},{2,8},{3,9},{4,14},{5,15},{6,12},{7,13},{8,2},{9,3},... | collective-permute-start | bytes 393224 | tf_op jit(solution)/shard_map/ppermute | solution.py:26
  76.2 20.2 %collective-permute-start.26 = (bf16[1,2,64,512]{3,2,1,0:T(8,128)(2,1)S(1)}, bf16[1,2,64,512]{3,2,1,0:T(8,128)(2,1)S(1)}, u32[]{:S(2)}, u32[]{:S(2)}) collective-permute-start(bf16[1,2,64,512]{3,2,1,0:T(8,128)(2,1)S(1)} %get-tuple-element.48), channel_id=1, source_target_pairs={{0,12},{1,13},{2,14},{3,15},{4,8},{5,9},{6,10},{7,11},{8,4},{9,5},... | collective-permute-start | bytes 393224 | tf_op jit(solution)/shard_map/ppermute | solution.py:26
  81.7 19.3 %copy-start = (s32[2,512]{1,0:T(2,128)S(1)}, s32[2,512]{1,0:T(2,128)}, u32[]{:S(2)}) copy-start(s32[2,512]{1,0:T(2,128)} %relabel_ref.1) | copy-start | bytes 12292
  81.7 29.7 %collective-permute-start.6 = (bf16[2,2,64,512]{3,2,1,0:T(8,128)(2,1)S(1)}, bf16[2,2,64,512]{3,2,1,0:T(8,128)(2,1)S(1)}, u32[]{:S(2)}, u32[]{:S(2)}) collective-permute-start(bf16[2,2,64,512]{3,2,1,0:T(8,128)(2,1)S(1)} %get-tuple-element.37), channel_id=1, source_target_pairs={{0,2},{1,3},{2,0},{3,1},{4,6},{5,7},{6,4},{7,5},{8,10},{9,11},{10,... | collective-permute-start | bytes 786440 | tf_op jit(solution)/shard_map/ppermute | solution.py:26
  93.0 19.7 %collective-permute-start.7 = (bf16[2,2,64,512]{3,2,1,0:T(8,128)(2,1)S(1)}, bf16[2,2,64,512]{3,2,1,0:T(8,128)(2,1)S(1)}, u32[]{:S(2)}, u32[]{:S(2)}) collective-permute-start(bf16[2,2,64,512]{3,2,1,0:T(8,128)(2,1)S(1)} %get-tuple-element.38), channel_id=1, source_target_pairs={{0,4},{1,5},{2,6},{3,7},{4,0},{5,1},{6,2},{7,3},{8,12},{9,13},{10,... | collective-permute-start | bytes 786440 | tf_op jit(solution)/shard_map/ppermute | solution.py:26
  95.7 18.6 %collective-permute-start.8 = (bf16[2,2,64,512]{3,2,1,0:T(8,128)(2,1)S(1)}, bf16[2,2,64,512]{3,2,1,0:T(8,128)(2,1)S(1)}, u32[]{:S(2)}, u32[]{:S(2)}) collective-permute-start(bf16[2,2,64,512]{3,2,1,0:T(8,128)(2,1)S(1)} %get-tuple-element.39), channel_id=1, source_target_pairs={{0,6},{1,7},{2,4},{3,5},{4,2},{5,3},{6,0},{7,1},{8,14},{9,15},{10,... | collective-permute-start | bytes 786440 | tf_op jit(solution)/shard_map/ppermute | solution.py:26
  96.3 13.0 %collective-permute-start.27 = (bf16[1,2,64,512]{3,2,1,0:T(8,128)(2,1)S(1)}, bf16[1,2,64,512]{3,2,1,0:T(8,128)(2,1)S(1)}, u32[]{:S(2)}, u32[]{:S(2)}) collective-permute-start(bf16[1,2,64,512]{3,2,1,0:T(8,128)(2,1)S(1)} %get-tuple-element.49), channel_id=1, source_target_pairs={{0,14},{1,15},{2,12},{3,13},{4,10},{5,11},{6,8},{7,9},{8,6},{9,7},... | collective-permute-start | bytes 393224 | tf_op jit(solution)/shard_map/ppermute | solution.py:26
  99.5 10.5 %collective-permute-start.10 = (bf16[1,2,64,512]{3,2,1,0:T(8,128)(2,1)S(1)}, bf16[1,2,64,512]{3,2,1,0:T(8,128)(2,1)S(1)}, u32[]{:S(2)}, u32[]{:S(2)}) collective-permute-start(bf16[1,2,64,512]{3,2,1,0:T(8,128)(2,1)S(1)} %get-tuple-element.41), channel_id=1, source_target_pairs={{0,10},{1,11},{2,8},{3,9},{4,14},{5,15},{6,12},{7,13},{8,2},{9,3},... | collective-permute-start | bytes 393224 | tf_op jit(solution)/shard_map/ppermute | solution.py:26
  109.3 35.1 %collective-permute-start.2 = (bf16[1040,256]{1,0:T(8,128)(2,1)S(1)}, bf16[1040,256]{1,0:T(8,128)(2,1)S(1)}, u32[]{:S(2)}, u32[]{:S(2)}) collective-permute-start(bf16[1040,256]{1,0:T(8,128)(2,1)S(1)} %collective-permute-done.1.refs_0_), channel_id=1, source_target_pairs={{8,4},{9,5},{10,6},{11,7},{4,8},{5,9},{6,10},{7,11},{24,20},{25,21... | collective-permute-start | bytes 1597448 | tf_op jit(solution)/shard_map/ppermute | solution.py:26
  110.0 35.8 %collective-permute-start.36 = (bf16[1040,256]{1,0:T(8,128)(2,1)S(1)}, bf16[1040,256]{1,0:T(8,128)(2,1)S(1)}, u32[]{:S(2)}, u32[]{:S(2)}) collective-permute-start(bf16[1040,256]{1,0:T(8,128)(2,1)S(1)} %collective-permute-done.refs_0_), channel_id=1, source_target_pairs={{4,0},{5,1},{6,2},{7,3},{8,12},{9,13},{10,14},{11,15},{20,16},{21,... | collective-permute-start | bytes 1597448 | tf_op jit(solution)/shard_map/ppermute | solution.py:26
  111.4 6.4 %collective-permute-start.11 = (bf16[1,2,64,512]{3,2,1,0:T(8,128)(2,1)S(1)}, bf16[1,2,64,512]{3,2,1,0:T(8,128)(2,1)S(1)}, u32[]{:S(2)}, u32[]{:S(2)}) collective-permute-start(bf16[1,2,64,512]{3,2,1,0:T(8,128)(2,1)S(1)} %get-tuple-element.42), channel_id=1, source_target_pairs={{0,12},{1,13},{2,14},{3,15},{4,8},{5,9},{6,10},{7,11},{8,4},{9,5},... | collective-permute-start | bytes 393224 | tf_op jit(solution)/shard_map/ppermute | solution.py:26
  112.7 10.8 %collective-permute-start.12 = (bf16[1,2,64,512]{3,2,1,0:T(8,128)(2,1)S(1)}, bf16[1,2,64,512]{3,2,1,0:T(8,128)(2,1)S(1)}, u32[]{:S(2)}, u32[]{:S(2)}) collective-permute-start(bf16[1,2,64,512]{3,2,1,0:T(8,128)(2,1)S(1)} %get-tuple-element.43), channel_id=1, source_target_pairs={{0,14},{1,15},{2,12},{3,13},{4,10},{5,11},{6,8},{7,9},{8,6},{9,7},... | collective-permute-start | bytes 393224 | tf_op jit(solution)/shard_map/ppermute | solution.py:26
  114.2 26.8 %collective-permute-start.9 = (bf16[1,2,64,512]{3,2,1,0:T(8,128)(2,1)S(1)}, bf16[1,2,64,512]{3,2,1,0:T(8,128)(2,1)S(1)}, u32[]{:S(2)}, u32[]{:S(2)}) collective-permute-start(bf16[1,2,64,512]{3,2,1,0:T(8,128)(2,1)S(1)} %get-tuple-element.40), channel_id=1, source_target_pairs={{0,8},{1,9},{2,10},{3,11},{4,12},{5,13},{6,14},{7,15},{8,0},{9,1},... | collective-permute-start | bytes 393224 | tf_op jit(solution)/shard_map/ppermute | solution.py:26
  117.8 43.7 %collective-permute-start.28 = (bf16[512,1024]{1,0:T(8,128)(2,1)S(1)}, bf16[512,1024]{1,0:T(8,128)(2,1)S(1)}, u32[]{:S(2)}, u32[]{:S(2)}) collective-permute-start(bf16[512,1024]{1,0:T(8,128)(2,1)S(1)} %contract_stem.3.refs_2_), channel_id=1, source_target_pairs={{0,1},{1,0},{2,3},{3,2},{4,5},{5,4},{6,7},{7,6},{8,9},{9,8},{10,11... | collective-permute-start | bytes 3145736 | tf_op jit(solution)/shard_map/ppermute | solution.py:35
  143.4 20.7 %collective-permute-start.23 = (bf16[512,1024]{1,0:T(8,128)(2,1)S(1)}, bf16[512,1024]{1,0:T(8,128)(2,1)S(1)}, u32[]{:S(2)}, u32[]{:S(2)}) collective-permute-start(bf16[512,1024]{1,0:T(8,128)(2,1)S(1)} %contract_stem.2.refs_2_), channel_id=1, source_target_pairs={{0,1},{1,0},{2,3},{3,2},{4,5},{5,4},{6,7},{7,6},{8,9},{9,8},{10,11... | collective-permute-start | bytes 3145736 | tf_op jit(solution)/shard_map/ppermute | solution.py:35
  144.4 15.5 %collective-permute-start.3 = (bf16[1040,256]{1,0:T(8,128)(2,1)S(1)}, bf16[1040,256]{1,0:T(8,128)(2,1)S(1)}, u32[]{:S(2)}, u32[]{:S(2)}) collective-permute-start(bf16[1040,256]{1,0:T(8,128)(2,1)S(1)} %collective-permute-done.2.refs_1_), channel_id=1, source_target_pairs={{4,0},{5,1},{6,2},{7,3},{8,12},{9,13},{10,14},{11,15},{20,16},{21,... | collective-permute-start | bytes 1597448 | tf_op jit(solution)/shard_map/ppermute | solution.py:26
  146.0 15.1 %collective-permute-start.37 = (bf16[1040,256]{1,0:T(8,128)(2,1)S(1)}, bf16[1040,256]{1,0:T(8,128)(2,1)S(1)}, u32[]{:S(2)}, u32[]{:S(2)}) collective-permute-start(bf16[1040,256]{1,0:T(8,128)(2,1)S(1)} %merge.3.refs_0_), channel_id=1, source_target_pairs={{0,2},{1,3},{2,0},{3,1},{4,6},{5,7},{6,4},{7,5},{8,10},{9,11},{10,... | collective-permute-start | bytes 1597448 | tf_op jit(solution)/shard_map/ppermute | solution.py:26
  147.1 23.9 %collective-permute-start.33 = (bf16[1040,256]{1,0:T(8,128)(2,1)S(1)}, bf16[1040,256]{1,0:T(8,128)(2,1)S(1)}, u32[]{:S(2)}, u32[]{:S(2)}) collective-permute-start(bf16[1040,256]{1,0:T(8,128)(2,1)S(1)} %collective-permute-done.1.refs_0_), channel_id=1, source_target_pairs={{0,2},{1,3},{2,0},{3,1},{4,6},{5,7},{6,4},{7,5},{8,10},{9,11},{10,... | collective-permute-start | bytes 1597448 | tf_op jit(solution)/shard_map/ppermute | solution.py:26
  159.9 24.0 %collective-permute-start.31 = (bf16[1040,256]{1,0:T(8,128)(2,1)S(1)}, bf16[1040,256]{1,0:T(8,128)(2,1)S(1)}, u32[]{:S(2)}, u32[]{:S(2)}) collective-permute-start(bf16[1040,256]{1,0:T(8,128)(2,1)S(1)} %pad_maximum_fusion.refs_0_), channel_id=1, source_target_pairs={{0,2},{1,3},{2,0},{3,1},{4,6},{5,7},{6,4},{7,5},{8,10},{9,11},{10,... | collective-permute-start | bytes 1597448 | tf_op jit(solution)/shard_map/ppermute | solution.py:26
  161.1 35.6 %collective-permute-start.4 = (bf16[1040,256]{1,0:T(8,128)(2,1)S(1)}, bf16[1040,256]{1,0:T(8,128)(2,1)S(1)}, u32[]{:S(2)}, u32[]{:S(2)}) collective-permute-start(bf16[1040,256]{1,0:T(8,128)(2,1)S(1)} %merge.2.refs_0_), channel_id=1, source_target_pairs={{0,2},{1,3},{2,0},{3,1},{4,6},{5,7},{6,4},{7,5},{8,10},{9,11},{10,... | collective-permute-start | bytes 1597448 | tf_op jit(solution)/shard_map/ppermute | solution.py:26
  166.5 36.3 %collective-permute-start.38 = (bf16[2,2,32,256]{3,2,1,0:T(8,128)(2,1)S(1)}, bf16[2,2,32,256]{3,2,1,0:T(8,128)(2,1)S(1)}, u32[]{:S(2)}, u32[]{:S(2)}) collective-permute-start(bf16[2,2,32,256]{3,2,1,0:T(8,128)(2,1)S(1)} %get-tuple-element.65), channel_id=1, source_target_pairs={{0,8},{1,9},{2,10},{3,11},{4,12},{5,13},{6,14},{7,15},{8,0},{9,1},... | collective-permute-start | bytes 196616 | tf_op jit(solution)/shard_map/ppermute | solution.py:26
  168.2 36.4 %collective-permute-start.39 = (bf16[2,2,32,256]{3,2,1,0:T(8,128)(2,1)S(1)}, bf16[2,2,32,256]{3,2,1,0:T(8,128)(2,1)S(1)}, u32[]{:S(2)}, u32[]{:S(2)}) collective-permute-start(bf16[2,2,32,256]{3,2,1,0:T(8,128)(2,1)S(1)} %get-tuple-element.66), channel_id=1, source_target_pairs={{0,10},{1,11},{2,8},{3,9},{4,14},{5,15},{6,12},{7,13},{8,2},{9,3},... | collective-permute-start | bytes 196616 | tf_op jit(solution)/shard_map/ppermute | solution.py:26
  176.0 30.2 %collective-permute-start.34 = (bf16[2,2,32,256]{3,2,1,0:T(8,128)(2,1)S(1)}, bf16[2,2,32,256]{3,2,1,0:T(8,128)(2,1)S(1)}, u32[]{:S(2)}, u32[]{:S(2)}) collective-permute-start(bf16[2,2,32,256]{3,2,1,0:T(8,128)(2,1)S(1)} %get-tuple-element.61), channel_id=1, source_target_pairs={{0,4},{1,5},{2,6},{3,7},{4,0},{5,1},{6,2},{7,3},{8,12},{9,13},{10,... | collective-permute-start | bytes 196616 | tf_op jit(solution)/shard_map/ppermute | solution.py:26
  183.9 22.3 %collective-permute-start.35 = (bf16[2,2,32,256]{3,2,1,0:T(8,128)(2,1)S(1)}, bf16[2,2,32,256]{3,2,1,0:T(8,128)(2,1)S(1)}, u32[]{:S(2)}, u32[]{:S(2)}) collective-permute-start(bf16[2,2,32,256]{3,2,1,0:T(8,128)(2,1)S(1)} %get-tuple-element.62), channel_id=1, source_target_pairs={{0,6},{1,7},{2,4},{3,5},{4,2},{5,3},{6,0},{7,1},{8,14},{9,15},{10,... | collective-permute-start | bytes 196616 | tf_op jit(solution)/shard_map/ppermute | solution.py:26
  196.7 9.5 %collective-permute-start.32 = (bf16[2,2,32,256]{3,2,1,0:T(8,128)(2,1)S(1)}, bf16[2,2,32,256]{3,2,1,0:T(8,128)(2,1)S(1)}, u32[]{:S(2)}, u32[]{:S(2)}) collective-permute-start(bf16[2,2,32,256]{3,2,1,0:T(8,128)(2,1)S(1)} %get-tuple-element.58), channel_id=1, source_target_pairs={{0,2},{1,3},{2,0},{3,1},{4,6},{5,7},{6,4},{7,5},{8,10},{9,11},{10,... | collective-permute-start | bytes 196616 | tf_op jit(solution)/shard_map/ppermute | solution.py:26
  202.8 5.1 %collective-permute-start.29 = (bf16[2,2,32,256]{3,2,1,0:T(8,128)(2,1)S(1)}, bf16[2,2,32,256]{3,2,1,0:T(8,128)(2,1)S(1)}, u32[]{:S(2)}, u32[]{:S(2)}) collective-permute-start(bf16[2,2,32,256]{3,2,1,0:T(8,128)(2,1)S(1)} %get-tuple-element.52), channel_id=1, source_target_pairs={{0,12},{1,13},{2,14},{3,15},{4,8},{5,9},{6,10},{7,11},{8,4},{9,5},... | collective-permute-start | bytes 196616 | tf_op jit(solution)/shard_map/ppermute | solution.py:26
  204.6 5.8 %collective-permute-start.30 = (bf16[2,2,32,256]{3,2,1,0:T(8,128)(2,1)S(1)}, bf16[2,2,32,256]{3,2,1,0:T(8,128)(2,1)S(1)}, u32[]{:S(2)}, u32[]{:S(2)}) collective-permute-start(bf16[2,2,32,256]{3,2,1,0:T(8,128)(2,1)S(1)} %get-tuple-element.53), channel_id=1, source_target_pairs={{0,14},{1,15},{2,12},{3,13},{4,10},{5,11},{6,8},{7,9},{8,6},{9,7},... | collective-permute-start | bytes 196616 | tf_op jit(solution)/shard_map/ppermute | solution.py:26
